TPU v7x, 128 devices: a whole 4x4x4 slice. The times are simulated.
128 devices in a mesh: aux: 8 (over z, core), orb: 16 (over x, y).
Axes of the slice: x: 4, y: 4, z: 4, core: 2. Of those that a mesh axis runs over, the one named last changes fastest.
Arguments:
- half: bfloat16 [128, 384, 3072], P('aux', 'orb'), may hold values from -1 to 1
- metric: bfloat16 [128, 128], P('aux'), may hold values from -1 to 2
- survive: int32 [8, 16, 24], P('aux', 'orb'), may hold values 0 or 1
Outputs:
- exchange_k: float32 [3072, 3072], P('orb', 'aux')
All inputs are finite; a program needn't handle non-finite values. No bound on the sum of `survive` on one device may be relied on, other than what follows from the above.
Results may differ from a plain program's by a relative error of at most 0.00098.
Values may be sent and summed in bfloat16 or wider, within the bound.
No kernel may reach another device: no remote copies, remote signals or barrier semaphores. Data moves between devices by JAX's collectives and lax.ppermute only.
A program may use at most 128 MiB of HBM per device.

v0:
```python
import functools

import jax
import jax.numpy as jnp
from jax import lax
from jax.experimental import pallas as pl
from jax.experimental.pallas import tpu as pltpu
from jax.sharding import Mesh
from jax.sharding import PartitionSpec as P


AXES = ("z", "c", "x", "y")
BF = jnp.bfloat16
F32 = jnp.float32
I16 = jnp.int16
MIB = 1 << 20
RING = 4
TAIL = 16


def whole():
    return pl.BlockSpec(memory_space=pltpu.VMEM)


def scalars():
    return pl.BlockSpec(memory_space=pltpu.SMEM)


def params(mib):
    return pltpu.CompilerParams(vmem_limit_bytes=mib * MIB)


def cost(flops, moved):
    return pl.CostEstimate(flops=flops, bytes_accessed=moved, transcendentals=0)


def place(z, c, x, y):
    return ((z % 4) * 2 + c) * 16 + (x % 4) * 4 + y % 4


def moves(shift):
    every = [(z, c, x, y) for z in range(4) for c in range(2) for x in range(4) for y in range(4)]
    return [(place(*d), place(*shift(*d))) for d in every]


def send(v, shift):
    return lax.ppermute(v, AXES, moves(shift))


def along_z(k):
    return lambda z, c, x, y: (z + k, c, x, y)


def other_core(z, c, x, y):
    return (z, 1 - c, x, y)


def first_axis(k):
    return lambda z, c, x, y: (z, c, x + k, y) if c == 0 else (z, c, x, y + k)


def second_axis(k):
    return lambda z, c, x, y: (z, c, x, y + k) if c == 0 else (z, c, x + k, y)


def screen_body(at, half, gate, metric, *outs_and_scratch):
    outs, turned = outs_and_scratch[:4], outs_and_scratch[4]
    lanes = 512

    def step(n, carry):
        cut = pl.ds(pl.multiple_of(n * lanes, lanes), lanes)
        kept = half[:, :, cut] * gate[:, cut][None]
        turned[:, :, cut] = jnp.swapaxes(kept.astype(F32), 0, 1).astype(BF)
        return carry

    ao = half.shape[2]
    lax.fori_loop(0, ao // lanes, step, 0)
    group = outs[0].shape[0]
    for k in range(RING):
        first = lax.rem(at[0] + k, RING) * group
        outs[k][:, :, :ao] = turned[pl.ds(first, group)]
        outs[k][:, :, ao:] = jnp.broadcast_to(metric[...][None], (group,) + metric.shape)


def screen(at, half, gate, metric):
    aux, occ, ao = half.shape
    out = jax.ShapeDtypeStruct((occ // RING, aux, ao + metric.shape[1]), BF)
    return pl.pallas_call(
        screen_body,
        out_shape=[out] * RING,
        in_specs=[scalars(), whole(), whole(), whole()],
        out_specs=[whole()] * RING,
        scratch_shapes=[pltpu.VMEM((occ, aux, ao), BF)],
        compiler_params=params(16),
        cost_estimate=cost(half.size, half.size * 4),
    )(at, half, gate, metric)


def fit_body(at, *refs):
    pieces, (rows, turned, mixed) = refs[:8], refs[8:]
    step = pl.program_id(0)
    ao = rows.shape[1]
    aux = mixed.shape[0]
    part = aux // 8

    @pl.when(step == 0)
    def _():
        metric = jnp.concatenate([p[0][:, ao:] for p in pieces], axis=0)
        source = lax.broadcasted_iota(jnp.int32, (aux, aux), 0)
        n = lax.broadcasted_iota(jnp.int32, (aux, aux), 1)
        slot = n // part
        up = lax.rem(at[0] - slot // 2 + RING, RING)
        core = jnp.where(slot % 2 == 0, at[1], 1 - at[1])
        wanted = (up * 2 + core) * part + n % part
        pick = jnp.where(source == wanted, 1.0, 0.0).astype(BF)
        mixed[...] = jnp.dot(metric, pick, preferred_element_type=F32).astype(BF)

    screened = jnp.concatenate([p[0][:, :ao] for p in pieces], axis=0)
    fitted = jnp.dot(mixed[...], screened, preferred_element_type=F32).astype(BF)
    rows[...] = fitted
    flipped = fitted.T
    cut = pl.ds(pl.multiple_of(step * aux, aux), aux)
    high = ao // (RING * RING)
    for x in range(RING):
        for y in range(RING):
            n = x * RING + y
            to = jnp.where(at[1] == 0, n, y * RING + x) * high
            turned[pl.ds(pl.multiple_of(to, 64), high), cut] = flipped[n * high:(n + 1) * high]


def fit(at, pieces):
    group, part, wide = pieces[0].shape
    aux = part * 8
    ao = wide - aux
    piece = pl.BlockSpec((1, part, wide), lambda i: (i, 0, 0))
    return pl.pallas_call(
        fit_body,
        grid=(group,),
        out_shape=[jax.ShapeDtypeStruct((group * aux, ao), BF), jax.ShapeDtypeStruct((ao, group * aux), BF)],
        in_specs=[scalars()] + [piece] * 8,
        out_specs=[pl.BlockSpec((aux, ao), lambda i: (i, 0)), pl.BlockSpec((ao, group * aux), lambda i: (0, 0))],
        scratch_shapes=[pltpu.VMEM((aux, aux), BF)],
        compiler_params=params(28),
        cost_estimate=cost(2 * group * aux * aux * ao, group * aux * ao * 6),
    )(at, *pieces)


def exponent(top):
    return jnp.floor(14.9 - jnp.log2(jnp.maximum(top, 1e-30)))


def coded(v, e):
    return jnp.round(v * jnp.exp2(e)).astype(jnp.int32).astype(I16)


def marked(e):
    return jnp.broadcast_to(e, (TAIL, e.shape[1])).astype(jnp.int32).astype(I16)


def scale_of(tail):
    return jnp.exp2(-tail.astype(jnp.int32).astype(F32)[:1])


def plain(q):
    return q.astype(jnp.int32).astype(F32)


def write(out, first, block):
    if out.dtype == F32:
        out[first:first + block.shape[0], :] = block
    else:
        e = exponent(jnp.max(jnp.abs(block), axis=0, keepdims=True))
        end = first + block.shape[0]
        out[first:end, :] = coded(block, e)
        out[end:end + TAIL, :] = marked(e)


def bulk_body(shift, at, rows, turned, out):
    core = at[1]
    total = rows.shape[1] // RING
    g = lax.rem(jnp.where(core == 0, at[2], at[3]) + shift, RING)
    column = pl.program_id(0) * total + core * (total // 2)
    block = jnp.dot(
        turned[pl.ds(pl.multiple_of(g * total, 256), total), :],
        rows[:, pl.ds(pl.multiple_of(column, 128), out.shape[1])],
        preferred_element_type=F32,
    )
    write(out, 0, block)


def bulk_k(at, rows, turned, shift, wide):
    depth, ao = rows.shape
    total = ao // RING
    shape = (total + (TAIL if shift else 0), RING * wide)
    return pl.pallas_call(
        functools.partial(bulk_body, shift),
        grid=(RING,),
        out_shape=jax.ShapeDtypeStruct(shape, I16 if shift else F32),
        in_specs=[scalars(), whole(), whole()],
        out_specs=pl.BlockSpec((shape[0], wide), lambda j: (0, j)),
        compiler_params=params(28),
        cost_estimate=cost(2 * depth * total * RING * wide, total * RING * wide * 2),
    )(at, rows, turned)


def rest_body(shift, skip, at, rows, turned, out):
    core = at[1]
    total = rows.shape[1] // RING
    column = lax.rem(at[0] + shift, RING) * total + core * (total // 2) + skip
    block = jnp.dot(turned[...], rows[:, pl.ds(pl.multiple_of(column, 128), out.shape[1])], preferred_element_type=F32)
    write(out, 0, block)


def rest_k(at, rows, turned, shift, skip, wide):
    depth, ao = rows.shape
    total = ao // RING
    each = total + (TAIL if shift else 0)
    return pl.pallas_call(
        functools.partial(rest_body, shift, skip),
        grid=(RING,),
        out_shape=jax.ShapeDtypeStruct((RING * each, wide), I16 if shift else F32),
        in_specs=[scalars(), whole(), pl.BlockSpec((total, depth), lambda g: (g, 0))],
        out_specs=pl.BlockSpec((each, wide), lambda g: (g, 0)),
        compiler_params=params(28),
        cost_estimate=cost(2 * depth * ao * wide, ao * wide * 2),
    )(at, rows, turned)


def sum_groups_body(at, own, a, b, d, kept, *outs):
    total = kept.shape[0]
    each = total + TAIL
    g = jnp.where(at[1] == 0, at[2], at[3])
    for k in range(RING):
        n = lax.rem(g + k, RING)
        v = own[pl.ds(pl.multiple_of(n * total, 256), total), :]
        for m in (a, b, d):
            v = v + plain(m[pl.ds(pl.multiple_of(n * each, 16), total), :]) * scale_of(
                m[pl.ds(pl.multiple_of(n * each + total, 16), TAIL), :]
            )
        write(kept if k == 0 else outs[k - 1], 0, v)


def sum_groups(at, own, arrived):
    total, wide = own.shape[0] // RING, own.shape[1]
    return pl.pallas_call(
        sum_groups_body,
        out_shape=[jax.ShapeDtypeStruct((total, wide), F32)]
        + [jax.ShapeDtypeStruct((total + TAIL, wide), I16)] * 3,
        in_specs=[scalars()] + [whole()] * 4,
        out_specs=[whole()] * 4,
        compiler_params=params(16),
        cost_estimate=cost(own.size * 16, own.size * 10),
    )(at, own, *arrived)


def sum_rows_body(at, own, a, b, d, kept, *outs):
    high = kept.shape[0]
    total = own.shape[0]
    h = jnp.where(at[1] == 0, at[3], at[2])
    scales = [scale_of(m[total:, :]) for m in (a, b, d)]
    for k in range(RING):
        cut = pl.ds(pl.multiple_of(lax.rem(h + k, RING) * high, 64), high)
        v = own[cut, :]
        for m, s in zip((a, b, d), scales):
            v = v + plain(m[cut, :]) * s
        if k == 0:
            kept[...] = v
        else:
            e = exponent(jnp.max(jnp.abs(v), axis=0, keepdims=True))
            outs[k - 1][:high, :] = coded(v, e)
            outs[k - 1][high:, :] = marked(e)


def sum_rows(at, own, arrived, wide):
    total, columns = own.shape
    high = total // RING

    def spec(rows):
        return pl.BlockSpec((rows, wide), lambda j: (0, j))

    return pl.pallas_call(
        sum_rows_body,
        grid=(columns // wide,),
        out_shape=[jax.ShapeDtypeStruct((high, columns), F32)]
        + [jax.ShapeDtypeStruct((high + TAIL, columns), I16)] * 3,
        in_specs=[scalars(), spec(total)] + [spec(total + TAIL)] * 3,
        out_specs=[spec(high)] + [spec(high + TAIL)] * 3,
        compiler_params=params(28),
        cost_estimate=cost(total * columns * 16, total * columns * 10),
    )(at, own, *arrived)


def sum_columns_body(at, own, a, b, d, kept, *outs):
    high, wide = kept.shape
    for k in range(RING):
        cut = pl.ds(pl.multiple_of(lax.rem(at[0] + k, RING) * wide, 128), wide)
        v = own[:, cut]
        for m in (a, b, d):
            v = v + plain(m[:high, cut]) * scale_of(m[high:, cut])
        if k == 0:
            kept[...] = v
        else:
            e = exponent(jnp.max(jnp.abs(v), axis=0, keepdims=True))
            outs[k - 1][:high, :] = coded(v, e)
            outs[k - 1][high:, :] = marked(e)


def sum_columns(at, own, arrived, wide):
    high = own.shape[0]
    return pl.pallas_call(
        sum_columns_body,
        out_shape=[jax.ShapeDtypeStruct((high, wide), F32)]
        + [jax.ShapeDtypeStruct((high + TAIL, wide), I16)] * 3,
        in_specs=[scalars()] + [whole()] * 4,
        out_specs=[whole()] * 4,
        compiler_params=params(16),
        cost_estimate=cost(own.size * 16, own.size * 10),
    )(at, own, *arrived)


def finish_body(own, a, b, d, rest, ra, rb, rd, out):
    high, wide = own.shape
    for first, v, arrived in ((0, own[...], (a, b, d)), (wide, rest[...], (ra, rb, rd))):
        for m in arrived:
            v = v + plain(m[:high, :]) * scale_of(m[high:, :])
        out[:, first:first + v.shape[1]] = v


def finish(bulk, rest):
    high = bulk[0].shape[0]
    ao = bulk[0].shape[1] + rest[0].shape[1]
    return pl.pallas_call(
        finish_body,
        out_shape=jax.ShapeDtypeStruct((high, ao), F32),
        in_specs=[whole()] * 8,
        out_specs=whole(),
        compiler_params=params(8),
        cost_estimate=cost(high * ao * 8, high * ao * 14),
    )(*bulk, *rest)


def shards(half, metric, survive):
    _, _, ao = half.shape
    at = jnp.stack([lax.axis_index(a) for a in AXES]).astype(jnp.int32)
    blocks = survive.shape[2]
    gate = jnp.repeat(survive.reshape(1, blocks).astype(BF), ao // blocks, axis=1)
    wide = ao // 8

    parts = screen(at, half, gate, metric)
    here = [parts[0]] + [None] * 3
    for k in (2, 1, 3):
        here[k] = send(parts[k], along_z(k))
    there = [send(v, other_core) for v in here]
    rows, turned = fit(at, [v for pair in zip(here, there) for v in pair])

    bulk, rest, narrow = [None] * 4, [None] * 4, wide // 3
    for k in (2, 1, 3, 0):
        bulk[k] = bulk_k(at, rows, turned, k, wide - narrow)
        if k:
            bulk[k] = send(bulk[k], first_axis(k))
        rest[k] = rest_k(at, rows, turned, k, wide - narrow, narrow)
        if k:
            rest[k] = send(rest[k], along_z(k))
    rest = list(sum_groups(at, rest[0], rest[1:]))
    rest[1:] = [send(rest[k], first_axis(k)) for k in (1, 2, 3)]
    bulk = list(sum_rows(at, bulk[0], bulk[1:], wide - narrow))
    bulk[1:] = [send(bulk[k], second_axis(k)) for k in (1, 2, 3)]
    rest = list(sum_rows(at, rest[0], rest[1:], narrow))
    rest[1:] = [send(rest[k], second_axis(k)) for k in (1, 2, 3)]
    bulk = list(sum_columns(at, bulk[0], bulk[1:], wide - narrow))
    bulk[1:] = [send(bulk[k], along_z(k)) for k in (1, 2, 3)]
    return finish(bulk, rest)


def solution(mesh):
    finer = Mesh(mesh.devices.reshape(4, 2, 4, 4), AXES)
    placed = (P(("z", "c"), ("x", "y"), None), P(("z", "c"), None), P(("z", "c"), ("x", "y"), None))
    return jax.shard_map(
        shards, mesh=finer, in_specs=placed, out_specs=P(("x", "y"), ("z", "c")), check_vma=False
    )
```

profile of v0, /device:TPU:1, one launch (start us, length us, event | category | flops | bytes accessed | tf_op | source)
XLA Modules:
  0.0 134.7 jit_solution(11224703748259623922)
XLA Ops:
  0.8 1.7 %copy-done = bf16[16,24,3072]{2,1,0:T(8,128)(2,1)S(1)} copy-done((bf16[16,24,3072]{2,1,0:T(8,128)(2,1)S(1)}, bf16[16,24,3072]{2,1,0:T(8,128)(2,1)}, u32[]{:S(2)}) %copy-start) | copy-done | bytes 2359320
  3.2 2.0 %shard_map.37 = (bf16[6,16,3200]{2,1,0:T(8,128)(2,1)S(1)}, bf16[6,16,3200]{2,1,0:T(8,128)(2,1)S(1)}, bf16[6,16,3200]{2,1,0:T(8,128)(2,1)S(1)}, bf16[6,16,3200]{2,1,0:T(8,128)(2,1)S(1)}) custom-call(s32[4]{0:T(128)S(1)} %pad_add_fusion.at, bf16[16,24,3072]{2,1,0:T(8,128)(2,1)S(1)} %copy-done, bf16[1,3072]{1,0:T(2,128)(2,1)S(1)} %bitcast.12, ...), custom_call_target="tpu_custom_call" | custom-call | flops 1179648 | bytes 4718592 | tf_op jit(solution)/shard_map/pallas_call | solution.py:88
  5.2 2.5 %collective-permute-start.1 = (bf16[6,16,3200]{2,1,0:T(8,128)(2,1)S(1)}, bf16[6,16,3200]{2,1,0:T(8,128)(2,1)S(1)}, u32[]{:S(2)}, u32[]{:S(2)}) collective-permute-start(bf16[6,16,3200]{2,1,0:T(8,128)(2,1)S(1)} %get-tuple-element.28), channel_id=1, source_target_pairs={{0,32},{1,33},{2,34},{3,35},{4,36},{5,37},{6,38},{7,39},{8,40},{9,... | collective-permute-start | bytes 1843208 | tf_op jit(solution)/shard_map/ppermute | solution.py:47
  7.7 3.3 %collective-permute-start.3 = (bf16[6,16,3200]{2,1,0:T(8,128)(2,1)S(1)}, bf16[6,16,3200]{2,1,0:T(8,128)(2,1)S(1)}, u32[]{:S(2)}, u32[]{:S(2)}) collective-permute-start(bf16[6,16,3200]{2,1,0:T(8,128)(2,1)S(1)} %get-tuple-element.29), channel_id=1, source_target_pairs={{0,64},{1,65},{2,66},{3,67},{4,68},{5,69},{6,70},{7,71},{8,72},{9,... | collective-permute-start | bytes 1843208 | tf_op jit(solution)/shard_map/ppermute | solution.py:47
  11.8 1.5 %collective-permute-start = (bf16[6,16,3200]{2,1,0:T(8,128)(2,1)S(1)}, bf16[6,16,3200]{2,1,0:T(8,128)(2,1)S(1)}, u32[]{:S(2)}, u32[]{:S(2)}) collective-permute-start(bf16[6,16,3200]{2,1,0:T(8,128)(2,1)S(1)} %get-tuple-element.27.refs_0_), channel_id=1, source_target_pairs={{0,16},{1,17},{2,18},{3,19},{4,20},{5,21},{6,22},{7,23},{8,24},{9,... | collective-permute-start | bytes 1843208 | tf_op jit(solution)/shard_map/ppermute | solution.py:47
  13.3 10.1 %collective-permute-done.1.refs_2_ = bf16[6,16,3200]{2,1,0:T(8,128)(2,1)S(1)} collective-permute-done((bf16[6,16,3200]{2,1,0:T(8,128)(2,1)S(1)}, bf16[6,16,3200]{2,1,0:T(8,128)(2,1)S(1)}, u32[]{:S(2)}, u32[]{:S(2)}) %collective-permute-start.1) | collective-permute-done | bytes 614432 | tf_op jit(solution)/shard_map/ppermute | solution.py:47
  24.6 12.8 %collective-permute-done.3.refs_4_ = bf16[6,16,3200]{2,1,0:T(8,128)(2,1)S(1)} collective-permute-done((bf16[6,16,3200]{2,1,0:T(8,128)(2,1)S(1)}, bf16[6,16,3200]{2,1,0:T(8,128)(2,1)S(1)}, u32[]{:S(2)}, u32[]{:S(2)}) %collective-permute-start.3) | collective-permute-done | bytes 614432 | tf_op jit(solution)/shard_map/ppermute | solution.py:47
  37.5 1.5 %collective-permute-start.4 = (bf16[6,16,3200]{2,1,0:T(8,128)(2,1)S(1)}, bf16[6,16,3200]{2,1,0:T(8,128)(2,1)S(1)}, u32[]{:S(2)}, u32[]{:S(2)}) collective-permute-start(bf16[6,16,3200]{2,1,0:T(8,128)(2,1)S(1)} %collective-permute-done.3.refs_4_), channel_id=1, source_target_pairs={{0,16},{1,17},{2,18},{3,19},{4,20},{5,21},{6,22},{7,23},{8,24},{9,... | collective-permute-start | bytes 1843208 | tf_op jit(solution)/shard_map/ppermute | solution.py:47
  39.0 1.6 %collective-permute-done.4.refs_5_ = bf16[6,16,3200]{2,1,0:T(8,128)(2,1)S(1)} collective-permute-done((bf16[6,16,3200]{2,1,0:T(8,128)(2,1)S(1)}, bf16[6,16,3200]{2,1,0:T(8,128)(2,1)S(1)}, u32[]{:S(2)}, u32[]{:S(2)}) %collective-permute-start.4) | collective-permute-done | bytes 614432 | tf_op jit(solution)/shard_map/ppermute | solution.py:47
  41.5 3.4 %shard_map.38 = (bf16[768,3072]{1,0:T(8,128)(2,1)S(1)}, bf16[3072,768]{1,0:T(8,128)(2,1)S(1)}) custom-call(s32[4]{0:T(128)S(1)} %pad_add_fusion.at, bf16[6,16,3200]{2,1,0:T(8,128)(2,1)S(1)} %get-tuple-element.27.refs_0_, bf16[6,16,3200]{2,1,0:T(8,128)(2,1)S(1)} %collective-permute-done.refs_1_, bf16[6,16,3200]{2,1,0:T(8,128)(2,1)S(1)} %collective-permute-done.1.refs_2_, ...), custom_call_target="tpu_custom_call" | custom-call | flops 603979776 | bytes 14155776 | tf_op jit(solution)/shard_map/pallas_call | solution.py:136
  45.0 3.2 %shard_map.40 = s16[784,1024]{1,0:T(8,128)(2,1)S(1)} custom-call(s32[4]{0:T(128)S(1)} %pad_add_fusion.at, bf16[768,3072]{1,0:T(8,128)(2,1)S(1)} %get-tuple-element.31.rows, bf16[3072,768]{1,0:T(8,128)(2,1)S(1)} %get-tuple-element.32.turned), custom_call_target="tpu_custom_call" | custom-call | flops 1207959552 | bytes 1572864 | tf_op jit(solution)/shard_map/pallas_call | solution.py:195
  49.6 3.2 %shard_map.42 = s16[784,1024]{1,0:T(8,128)(2,1)S(1)} custom-call(s32[4]{0:T(128)S(1)} %pad_add_fusion.at, bf16[768,3072]{1,0:T(8,128)(2,1)S(1)} %get-tuple-element.31.rows, bf16[3072,768]{1,0:T(8,128)(2,1)S(1)} %get-tuple-element.32.turned), custom_call_target="tpu_custom_call" | custom-call | flops 1207959552 | bytes 1572864 | tf_op jit(solution)/shard_map/pallas_call | solution.py:195
  52.8 3.2 %shard_map.41 = s16[784,1024]{1,0:T(8,128)(2,1)S(1)} custom-call(s32[4]{0:T(128)S(1)} %pad_add_fusion.at, bf16[768,3072]{1,0:T(8,128)(2,1)S(1)} %get-tuple-element.31.rows, bf16[3072,768]{1,0:T(8,128)(2,1)S(1)} %get-tuple-element.32.turned), custom_call_target="tpu_custom_call" | custom-call | flops 1207959552 | bytes 1572864 | tf_op jit(solution)/shard_map/pallas_call | solution.py:195
  56.0 2.7 %collective-permute-start.8 = (s16[784,1024]{1,0:T(8,128)(2,1)S(1)}, s16[784,1024]{1,0:T(8,128)(2,1)S(1)}, u32[]{:S(2)}, u32[]{:S(2)}) collective-permute-start(s16[784,1024]{1,0:T(8,128)(2,1)S(1)} %shard_map.41), channel_id=1, source_target_pairs={{0,8},{1,9},{2,10},{3,11},{4,12},{5,13},{6,14},{7,15},{8,0},{9,1},... | collective-permute-start | bytes 4816904 | tf_op jit(solution)/shard_map/ppermute | solution.py:47
  59.7 2.9 %shard_map.46 = s16[3136,128]{1,0:T(8,128)(2,1)S(1)} custom-call(s32[4]{0:T(128)S(1)} %pad_add_fusion.at, bf16[768,3072]{1,0:T(8,128)(2,1)S(1)} %get-tuple-element.31.rows, bf16[3072,768]{1,0:T(8,128)(2,1)S(1)} %get-tuple-element.32.turned), custom_call_target="tpu_custom_call" | custom-call | flops 603979776 | bytes 786432 | tf_op jit(solution)/shard_map/pallas_call | solution.py:218
  62.8 2.9 %shard_map.47 = s16[3136,128]{1,0:T(8,128)(2,1)S(1)} custom-call(s32[4]{0:T(128)S(1)} %pad_add_fusion.at, bf16[768,3072]{1,0:T(8,128)(2,1)S(1)} %get-tuple-element.31.rows, bf16[3072,768]{1,0:T(8,128)(2,1)S(1)} %get-tuple-element.32.turned), custom_call_target="tpu_custom_call" | custom-call | flops 603979776 | bytes 786432 | tf_op jit(solution)/shard_map/pallas_call | solution.py:218
  65.6 2.2 %collective-permute-start.17 = (s16[3136,128]{1,0:T(8,128)(2,1)S(1)}, s16[3136,128]{1,0:T(8,128)(2,1)S(1)}, u32[]{:S(2)}, u32[]{:S(2)}) collective-permute-start(s16[3136,128]{1,0:T(8,128)(2,1)S(1)} %shard_map.47), channel_id=1, source_target_pairs={{0,64},{1,65},{2,66},{3,67},{4,68},{5,69},{6,70},{7,71},{8,72},{9,... | collective-permute-start | bytes 2408456 | tf_op jit(solution)/shard_map/ppermute | solution.py:47
  67.8 2.9 %shard_map.48 = s16[3136,128]{1,0:T(8,128)(2,1)S(1)} custom-call(s32[4]{0:T(128)S(1)} %pad_add_fusion.at, bf16[768,3072]{1,0:T(8,128)(2,1)S(1)} %get-tuple-element.31.rows, bf16[3072,768]{1,0:T(8,128)(2,1)S(1)} %get-tuple-element.32.turned), custom_call_target="tpu_custom_call" | custom-call | flops 603979776 | bytes 786432 | tf_op jit(solution)/shard_map/pallas_call | solution.py:218
  71.7 2.7 %shard_map.39.own = f32[768,1024]{1,0:T(8,128)S(1)} custom-call(s32[4]{0:T(128)S(1)} %pad_add_fusion.at, bf16[768,3072]{1,0:T(8,128)(2,1)S(1)} %get-tuple-element.31.rows, bf16[3072,768]{1,0:T(8,128)(2,1)S(1)} %get-tuple-element.32.turned), custom_call_target="tpu_custom_call" | custom-call | flops 1207959552 | bytes 1572864 | tf_op jit(solution)/shard_map/pallas_call | solution.py:195
  74.5 13.4 %collective-permute-done.8.b = s16[784,1024]{1,0:T(8,128)(2,1)S(1)} collective-permute-done((s16[784,1024]{1,0:T(8,128)(2,1)S(1)}, s16[784,1024]{1,0:T(8,128)(2,1)S(1)}, u32[]{:S(2)}, u32[]{:S(2)}) %collective-permute-start.8) | collective-permute-done | bytes 1605664 | tf_op jit(solution)/shard_map/ppermute | solution.py:47
  87.8 5.9 %collective-permute-done.9.d = s16[784,1024]{1,0:T(8,128)(2,1)S(1)} collective-permute-done((s16[784,1024]{1,0:T(8,128)(2,1)S(1)}, s16[784,1024]{1,0:T(8,128)(2,1)S(1)}, u32[]{:S(2)}, u32[]{:S(2)}) %collective-permute-start.9) | collective-permute-done | bytes 1605664 | tf_op jit(solution)/shard_map/ppermute | solution.py:47
  93.8 3.2 %shard_map.43 = (f32[192,1024]{1,0:T(8,128)S(1)}, s16[208,1024]{1,0:T(8,128)(2,1)S(1)}, s16[208,1024]{1,0:T(8,128)(2,1)S(1)}, s16[208,1024]{1,0:T(8,128)(2,1)S(1)}) custom-call(s32[4]{0:T(128)S(1)} %pad_add_fusion.at, f32[768,1024]{1,0:T(8,128)S(1)} %shard_map.39.own, s16[784,1024]{1,0:T(8,128)(2,1)S(1)} %collective-permute-done.7.a, ...), custom_call_target="tpu_custom_call" | custom-call | flops 12582912 | bytes 7864320 | tf_op jit(solution)/shard_map/pallas_call | solution.py:281
  98.2 2.5 %collective-permute-start.11 = (s16[208,1024]{1,0:T(8,128)(2,1)S(1)}, s16[208,1024]{1,0:T(8,128)(2,1)S(1)}, u32[]{:S(2)}, u32[]{:S(2)}) collective-permute-start(s16[208,1024]{1,0:T(8,128)(2,1)S(1)} %get-tuple-element.35), channel_id=1, source_target_pairs={{0,2},{1,3},{2,0},{3,1},{4,6},{5,7},{6,4},{7,5},{8,10},{9,11},{10,... | collective-permute-start | bytes 1277960 | tf_op jit(solution)/shard_map/ppermute | solution.py:47
  101.9 2.6 %shard_map.45.own = f32[3072,128]{1,0:T(8,128)S(1)} custom-call(s32[4]{0:T(128)S(1)} %pad_add_fusion.at, bf16[768,3072]{1,0:T(8,128)(2,1)S(1)} %get-tuple-element.31.rows, bf16[3072,768]{1,0:T(8,128)(2,1)S(1)} %get-tuple-element.32.turned), custom_call_target="tpu_custom_call" | custom-call | flops 603979776 | bytes 786432 | tf_op jit(solution)/shard_map/pallas_call | solution.py:218
  104.5 1.5 %shard_map.49 = (f32[768,128]{1,0:T(8,128)S(1)}, s16[784,128]{1,0:T(8,128)(2,1)S(1)}, s16[784,128]{1,0:T(8,128)(2,1)S(1)}, s16[784,128]{1,0:T(8,128)(2,1)S(1)}) custom-call(s32[4]{0:T(128)S(1)} %pad_add_fusion.at, f32[3072,128]{1,0:T(8,128)S(1)} %shard_map.45.own, s16[3136,128]{1,0:T(8,128)(2,1)S(1)} %collective-permute-done.16.a, ...), custom_call_target="tpu_custom_call" | custom-call | flops 6291456 | bytes 3932160 | tf_op jit(solution)/shard_map/pallas_call | solution.py:245
  107.4 2.1 %collective-permute-start.20 = (s16[784,128]{1,0:T(8,128)(2,1)S(1)}, s16[784,128]{1,0:T(8,128)(2,1)S(1)}, u32[]{:S(2)}, u32[]{:S(2)}) collective-permute-start(s16[784,128]{1,0:T(8,128)(2,1)S(1)} %get-tuple-element.43), channel_id=1, source_target_pairs={{0,8},{1,9},{2,10},{3,11},{4,12},{5,13},{6,14},{7,15},{8,0},{9,1},... | collective-permute-start | bytes 602120 | tf_op jit(solution)/shard_map/ppermute | solution.py:47
  109.5 5.5 %collective-permute-done.19.a = s16[784,128]{1,0:T(8,128)(2,1)S(1)} collective-permute-done((s16[784,128]{1,0:T(8,128)(2,1)S(1)}, s16[784,128]{1,0:T(8,128)(2,1)S(1)}, u32[]{:S(2)}, u32[]{:S(2)}) %collective-permute-start.19) | collective-permute-done | bytes 200736 | tf_op jit(solution)/shard_map/ppermute | solution.py:47
  115.4 2.1 %collective-permute-done.20.b = s16[784,128]{1,0:T(8,128)(2,1)S(1)} collective-permute-done((s16[784,128]{1,0:T(8,128)(2,1)S(1)}, s16[784,128]{1,0:T(8,128)(2,1)S(1)}, u32[]{:S(2)}, u32[]{:S(2)}) %collective-permute-start.20) | collective-permute-done | bytes 200736 | tf_op jit(solution)/shard_map/ppermute | solution.py:47
  117.5 2.4 %collective-permute-done.21.d = s16[784,128]{1,0:T(8,128)(2,1)S(1)} collective-permute-done((s16[784,128]{1,0:T(8,128)(2,1)S(1)}, s16[784,128]{1,0:T(8,128)(2,1)S(1)}, u32[]{:S(2)}, u32[]{:S(2)}) %collective-permute-start.21) | collective-permute-done | bytes 200736 | tf_op jit(solution)/shard_map/ppermute | solution.py:47
  122.1 3.5 %collective-permute-start.13 = (s16[208,256]{1,0:T(8,128)(2,1)S(1)}, s16[208,256]{1,0:T(8,128)(2,1)S(1)}, u32[]{:S(2)}, u32[]{:S(2)}) collective-permute-start(s16[208,256]{1,0:T(8,128)(2,1)S(1)} %get-tuple-element.38), channel_id=1, source_target_pairs={{0,32},{1,33},{2,34},{3,35},{4,36},{5,37},{6,38},{7,39},{8,40},{9,... | collective-permute-start | bytes 319496 | tf_op jit(solution)/shard_map/ppermute | solution.py:47
  125.7 2.6 %collective-permute-start.14 = (s16[208,256]{1,0:T(8,128)(2,1)S(1)}, s16[208,256]{1,0:T(8,128)(2,1)S(1)}, u32[]{:S(2)}, u32[]{:S(2)}) collective-permute-start(s16[208,256]{1,0:T(8,128)(2,1)S(1)} %get-tuple-element.39), channel_id=1, source_target_pairs={{0,64},{1,65},{2,66},{3,67},{4,68},{5,69},{6,70},{7,71},{8,72},{9,... | collective-permute-start | bytes 319496 | tf_op jit(solution)/shard_map/ppermute | solution.py:47
  128.3 2.6 %collective-permute-start.23 = (s16[208,128]{1,0:T(8,128)(2,1)S(1)}, s16[208,128]{1,0:T(8,128)(2,1)S(1)}, u32[]{:S(2)}, u32[]{:S(2)}) collective-permute-start(s16[208,128]{1,0:T(8,128)(2,1)S(1)} %get-tuple-element.47), channel_id=1, source_target_pairs={{0,2},{1,3},{2,0},{3,1},{4,6},{5,7},{6,4},{7,5},{8,10},{9,11},{10,... | collective-permute-start | bytes 159752 | tf_op jit(solution)/shard_map/ppermute | solution.py:47
  (41 shorter events, 18.2 us)
Async XLA Ops:
  0.8 1.7 %copy-start = (bf16[16,24,3072]{2,1,0:T(8,128)(2,1)S(1)}, bf16[16,24,3072]{2,1,0:T(8,128)(2,1)}, u32[]{:S(2)}) copy-start(bf16[16,24,3072]{2,1,0:T(8,128)(2,1)} %half.1) | copy-start | bytes 7077892
  2.5 0.7 copy-start.1
  5.2 18.2 %collective-permute-start.1 = (bf16[6,16,3200]{2,1,0:T(8,128)(2,1)S(1)}, bf16[6,16,3200]{2,1,0:T(8,128)(2,1)S(1)}, u32[]{:S(2)}, u32[]{:S(2)}) collective-permute-start(bf16[6,16,3200]{2,1,0:T(8,128)(2,1)S(1)} %get-tuple-element.28), channel_id=1, source_target_pairs={{0,32},{1,33},{2,34},{3,35},{4,36},{5,37},{6,38},{7,39},{8,40},{9,... | collective-permute-start | bytes 1843208 | tf_op jit(solution)/shard_map/ppermute | solution.py:47
  7.7 29.7 %collective-permute-start.3 = (bf16[6,16,3200]{2,1,0:T(8,128)(2,1)S(1)}, bf16[6,16,3200]{2,1,0:T(8,128)(2,1)S(1)}, u32[]{:S(2)}, u32[]{:S(2)}) collective-permute-start(bf16[6,16,3200]{2,1,0:T(8,128)(2,1)S(1)} %get-tuple-element.29), channel_id=1, source_target_pairs={{0,64},{1,65},{2,66},{3,67},{4,68},{5,69},{6,70},{7,71},{8,72},{9,... | collective-permute-start | bytes 1843208 | tf_op jit(solution)/shard_map/ppermute | solution.py:47
  11.0 28.0 %collective-permute-start.5 = (bf16[6,16,3200]{2,1,0:T(8,128)(2,1)S(1)}, bf16[6,16,3200]{2,1,0:T(8,128)(2,1)S(1)}, u32[]{:S(2)}, u32[]{:S(2)}) collective-permute-start(bf16[6,16,3200]{2,1,0:T(8,128)(2,1)S(1)} %get-tuple-element.30), channel_id=1, source_target_pairs={{0,96},{1,97},{2,98},{3,99},{4,100},{5,101},{6,102},{7,103},{8,104... | collective-permute-start | bytes 1843208 | tf_op jit(solution)/shard_map/ppermute | solution.py:47
  11.8 27.3 %collective-permute-start = (bf16[6,16,3200]{2,1,0:T(8,128)(2,1)S(1)}, bf16[6,16,3200]{2,1,0:T(8,128)(2,1)S(1)}, u32[]{:S(2)}, u32[]{:S(2)}) collective-permute-start(bf16[6,16,3200]{2,1,0:T(8,128)(2,1)S(1)} %get-tuple-element.27.refs_0_), channel_id=1, source_target_pairs={{0,16},{1,17},{2,18},{3,19},{4,20},{5,21},{6,22},{7,23},{8,24},{9,... | collective-permute-start | bytes 1843208 | tf_op jit(solution)/shard_map/ppermute | solution.py:47
  23.4 15.6 %collective-permute-start.2 = (bf16[6,16,3200]{2,1,0:T(8,128)(2,1)S(1)}, bf16[6,16,3200]{2,1,0:T(8,128)(2,1)S(1)}, u32[]{:S(2)}, u32[]{:S(2)}) collective-permute-start(bf16[6,16,3200]{2,1,0:T(8,128)(2,1)S(1)} %collective-permute-done.1.refs_2_), channel_id=1, source_target_pairs={{0,16},{1,17},{2,18},{3,19},{4,20},{5,21},{6,22},{7,23},{8,24},{9,... | collective-permute-start | bytes 1843208 | tf_op jit(solution)/shard_map/ppermute | solution.py:47
  37.5 3.2 %collective-permute-start.4 = (bf16[6,16,3200]{2,1,0:T(8,128)(2,1)S(1)}, bf16[6,16,3200]{2,1,0:T(8,128)(2,1)S(1)}, u32[]{:S(2)}, u32[]{:S(2)}) collective-permute-start(bf16[6,16,3200]{2,1,0:T(8,128)(2,1)S(1)} %collective-permute-done.3.refs_4_), channel_id=1, source_target_pairs={{0,16},{1,17},{2,18},{3,19},{4,20},{5,21},{6,22},{7,23},{8,24},{9,... | collective-permute-start | bytes 1843208 | tf_op jit(solution)/shard_map/ppermute | solution.py:47
  39.0 2.5 %collective-permute-start.6 = (bf16[6,16,3200]{2,1,0:T(8,128)(2,1)S(1)}, bf16[6,16,3200]{2,1,0:T(8,128)(2,1)S(1)}, u32[]{:S(2)}, u32[]{:S(2)}) collective-permute-start(bf16[6,16,3200]{2,1,0:T(8,128)(2,1)S(1)} %collective-permute-done.5.refs_6_), channel_id=1, source_target_pairs={{0,16},{1,17},{2,18},{3,19},{4,20},{5,21},{6,22},{7,23},{8,24},{9,... | collective-permute-start | bytes 1843208 | tf_op jit(solution)/shard_map/ppermute | solution.py:47
  48.2 22.5 %collective-permute-start.7 = (s16[784,1024]{1,0:T(8,128)(2,1)S(1)}, s16[784,1024]{1,0:T(8,128)(2,1)S(1)}, u32[]{:S(2)}, u32[]{:S(2)}) collective-permute-start(s16[784,1024]{1,0:T(8,128)(2,1)S(1)} %shard_map.40), channel_id=1, source_target_pairs={{0,4},{1,5},{2,6},{3,7},{4,8},{5,9},{6,10},{7,11},{8,12},{9,13},{1... | collective-permute-start | bytes 4816904 | tf_op jit(solution)/shard_map/ppermute | solution.py:47
  56.0 31.9 %collective-permute-start.8 = (s16[784,1024]{1,0:T(8,128)(2,1)S(1)}, s16[784,1024]{1,0:T(8,128)(2,1)S(1)}, u32[]{:S(2)}, u32[]{:S(2)}) collective-permute-start(s16[784,1024]{1,0:T(8,128)(2,1)S(1)} %shard_map.41), channel_id=1, source_target_pairs={{0,8},{1,9},{2,10},{3,11},{4,12},{5,13},{6,14},{7,15},{8,0},{9,1},... | collective-permute-start | bytes 4816904 | tf_op jit(solution)/shard_map/ppermute | solution.py:47
  58.7 35.1 %collective-permute-start.9 = (s16[784,1024]{1,0:T(8,128)(2,1)S(1)}, s16[784,1024]{1,0:T(8,128)(2,1)S(1)}, u32[]{:S(2)}, u32[]{:S(2)}) collective-permute-start(s16[784,1024]{1,0:T(8,128)(2,1)S(1)} %shard_map.42), channel_id=1, source_target_pairs={{0,12},{1,13},{2,14},{3,15},{4,0},{5,1},{6,2},{7,3},{8,4},{9,5},{1... | collective-permute-start | bytes 4816904 | tf_op jit(solution)/shard_map/ppermute | solution.py:47
  62.6 38.1 %collective-permute-start.16 = (s16[3136,128]{1,0:T(8,128)(2,1)S(1)}, s16[3136,128]{1,0:T(8,128)(2,1)S(1)}, u32[]{:S(2)}, u32[]{:S(2)}) collective-permute-start(s16[3136,128]{1,0:T(8,128)(2,1)S(1)} %shard_map.46), channel_id=1, source_target_pairs={{0,32},{1,33},{2,34},{3,35},{4,36},{5,37},{6,38},{7,39},{8,40},{9,... | collective-permute-start | bytes 2408456 | tf_op jit(solution)/shard_map/ppermute | solution.py:47
  65.6 38.8 %collective-permute-start.17 = (s16[3136,128]{1,0:T(8,128)(2,1)S(1)}, s16[3136,128]{1,0:T(8,128)(2,1)S(1)}, u32[]{:S(2)}, u32[]{:S(2)}) collective-permute-start(s16[3136,128]{1,0:T(8,128)(2,1)S(1)} %shard_map.47), channel_id=1, source_target_pairs={{0,64},{1,65},{2,66},{3,67},{4,68},{5,69},{6,70},{7,71},{8,72},{9,... | collective-permute-start | bytes 2408456 | tf_op jit(solution)/shard_map/ppermute | solution.py:47
  70.7 33.8 %collective-permute-start.18 = (s16[3136,128]{1,0:T(8,128)(2,1)S(1)}, s16[3136,128]{1,0:T(8,128)(2,1)S(1)}, u32[]{:S(2)}, u32[]{:S(2)}) collective-permute-start(s16[3136,128]{1,0:T(8,128)(2,1)S(1)} %shard_map.48), channel_id=1, source_target_pairs={{0,96},{1,97},{2,98},{3,99},{4,100},{5,101},{6,102},{7,103},{8,104... | collective-permute-start | bytes 2408456 | tf_op jit(solution)/shard_map/ppermute | solution.py:47
  97.0 24.1 %collective-permute-start.10 = (s16[208,1024]{1,0:T(8,128)(2,1)S(1)}, s16[208,1024]{1,0:T(8,128)(2,1)S(1)}, u32[]{:S(2)}, u32[]{:S(2)}) collective-permute-start(s16[208,1024]{1,0:T(8,128)(2,1)S(1)} %get-tuple-element.34), channel_id=1, source_target_pairs={{0,1},{1,2},{2,3},{3,0},{4,5},{5,6},{6,7},{7,4},{8,9},{9,10},{10,1... | collective-permute-start | bytes 1277960 | tf_op jit(solution)/shard_map/ppermute | solution.py:47
  98.2 22.9 %collective-permute-start.11 = (s16[208,1024]{1,0:T(8,128)(2,1)S(1)}, s16[208,1024]{1,0:T(8,128)(2,1)S(1)}, u32[]{:S(2)}, u32[]{:S(2)}) collective-permute-start(s16[208,1024]{1,0:T(8,128)(2,1)S(1)} %get-tuple-element.35), channel_id=1, source_target_pairs={{0,2},{1,3},{2,0},{3,1},{4,6},{5,7},{6,4},{7,5},{8,10},{9,11},{10,... | collective-permute-start | bytes 1277960 | tf_op jit(solution)/shard_map/ppermute | solution.py:47
  100.7 20.4 %collective-permute-start.12 = (s16[208,1024]{1,0:T(8,128)(2,1)S(1)}, s16[208,1024]{1,0:T(8,128)(2,1)S(1)}, u32[]{:S(2)}, u32[]{:S(2)}) collective-permute-start(s16[208,1024]{1,0:T(8,128)(2,1)S(1)} %get-tuple-element.36), channel_id=1, source_target_pairs={{0,3},{1,0},{2,1},{3,2},{4,7},{5,4},{6,5},{7,6},{8,11},{9,8},{10,9... | collective-permute-start | bytes 1277960 | tf_op jit(solution)/shard_map/ppermute | solution.py:47
  106.0 9.1 %collective-permute-start.19 = (s16[784,128]{1,0:T(8,128)(2,1)S(1)}, s16[784,128]{1,0:T(8,128)(2,1)S(1)}, u32[]{:S(2)}, u32[]{:S(2)}) collective-permute-start(s16[784,128]{1,0:T(8,128)(2,1)S(1)} %get-tuple-element.42), channel_id=1, source_target_pairs={{0,4},{1,5},{2,6},{3,7},{4,8},{5,9},{6,10},{7,11},{8,12},{9,13},{1... | collective-permute-start | bytes 602120 | tf_op jit(solution)/shard_map/ppermute | solution.py:47
  107.4 10.1 %collective-permute-start.20 = (s16[784,128]{1,0:T(8,128)(2,1)S(1)}, s16[784,128]{1,0:T(8,128)(2,1)S(1)}, u32[]{:S(2)}, u32[]{:S(2)}) collective-permute-start(s16[784,128]{1,0:T(8,128)(2,1)S(1)} %get-tuple-element.43), channel_id=1, source_target_pairs={{0,8},{1,9},{2,10},{3,11},{4,12},{5,13},{6,14},{7,15},{8,0},{9,1},... | collective-permute-start | bytes 602120 | tf_op jit(solution)/shard_map/ppermute | solution.py:47
  115.1 4.9 %collective-permute-start.21 = (s16[784,128]{1,0:T(8,128)(2,1)S(1)}, s16[784,128]{1,0:T(8,128)(2,1)S(1)}, u32[]{:S(2)}, u32[]{:S(2)}) collective-permute-start(s16[784,128]{1,0:T(8,128)(2,1)S(1)} %get-tuple-element.44), channel_id=1, source_target_pairs={{0,12},{1,13},{2,14},{3,15},{4,0},{5,1},{6,2},{7,3},{8,4},{9,5},{1... | collective-permute-start | bytes 602120 | tf_op jit(solution)/shard_map/ppermute | solution.py:47
  120.7 10.1 %collective-permute-start.22 = (s16[208,128]{1,0:T(8,128)(2,1)S(1)}, s16[208,128]{1,0:T(8,128)(2,1)S(1)}, u32[]{:S(2)}, u32[]{:S(2)}) collective-permute-start(s16[208,128]{1,0:T(8,128)(2,1)S(1)} %get-tuple-element.46), channel_id=1, source_target_pairs={{0,1},{1,2},{2,3},{3,0},{4,5},{5,6},{6,7},{7,4},{8,9},{9,10},{10,1... | collective-permute-start | bytes 159752 | tf_op jit(solution)/shard_map/ppermute | solution.py:47
  122.1 11.7 %collective-permute-start.13 = (s16[208,256]{1,0:T(8,128)(2,1)S(1)}, s16[208,256]{1,0:T(8,128)(2,1)S(1)}, u32[]{:S(2)}, u32[]{:S(2)}) collective-permute-start(s16[208,256]{1,0:T(8,128)(2,1)S(1)} %get-tuple-element.38), channel_id=1, source_target_pairs={{0,32},{1,33},{2,34},{3,35},{4,36},{5,37},{6,38},{7,39},{8,40},{9,... | collective-permute-start | bytes 319496 | tf_op jit(solution)/shard_map/ppermute | solution.py:47
  125.7 8.2 %collective-permute-start.14 = (s16[208,256]{1,0:T(8,128)(2,1)S(1)}, s16[208,256]{1,0:T(8,128)(2,1)S(1)}, u32[]{:S(2)}, u32[]{:S(2)}) collective-permute-start(s16[208,256]{1,0:T(8,128)(2,1)S(1)} %get-tuple-element.39), channel_id=1, source_target_pairs={{0,64},{1,65},{2,66},{3,67},{4,68},{5,69},{6,70},{7,71},{8,72},{9,... | collective-permute-start | bytes 319496 | tf_op jit(solution)/shard_map/ppermute | solution.py:47
  128.3 5.6 %collective-permute-start.15 = (s16[208,256]{1,0:T(8,128)(2,1)S(1)}, s16[208,256]{1,0:T(8,128)(2,1)S(1)}, u32[]{:S(2)}, u32[]{:S(2)}) collective-permute-start(s16[208,256]{1,0:T(8,128)(2,1)S(1)} %get-tuple-element.40), channel_id=1, source_target_pairs={{0,96},{1,97},{2,98},{3,99},{4,100},{5,101},{6,102},{7,103},{8,104... | collective-permute-start | bytes 319496 | tf_op jit(solution)/shard_map/ppermute | solution.py:47
  128.3 4.6 %collective-permute-start.23 = (s16[208,128]{1,0:T(8,128)(2,1)S(1)}, s16[208,128]{1,0:T(8,128)(2,1)S(1)}, u32[]{:S(2)}, u32[]{:S(2)}) collective-permute-start(s16[208,128]{1,0:T(8,128)(2,1)S(1)} %get-tuple-element.47), channel_id=1, source_target_pairs={{0,2},{1,3},{2,0},{3,1},{4,6},{5,7},{6,4},{7,5},{8,10},{9,11},{10,... | collective-permute-start | bytes 159752 | tf_op jit(solution)/shard_map/ppermute | solution.py:47
  130.9 3.0 %collective-permute-start.24 = (s16[208,128]{1,0:T(8,128)(2,1)S(1)}, s16[208,128]{1,0:T(8,128)(2,1)S(1)}, u32[]{:S(2)}, u32[]{:S(2)}) collective-permute-start(s16[208,128]{1,0:T(8,128)(2,1)S(1)} %get-tuple-element.48), channel_id=1, source_target_pairs={{0,3},{1,0},{2,1},{3,2},{4,7},{5,4},{6,5},{7,6},{8,11},{9,8},{10,9... | collective-permute-start | bytes 159752 | tf_op jit(solution)/shard_map/ppermute | solution.py:47
where the time goes:
time: 135 us
  waiting for transfers between devices  56.5 us (42%)
  starting transfers between devices  38.6 us (29%)
  Pallas kernels  36.2 us (27%)
  local copies, waits for them, and re-layouts  2.44 us (2%)
    ppermute x25, waiting for transfers between devices, send(): return lax.ppermute(v, AXES, moves(shift))  56.5 us
    ppermute x25, starting transfers between devices, send(): return lax.ppermute(v, AXES, moves(shift))  38.6 us
    pallas_call x4, Pallas kernels, bulk_k(): pl.pallas_call(functools.partial(bulk_body, shift), grid=(RING,), out_sha...  12.3 us
    pallas_call x4, Pallas kernels, rest_k(): pl.pallas_call(functools.partial(rest_body, shift, skip), grid=(RING,), o...  11.2 us
    pallas_call x2, Pallas kernels, sum_rows(): pl.pallas_call(sum_rows_body, grid=(columns // wide,), out_shape=[jax.Sha...  3.93 us
    pallas_call x1, Pallas kernels, fit(): pl.pallas_call(fit_body, grid=(group,), out_shape=[jax.ShapeDtypeStruct((...  3.45 us
  transfers between devices with their start and end apart: 25, of which 11 were waited for; matrix products, arithmetic and copies ran while one was open for 0% of the time, Pallas kernels for 20%

commit v1 on v0

v1 whole, which is shorter than its diff:
```python
import functools

import jax
import jax.numpy as jnp
from jax import lax
from jax.experimental import pallas as pl
from jax.experimental.pallas import tpu as pltpu
from jax.sharding import Mesh
from jax.sharding import PartitionSpec as P


AXES = ("z", "c", "x", "y")
BF = jnp.bfloat16
F32 = jnp.float32
I16 = jnp.int16
MIB = 1 << 20
RING = 4
ORDER = (2, 1, 3, 0)
TAIL = 16


def whole():
    return pl.BlockSpec(memory_space=pltpu.VMEM)


def scalars():
    return pl.BlockSpec(memory_space=pltpu.SMEM)


def params(mib):
    return pltpu.CompilerParams(vmem_limit_bytes=mib * MIB)


def cost(flops, moved):
    return pl.CostEstimate(flops=flops, bytes_accessed=moved, transcendentals=0)


def place(z, c, x, y):
    return ((z % 4) * 2 + c) * 16 + (x % 4) * 4 + y % 4


def moves(shift):
    every = [(z, c, x, y) for z in range(4) for c in range(2) for x in range(4) for y in range(4)]
    return [(place(*d), place(*shift(*d))) for d in every]


def send(v, shift):
    return lax.ppermute(v, AXES, moves(shift))


def along_z(k):
    return lambda z, c, x, y: (z + k, c, x, y)


def other_core(z, c, x, y):
    return (z, 1 - c, x, y)


def first_axis(k):
    return lambda z, c, x, y: (z, c, x + k, y) if c == 0 else (z, c, x, y + k)


def second_axis(k):
    return lambda z, c, x, y: (z, c, x, y + k) if c == 0 else (z, c, x + k, y)


def screen_body(at, half, gate, metric, *outs_and_scratch):
    outs, turned = outs_and_scratch[:4], outs_and_scratch[4]
    lanes = 512

    def step(n, carry):
        cut = pl.ds(pl.multiple_of(n * lanes, lanes), lanes)
        kept = half[:, :, cut] * gate[:, cut][None]
        turned[:, :, cut] = jnp.swapaxes(kept.astype(F32), 0, 1).astype(BF)
        return carry

    ao = half.shape[2]
    lax.fori_loop(0, ao // lanes, step, 0)
    group = outs[0].shape[0]
    for k in range(RING):
        first = lax.rem(at[0] + k, RING) * group
        outs[k][:, :, :ao] = turned[pl.ds(first, group)]
        outs[k][:, :, ao:] = jnp.broadcast_to(metric[...][None], (group,) + metric.shape)


def screen(at, half, gate, metric):
    aux, occ, ao = half.shape
    out = jax.ShapeDtypeStruct((occ // RING, aux, ao + metric.shape[1]), BF)
    return pl.pallas_call(
        screen_body,
        out_shape=[out] * RING,
        in_specs=[scalars(), whole(), whole(), whole()],
        out_specs=[whole()] * RING,
        scratch_shapes=[pltpu.VMEM((occ, aux, ao), BF)],
        compiler_params=params(16),
        cost_estimate=cost(half.size, half.size * 4),
    )(at, half, gate, metric)


def fit_body(at, *refs):
    pieces, (bulk, rest, turned, mixed, fresh) = refs[:8], refs[8:]
    step = pl.program_id(0)
    ao = fresh.shape[1]
    aux = mixed.shape[0]
    part = aux // 8

    @pl.when(step == 0)
    def _():
        metric = jnp.concatenate([p[0][:, ao:] for p in pieces], axis=0)
        source = lax.broadcasted_iota(jnp.int32, (aux, aux), 0)
        n = lax.broadcasted_iota(jnp.int32, (aux, aux), 1)
        slot = n // part
        up = lax.rem(at[0] - slot // 2 + RING, RING)
        core = jnp.where(slot % 2 == 0, at[1], 1 - at[1])
        wanted = (up * 2 + core) * part + n % part
        pick = jnp.where(source == wanted, 1.0, 0.0).astype(BF)
        mixed[...] = jnp.dot(metric, pick, preferred_element_type=F32).astype(BF)

    screened = jnp.concatenate([p[0][:, :ao] for p in pieces], axis=0)
    fitted = jnp.dot(mixed[...], screened, preferred_element_type=F32).astype(BF)
    fresh[...] = fitted
    wide, narrow = bulk.shape[1] // RING, rest.shape[1] // RING
    for n in range(RING):
        column = n * (ao // RING) + at[1] * (wide + narrow)
        bulk[:, n * wide:(n + 1) * wide] = fresh[:, pl.ds(pl.multiple_of(column, 128), wide)]
        column = lax.rem(at[0] + ORDER[n], RING) * (ao // RING) + at[1] * (wide + narrow) + wide
        rest[:, n * narrow:(n + 1) * narrow] = fresh[:, pl.ds(pl.multiple_of(column, 128), narrow)]
    flipped = fitted.T
    cut = pl.ds(pl.multiple_of(step * aux, aux), aux)
    high = ao // (RING * RING)
    for x in range(RING):
        for y in range(RING):
            n = x * RING + y
            to = jnp.where(at[1] == 0, n, y * RING + x) * high
            turned[pl.ds(pl.multiple_of(to, 64), high), cut] = flipped[n * high:(n + 1) * high]


def fit(at, pieces):
    group, part, wide = pieces[0].shape
    aux = part * 8
    ao = wide - aux
    piece = pl.BlockSpec((1, part, wide), lambda i: (i, 0, 0))
    return pl.pallas_call(
        fit_body,
        grid=(group,),
        out_shape=[jax.ShapeDtypeStruct((group * aux, n), BF) for n in (ao // 3, ao // 6)]
        + [jax.ShapeDtypeStruct((ao, group * aux), BF)],
        in_specs=[scalars()] + [piece] * 8,
        out_specs=[pl.BlockSpec((aux, n), lambda i: (i, 0)) for n in (ao // 3, ao // 6)]
        + [pl.BlockSpec((ao, group * aux), lambda i: (0, 0))],
        scratch_shapes=[pltpu.VMEM((aux, aux), BF), pltpu.VMEM((aux, ao), BF)],
        compiler_params=params(28),
        cost_estimate=cost(2 * group * aux * aux * ao, group * aux * ao * 6),
    )(at, *pieces)


def exponent(top):
    return jnp.floor(14.9 - jnp.log2(jnp.maximum(top, 1e-30)))


def coded(v, e):
    return jnp.round(v * jnp.exp2(e)).astype(jnp.int32).astype(I16)


def marked(e):
    return jnp.broadcast_to(e, (TAIL, e.shape[1])).astype(jnp.int32).astype(I16)


def scale_of(tail):
    return jnp.exp2(-tail.astype(jnp.int32).astype(F32)[:1])


def plain(q):
    return q.astype(jnp.int32).astype(F32)


def write(out, first, block):
    if out.dtype == F32:
        out[first:first + block.shape[0], :] = block
    else:
        e = exponent(jnp.max(jnp.abs(block), axis=0, keepdims=True))
        end = first + block.shape[0]
        out[first:end, :] = coded(block, e)
        out[end:end + TAIL, :] = marked(e)


def bulk_body(shift, at, bulk, turned, out):
    total = turned.shape[0] // RING
    g = lax.rem(jnp.where(at[1] == 0, at[2], at[3]) + shift, RING)
    left = turned[pl.ds(pl.multiple_of(g * total, 256), total), :]
    write(out, 0, jnp.dot(left, bulk[...], preferred_element_type=F32))


def bulk_k(at, bulk, turned, shift):
    depth, columns = bulk.shape
    total = turned.shape[0] // RING
    shape = (total + (TAIL if shift else 0), columns)
    half = columns // 2
    return pl.pallas_call(
        functools.partial(bulk_body, shift),
        grid=(2,),
        out_shape=jax.ShapeDtypeStruct(shape, I16 if shift else F32),
        in_specs=[scalars(), pl.BlockSpec((depth, half), lambda j: (0, j)), whole()],
        out_specs=pl.BlockSpec((shape[0], half), lambda j: (0, j)),
        compiler_params=params(28),
        cost_estimate=cost(2 * depth * total * columns, total * columns * 2),
    )(at, bulk, turned)


def rest_body(rest, turned, *outs):
    both = jnp.dot(turned[...], rest[...], preferred_element_type=F32)
    narrow = both.shape[1] // 2
    write(outs[0], 0, both[:, :narrow])
    write(outs[1], 0, both[:, narrow:])


def rest_k(rest, turned, pair):
    depth = rest.shape[0]
    ao = turned.shape[0]
    total, narrow = ao // RING, rest.shape[1] // RING
    each = [total + (TAIL if k else 0) for k in ORDER[2 * pair:2 * pair + 2]]
    return pl.pallas_call(
        rest_body,
        grid=(RING,),
        out_shape=[jax.ShapeDtypeStruct((RING * n, narrow), I16 if n > total else F32) for n in each],
        in_specs=[
            pl.BlockSpec((depth, 2 * narrow), lambda g: (0, pair)),
            pl.BlockSpec((total, depth), lambda g: (g, 0)),
        ],
        out_specs=[pl.BlockSpec((n, narrow), lambda g: (g, 0)) for n in each],
        compiler_params=params(28),
        cost_estimate=cost(4 * depth * ao * narrow, ao * narrow * 4),
    )(rest, turned)


def second_body(at, bulk, ba, bb, bd, rest, ra, rb, rd, kept, *outs):
    high = kept.shape[0]
    wide = kept.shape[1]
    total = bulk.shape[0]
    h = jnp.where(at[1] == 0, at[3], at[2])

    def part(k, own, arrived, first, lanes):
        row = pl.multiple_of(lax.rem(h + k, RING) * high, 64)
        v = own[pl.ds(pl.multiple_of(first * total + row, 64), high), :]
        for m in arrived:
            start = first * (total + TAIL)
            v = v + plain(m[pl.ds(pl.multiple_of(start + row, 16), high), :]) * scale_of(
                m[start + total:start + total + TAIL, :]
            )
        if k == 0:
            kept[:, lanes] = v
        else:
            e = exponent(jnp.max(jnp.abs(v), axis=0, keepdims=True))
            outs[k - 1][:high, lanes] = coded(v, e)
            outs[k - 1][high:, lanes] = marked(e)

    @pl.when(pl.program_id(0) < RING)
    def _():
        for k in range(RING):
            part(k, bulk, (ba, bb, bd), 0, slice(0, wide))

    @pl.when(pl.program_id(0) >= RING)
    def _():
        for k in range(RING):
            for n in range(2):
                part(k, rest, (ra, rb, rd), n, slice(n * wide // 2, (n + 1) * wide // 2))


def second(at, bulk, rest):
    total, columns = bulk[0].shape
    wide, high = columns // RING, total // RING
    narrow = wide // 2
    every = columns + RING * narrow

    def of_bulk(rows):
        return pl.BlockSpec((rows, wide), lambda j: (0, jnp.minimum(j, RING - 1)))

    def of_rest(rows):
        return pl.BlockSpec((2 * rows, narrow), lambda j: (jnp.maximum(j - RING, 0), 0))

    return pl.pallas_call(
        second_body,
        grid=(RING + 2,),
        out_shape=[jax.ShapeDtypeStruct((high, every), F32)]
        + [jax.ShapeDtypeStruct((high + TAIL, every), I16)] * 3,
        in_specs=[scalars(), of_bulk(total)] + [of_bulk(total + TAIL)] * 3
        + [of_rest(total)] + [of_rest(total + TAIL)] * 3,
        out_specs=[pl.BlockSpec((n, wide), lambda j: (0, j)) for n in [high] + [high + TAIL] * 3],
        compiler_params=params(24),
        cost_estimate=cost(total * every * 16, total * every * 10),
        name="second_sum",
    )(at, *bulk, *rest)


def third_body(at, own, a, b, d, bulk, b1, b2, b3, rest, r1, r2, r3):
    high, wide = bulk.shape
    narrow = rest.shape[1]
    g = jnp.where(at[1] == 0, at[2], at[3])
    for base, step, place_at, outs in (
        (0, wide, at[0], (bulk, b1, b2, b3)), (RING * wide, narrow, g, (rest, r1, r2, r3))
    ):
        for k in range(RING):
            cut = pl.ds(pl.multiple_of(base + lax.rem(place_at + k, RING) * step, 128), step)
            v = own[:, cut]
            for m in (a, b, d):
                v = v + plain(m[:high, cut]) * scale_of(m[high:, cut])
            write(outs[k], 0, v)


def third(at, own, arrived, wide, narrow):
    high = own.shape[0]

    def four(lanes):
        return [jax.ShapeDtypeStruct((high, lanes), F32)] + [jax.ShapeDtypeStruct((high + TAIL, lanes), I16)] * 3

    out = pl.pallas_call(
        third_body,
        out_shape=four(wide) + four(narrow),
        in_specs=[scalars()] + [whole()] * 4,
        out_specs=[whole()] * 8,
        compiler_params=params(16),
        cost_estimate=cost(own.size * 16, own.size * 10),
        name="third_sum",
    )(at, own, *arrived)
    return list(out[:4]), list(out[4:])


def finish_body(own, a, b, d, rest, ra, rb, rd, out):
    high, wide = own.shape
    for first, v, arrived in ((0, own[...], (a, b, d)), (wide, rest[...], (ra, rb, rd))):
        for m in arrived:
            v = v + plain(m[:high, :]) * scale_of(m[high:, :])
        out[:, first:first + v.shape[1]] = v


def finish(bulk, rest):
    high = bulk[0].shape[0]
    ao = bulk[0].shape[1] + rest[0].shape[1]
    return pl.pallas_call(
        finish_body,
        out_shape=jax.ShapeDtypeStruct((high, ao), F32),
        in_specs=[whole()] * 8,
        out_specs=whole(),
        compiler_params=params(8),
        cost_estimate=cost(high * ao * 8, high * ao * 14),
    )(*bulk, *rest)


def shards(half, metric, survive):
    _, _, ao = half.shape
    at = jnp.stack([lax.axis_index(a) for a in AXES]).astype(jnp.int32)
    blocks = survive.shape[2]
    gate = jnp.repeat(survive.reshape(1, blocks).astype(BF), ao // blocks, axis=1)
    wide = ao // 8

    parts = screen(at, half, gate, metric)
    here = [parts[0]] + [None] * 3
    for k in (2, 1, 3):
        here[k] = send(parts[k], along_z(k))
    there = [send(v, other_core) for v in here]
    bulk_rows, rest_rows, turned = fit(at, [v for pair in zip(here, there) for v in pair])

    bulk, rest = [None] * 4, [None] * 4

    def bulk_step(k):
        bulk[k] = bulk_k(at, bulk_rows, turned, k)
        if k:
            bulk[k] = send(bulk[k], first_axis(k))

    def rest_step(pair):
        out = rest_k(rest_rows, turned, pair)
        for k, v in zip(ORDER[2 * pair:2 * pair + 2], out):
            rest[k] = send(v, along_z(k)) if k else v

    bulk_step(2)
    rest_step(0)
    bulk_step(1)
    bulk_step(3)
    rest_step(1)
    bulk_step(0)
    own, *out = second(at, bulk, rest)
    arrived = [send(out[k - 1], second_axis(k)) for k in (2, 1, 3)]
    bulk, rest = third(at, own, arrived, wide - wide // 3, wide // 3)
    bulk[1:] = [send(bulk[k], along_z(k)) for k in (1, 2, 3)]
    rest[1:] = [send(rest[k], first_axis(k)) for k in (1, 2, 3)]
    return finish(bulk, rest)


def solution(mesh):
    finer = Mesh(mesh.devices.reshape(4, 2, 4, 4), AXES)
    placed = (P(("z", "c"), ("x", "y"), None), P(("z", "c"), None), P(("z", "c"), ("x", "y"), None))
    return jax.shard_map(
        shards, mesh=finer, in_specs=placed, out_specs=P(("x", "y"), ("z", "c")), check_vma=False
    )
```

time: 135 us -> 141 us (1.044)
  the two profiles are of different devices: /device:TPU:1 before, /device:TPU:8 now
where the time goes in v1:
time: 141 us; the launch traced here: 140 us
  waiting for transfers between devices  80.7 us (57%)
  starting transfers between devices  29 us (21%)
  Pallas kernels  27.4 us (19%)
  local copies, waits for them, and re-layouts  2.44 us (2%)
    ppermute x22, waiting for transfers between devices, send(): return lax.ppermute(v, AXES, moves(shift))  80.7 us
    ppermute x22, starting transfers between devices, send(): return lax.ppermute(v, AXES, moves(shift))  29 us
    pallas_call x4, Pallas kernels, bulk_k(): pl.pallas_call(functools.partial(bulk_body, shift), grid=(2,), out_shape=...  10.6 us
    pallas_call x2, Pallas kernels, rest_k(): pl.pallas_call(rest_body, grid=(RING,), out_shape=[jax.ShapeDtypeStruct((...  4.73 us
    pallas_call x1, Pallas kernels, second(): pl.pallas_call(second_body, grid=(RING + 2,), out_shape=[jax.ShapeDtypeSt...  4.39 us
    pallas_call x1, Pallas kernels, fit(): pl.pallas_call(fit_body, grid=(group,), out_shape=[jax.ShapeDtypeStruct((...  3.62 us
  transfers between devices with their start and end apart: 22, of which 10 were waited for; matrix products, arithmetic and copies ran while one was open for 0% of the time, Pallas kernels for 5%

profile of v1, /device:TPU:8, one launch (start us, length us, event | category | flops | bytes accessed | tf_op | source)
XLA Modules:
  0.0 140.4 jit_solution(73370046130943720)
XLA Ops:
  0.8 1.7 %copy-done = bf16[16,24,3072]{2,1,0:T(8,128)(2,1)S(1)} copy-done((bf16[16,24,3072]{2,1,0:T(8,128)(2,1)S(1)}, bf16[16,24,3072]{2,1,0:T(8,128)(2,1)}, u32[]{:S(2)}) %copy-start) | copy-done | bytes 2359320
  3.2 2.0 %shard_map.37 = (bf16[6,16,3200]{2,1,0:T(8,128)(2,1)S(1)}, bf16[6,16,3200]{2,1,0:T(8,128)(2,1)S(1)}, bf16[6,16,3200]{2,1,0:T(8,128)(2,1)S(1)}, bf16[6,16,3200]{2,1,0:T(8,128)(2,1)S(1)}) custom-call(s32[4]{0:T(128)S(1)} %pad_add_fusion.at, bf16[16,24,3072]{2,1,0:T(8,128)(2,1)S(1)} %copy-done, bf16[1,3072]{1,0:T(2,128)(2,1)S(1)} %bitcast.12, ...), custom_call_target="tpu_custom_call" | custom-call | flops 1179648 | bytes 4718592 | tf_op jit(solution)/shard_map/pallas_call | solution.py:89
  5.2 2.0 %collective-permute-start.1 = (bf16[6,16,3200]{2,1,0:T(8,128)(2,1)S(1)}, bf16[6,16,3200]{2,1,0:T(8,128)(2,1)S(1)}, u32[]{:S(2)}, u32[]{:S(2)}) collective-permute-start(bf16[6,16,3200]{2,1,0:T(8,128)(2,1)S(1)} %get-tuple-element.29), channel_id=1, source_target_pairs={{0,32},{1,33},{2,34},{3,35},{4,36},{5,37},{6,38},{7,39},{8,40},{9,... | collective-permute-start | bytes 1843208 | tf_op jit(solution)/shard_map/ppermute | solution.py:48
  7.2 3.6 %collective-permute-start.3 = (bf16[6,16,3200]{2,1,0:T(8,128)(2,1)S(1)}, bf16[6,16,3200]{2,1,0:T(8,128)(2,1)S(1)}, u32[]{:S(2)}, u32[]{:S(2)}) collective-permute-start(bf16[6,16,3200]{2,1,0:T(8,128)(2,1)S(1)} %get-tuple-element.30), channel_id=1, source_target_pairs={{0,64},{1,65},{2,66},{3,67},{4,68},{5,69},{6,70},{7,71},{8,72},{9,... | collective-permute-start | bytes 1843208 | tf_op jit(solution)/shard_map/ppermute | solution.py:48
  11.8 11.4 %collective-permute-done.1.refs_2_ = bf16[6,16,3200]{2,1,0:T(8,128)(2,1)S(1)} collective-permute-done((bf16[6,16,3200]{2,1,0:T(8,128)(2,1)S(1)}, bf16[6,16,3200]{2,1,0:T(8,128)(2,1)S(1)}, u32[]{:S(2)}, u32[]{:S(2)}) %collective-permute-start.1) | collective-permute-done | bytes 614432 | tf_op jit(solution)/shard_map/ppermute | solution.py:48
  23.2 14.3 %collective-permute-done.3.refs_4_ = bf16[6,16,3200]{2,1,0:T(8,128)(2,1)S(1)} collective-permute-done((bf16[6,16,3200]{2,1,0:T(8,128)(2,1)S(1)}, bf16[6,16,3200]{2,1,0:T(8,128)(2,1)S(1)}, u32[]{:S(2)}, u32[]{:S(2)}) %collective-permute-start.3) | collective-permute-done | bytes 614432 | tf_op jit(solution)/shard_map/ppermute | solution.py:48
  38.0 1.5 %collective-permute-done.4.refs_5_ = bf16[6,16,3200]{2,1,0:T(8,128)(2,1)S(1)} collective-permute-done((bf16[6,16,3200]{2,1,0:T(8,128)(2,1)S(1)}, bf16[6,16,3200]{2,1,0:T(8,128)(2,1)S(1)}, u32[]{:S(2)}, u32[]{:S(2)}) %collective-permute-start.4) | collective-permute-done | bytes 614432 | tf_op jit(solution)/shard_map/ppermute | solution.py:48
  40.4 3.6 %shard_map.38 = (bf16[768,1024]{1,0:T(8,128)(2,1)S(1)}, bf16[768,512]{1,0:T(8,128)(2,1)S(1)}, bf16[3072,768]{1,0:T(8,128)(2,1)S(1)}) custom-call(s32[4]{0:T(128)S(1)} %pad_add_fusion.at, bf16[6,16,3200]{2,1,0:T(8,128)(2,1)S(1)} %get-tuple-element.28.refs_0_, bf16[6,16,3200]{2,1,0:T(8,128)(2,1)S(1)} %collective-permute-done.refs_1_, ...), custom_call_target="tpu_custom_call" | custom-call | flops 603979776 | bytes 14155776 | tf_op jit(solution)/shard_map/pallas_call | solution.py:143
  44.0 2.8 %shard_map.42 = s16[784,1024]{1,0:T(8,128)(2,1)S(1)} custom-call(s32[4]{0:T(128)S(1)} %pad_add_fusion.at, bf16[768,1024]{1,0:T(8,128)(2,1)S(1)} %get-tuple-element.32.bulk, bf16[3072,768]{1,0:T(8,128)(2,1)S(1)} %get-tuple-element.33.turned), custom_call_target="tpu_custom_call" | custom-call | flops 1207959552 | bytes 1572864 | tf_op jit(solution)/shard_map/pallas_call | solution.py:199
  46.8 2.8 %shard_map.41 = s16[784,1024]{1,0:T(8,128)(2,1)S(1)} custom-call(s32[4]{0:T(128)S(1)} %pad_add_fusion.at, bf16[768,1024]{1,0:T(8,128)(2,1)S(1)} %get-tuple-element.32.bulk, bf16[3072,768]{1,0:T(8,128)(2,1)S(1)} %get-tuple-element.33.turned), custom_call_target="tpu_custom_call" | custom-call | flops 1207959552 | bytes 1572864 | tf_op jit(solution)/shard_map/pallas_call | solution.py:199
  49.6 2.5 %shard_map.44 = (s16[3136,128]{1,0:T(8,128)(2,1)S(1)}, s16[3136,128]{1,0:T(8,128)(2,1)S(1)}) custom-call(bf16[768,512]{1,0:T(8,128)(2,1)S(1)} %get-tuple-element.34.rest, bf16[3072,768]{1,0:T(8,128)(2,1)S(1)} %get-tuple-element.33.turned), custom_call_target="tpu_custom_call" | custom-call | flops 1207959552 | bytes 1572864 | tf_op jit(solution)/shard_map/pallas_call | solution.py:222
  52.5 2.7 %shard_map.40 = s16[784,1024]{1,0:T(8,128)(2,1)S(1)} custom-call(s32[4]{0:T(128)S(1)} %pad_add_fusion.at, bf16[768,1024]{1,0:T(8,128)(2,1)S(1)} %get-tuple-element.32.bulk, bf16[3072,768]{1,0:T(8,128)(2,1)S(1)} %get-tuple-element.33.turned), custom_call_target="tpu_custom_call" | custom-call | flops 1207959552 | bytes 1572864 | tf_op jit(solution)/shard_map/pallas_call | solution.py:199
  55.2 1.6 %collective-permute-start.7 = (s16[784,1024]{1,0:T(8,128)(2,1)S(1)}, s16[784,1024]{1,0:T(8,128)(2,1)S(1)}, u32[]{:S(2)}, u32[]{:S(2)}) collective-permute-start(s16[784,1024]{1,0:T(8,128)(2,1)S(1)} %shard_map.40), channel_id=1, source_target_pairs={{0,4},{1,5},{2,6},{3,7},{4,8},{5,9},{6,10},{7,11},{8,12},{9,13},{1... | collective-permute-start | bytes 4816904 | tf_op jit(solution)/shard_map/ppermute | solution.py:48
  56.8 2.7 %collective-permute-start.8 = (s16[784,1024]{1,0:T(8,128)(2,1)S(1)}, s16[784,1024]{1,0:T(8,128)(2,1)S(1)}, u32[]{:S(2)}, u32[]{:S(2)}) collective-permute-start(s16[784,1024]{1,0:T(8,128)(2,1)S(1)} %shard_map.41), channel_id=1, source_target_pairs={{0,8},{1,9},{2,10},{3,11},{4,12},{5,13},{6,14},{7,15},{8,0},{9,1},... | collective-permute-start | bytes 4816904 | tf_op jit(solution)/shard_map/ppermute | solution.py:48
  59.5 1.4 %collective-permute-start.9 = (s16[784,1024]{1,0:T(8,128)(2,1)S(1)}, s16[784,1024]{1,0:T(8,128)(2,1)S(1)}, u32[]{:S(2)}, u32[]{:S(2)}) collective-permute-start(s16[784,1024]{1,0:T(8,128)(2,1)S(1)} %shard_map.42), channel_id=1, source_target_pairs={{0,12},{1,13},{2,14},{3,15},{4,0},{5,1},{6,2},{7,3},{8,4},{9,5},{1... | collective-permute-start | bytes 4816904 | tf_op jit(solution)/shard_map/ppermute | solution.py:48
  61.0 2.4 %collective-permute-start.11 = (s16[3136,128]{1,0:T(8,128)(2,1)S(1)}, s16[3136,128]{1,0:T(8,128)(2,1)S(1)}, u32[]{:S(2)}, u32[]{:S(2)}) collective-permute-start(s16[3136,128]{1,0:T(8,128)(2,1)S(1)} %get-tuple-element.37), channel_id=1, source_target_pairs={{0,64},{1,65},{2,66},{3,67},{4,68},{5,69},{6,70},{7,71},{8,72},{9,... | collective-permute-start | bytes 2408456 | tf_op jit(solution)/shard_map/ppermute | solution.py:48
  63.4 2.3 %shard_map.43 = (s16[3136,128]{1,0:T(8,128)(2,1)S(1)}, f32[3072,128]{1,0:T(8,128)S(1)}) custom-call(bf16[768,512]{1,0:T(8,128)(2,1)S(1)} %get-tuple-element.34.rest, bf16[3072,768]{1,0:T(8,128)(2,1)S(1)} %get-tuple-element.33.turned), custom_call_target="tpu_custom_call" | custom-call | flops 1207959552 | bytes 1572864 | tf_op jit(solution)/shard_map/pallas_call | solution.py:222
  65.6 24.9 %collective-permute-done.10.ra = s16[3136,128]{1,0:T(8,128)(2,1)S(1)} collective-permute-done((s16[3136,128]{1,0:T(8,128)(2,1)S(1)}, s16[3136,128]{1,0:T(8,128)(2,1)S(1)}, u32[]{:S(2)}, u32[]{:S(2)}) %collective-permute-start.10) | collective-permute-done | bytes 802848 | tf_op jit(solution)/shard_map/ppermute | solution.py:48
  90.5 2.4 %shard_map.39.bulk = f32[768,1024]{1,0:T(8,128)S(1)} custom-call(s32[4]{0:T(128)S(1)} %pad_add_fusion.at, bf16[768,1024]{1,0:T(8,128)(2,1)S(1)} %get-tuple-element.32.bulk, bf16[3072,768]{1,0:T(8,128)(2,1)S(1)} %get-tuple-element.33.turned), custom_call_target="tpu_custom_call" | custom-call | flops 1207959552 | bytes 1572864 | tf_op jit(solution)/shard_map/pallas_call | solution.py:199
  92.9 9.8 %collective-permute-done.12.rd = s16[3136,128]{1,0:T(8,128)(2,1)S(1)} collective-permute-done((s16[3136,128]{1,0:T(8,128)(2,1)S(1)}, s16[3136,128]{1,0:T(8,128)(2,1)S(1)}, u32[]{:S(2)}, u32[]{:S(2)}) %collective-permute-start.12) | collective-permute-done | bytes 802848 | tf_op jit(solution)/shard_map/ppermute | solution.py:48
  102.7 4.4 %second_sum.1 = (f32[192,1536]{1,0:T(8,128)S(1)}, s16[208,1536]{1,0:T(8,128)(2,1)S(1)}, s16[208,1536]{1,0:T(8,128)(2,1)S(1)}, s16[208,1536]{1,0:T(8,128)(2,1)S(1)}) custom-call(s32[4]{0:T(128)S(1)} %pad_add_fusion.at, f32[768,1024]{1,0:T(8,128)S(1)} %shard_map.39.bulk, s16[784,1024]{1,0:T(8,128)(2,1)S(1)} %collective-permute-done.7.ba, ...), custom_call_target="tpu_custom_call" | custom-call | flops 18874368 | bytes 11796480 | tf_op jit(solution)/shard_map/second_sum/pallas_call | solution.py:281
  107.1 2.4 %collective-permute-start.13 = (s16[208,1536]{1,0:T(8,128)(2,1)S(1)}, s16[208,1536]{1,0:T(8,128)(2,1)S(1)}, u32[]{:S(2)}, u32[]{:S(2)}) collective-permute-start(s16[208,1536]{1,0:T(8,128)(2,1)S(1)} %get-tuple-element.40), channel_id=1, source_target_pairs={{0,2},{1,3},{2,0},{3,1},{4,6},{5,7},{6,4},{7,5},{8,10},{9,11},{10,... | collective-permute-start | bytes 1916936 | tf_op jit(solution)/shard_map/ppermute | solution.py:48
  109.4 2.0 %collective-permute-start.15 = (s16[208,1536]{1,0:T(8,128)(2,1)S(1)}, s16[208,1536]{1,0:T(8,128)(2,1)S(1)}, u32[]{:S(2)}, u32[]{:S(2)}) collective-permute-start(s16[208,1536]{1,0:T(8,128)(2,1)S(1)} %get-tuple-element.42), channel_id=1, source_target_pairs={{0,3},{1,0},{2,1},{3,2},{4,7},{5,4},{6,5},{7,6},{8,11},{9,8},{10,9... | collective-permute-start | bytes 1916936 | tf_op jit(solution)/shard_map/ppermute | solution.py:48
  111.5 7.7 %collective-permute-done.13.a = s16[208,1536]{1,0:T(8,128)(2,1)S(1)} collective-permute-done((s16[208,1536]{1,0:T(8,128)(2,1)S(1)}, s16[208,1536]{1,0:T(8,128)(2,1)S(1)}, u32[]{:S(2)}, u32[]{:S(2)}) %collective-permute-start.13) | collective-permute-done | bytes 639008 | tf_op jit(solution)/shard_map/ppermute | solution.py:48
  119.1 7.5 %collective-permute-done.14.b = s16[208,1536]{1,0:T(8,128)(2,1)S(1)} collective-permute-done((s16[208,1536]{1,0:T(8,128)(2,1)S(1)}, s16[208,1536]{1,0:T(8,128)(2,1)S(1)}, u32[]{:S(2)}, u32[]{:S(2)}) %collective-permute-start.14) | collective-permute-done | bytes 639008 | tf_op jit(solution)/shard_map/ppermute | solution.py:48
  126.6 1.2 third_sum.1
  127.9 1.6 %collective-permute-start.19 = (s16[208,128]{1,0:T(8,128)(2,1)S(1)}, s16[208,128]{1,0:T(8,128)(2,1)S(1)}, u32[]{:S(2)}, u32[]{:S(2)}) collective-permute-start(s16[208,128]{1,0:T(8,128)(2,1)S(1)} %get-tuple-element.48), channel_id=1, source_target_pairs={{0,4},{1,5},{2,6},{3,7},{4,8},{5,9},{6,10},{7,11},{8,12},{9,13},{1... | collective-permute-start | bytes 159752 | tf_op jit(solution)/shard_map/ppermute | solution.py:48
  129.4 2.7 %collective-permute-start.17 = (s16[208,256]{1,0:T(8,128)(2,1)S(1)}, s16[208,256]{1,0:T(8,128)(2,1)S(1)}, u32[]{:S(2)}, u32[]{:S(2)}) collective-permute-start(s16[208,256]{1,0:T(8,128)(2,1)S(1)} %get-tuple-element.45), channel_id=1, source_target_pairs={{0,64},{1,65},{2,66},{3,67},{4,68},{5,69},{6,70},{7,71},{8,72},{9,... | collective-permute-start | bytes 319496 | tf_op jit(solution)/shard_map/ppermute | solution.py:48
  132.7 2.7 %collective-permute-start.20 = (s16[208,128]{1,0:T(8,128)(2,1)S(1)}, s16[208,128]{1,0:T(8,128)(2,1)S(1)}, u32[]{:S(2)}, u32[]{:S(2)}) collective-permute-start(s16[208,128]{1,0:T(8,128)(2,1)S(1)} %get-tuple-element.49), channel_id=1, source_target_pairs={{0,8},{1,9},{2,10},{3,11},{4,12},{5,13},{6,14},{7,15},{8,0},{9,1},... | collective-permute-start | bytes 159752 | tf_op jit(solution)/shard_map/ppermute | solution.py:48
  135.4 1.4 %collective-permute-start.21 = (s16[208,128]{1,0:T(8,128)(2,1)S(1)}, s16[208,128]{1,0:T(8,128)(2,1)S(1)}, u32[]{:S(2)}, u32[]{:S(2)}) collective-permute-start(s16[208,128]{1,0:T(8,128)(2,1)S(1)} %get-tuple-element.50), channel_id=1, source_target_pairs={{0,12},{1,13},{2,14},{3,15},{4,0},{5,1},{6,2},{7,3},{8,4},{9,5},{1... | collective-permute-start | bytes 159752 | tf_op jit(solution)/shard_map/ppermute | solution.py:48
  136.8 1.5 %collective-permute-done.20.rb = s16[208,128]{1,0:T(8,128)(2,1)S(1)} collective-permute-done((s16[208,128]{1,0:T(8,128)(2,1)S(1)}, s16[208,128]{1,0:T(8,128)(2,1)S(1)}, u32[]{:S(2)}, u32[]{:S(2)}) %collective-permute-start.20) | collective-permute-done | bytes 53280 | tf_op jit(solution)/shard_map/ppermute | solution.py:48
  138.3 1.2 collective-permute-done.21.rd
  (31 shorter events, 5.8 us)
Async XLA Ops:
  0.8 1.7 %copy-start = (bf16[16,24,3072]{2,1,0:T(8,128)(2,1)S(1)}, bf16[16,24,3072]{2,1,0:T(8,128)(2,1)}, u32[]{:S(2)}) copy-start(bf16[16,24,3072]{2,1,0:T(8,128)(2,1)} %half.1) | copy-start | bytes 7077892
  2.5 0.7 copy-start.1
  5.2 18.0 %collective-permute-start.1 = (bf16[6,16,3200]{2,1,0:T(8,128)(2,1)S(1)}, bf16[6,16,3200]{2,1,0:T(8,128)(2,1)S(1)}, u32[]{:S(2)}, u32[]{:S(2)}) collective-permute-start(bf16[6,16,3200]{2,1,0:T(8,128)(2,1)S(1)} %get-tuple-element.29), channel_id=1, source_target_pairs={{0,32},{1,33},{2,34},{3,35},{4,36},{5,37},{6,38},{7,39},{8,40},{9,... | collective-permute-start | bytes 1843208 | tf_op jit(solution)/shard_map/ppermute | solution.py:48
  7.2 30.3 %collective-permute-start.3 = (bf16[6,16,3200]{2,1,0:T(8,128)(2,1)S(1)}, bf16[6,16,3200]{2,1,0:T(8,128)(2,1)S(1)}, u32[]{:S(2)}, u32[]{:S(2)}) collective-permute-start(bf16[6,16,3200]{2,1,0:T(8,128)(2,1)S(1)} %get-tuple-element.30), channel_id=1, source_target_pairs={{0,64},{1,65},{2,66},{3,67},{4,68},{5,69},{6,70},{7,71},{8,72},{9,... | collective-permute-start | bytes 1843208 | tf_op jit(solution)/shard_map/ppermute | solution.py:48
  10.8 26.7 %collective-permute-start.5 = (bf16[6,16,3200]{2,1,0:T(8,128)(2,1)S(1)}, bf16[6,16,3200]{2,1,0:T(8,128)(2,1)S(1)}, u32[]{:S(2)}, u32[]{:S(2)}) collective-permute-start(bf16[6,16,3200]{2,1,0:T(8,128)(2,1)S(1)} %get-tuple-element.31), channel_id=1, source_target_pairs={{0,96},{1,97},{2,98},{3,99},{4,100},{5,101},{6,102},{7,103},{8,104... | collective-permute-start | bytes 1843208 | tf_op jit(solution)/shard_map/ppermute | solution.py:48
  11.8 26.2 %collective-permute-start = (bf16[6,16,3200]{2,1,0:T(8,128)(2,1)S(1)}, bf16[6,16,3200]{2,1,0:T(8,128)(2,1)S(1)}, u32[]{:S(2)}, u32[]{:S(2)}) collective-permute-start(bf16[6,16,3200]{2,1,0:T(8,128)(2,1)S(1)} %get-tuple-element.28.refs_0_), channel_id=1, source_target_pairs={{0,16},{1,17},{2,18},{3,19},{4,20},{5,21},{6,22},{7,23},{8,24},{9,... | collective-permute-start | bytes 1843208 | tf_op jit(solution)/shard_map/ppermute | solution.py:48
  23.2 14.9 %collective-permute-start.2 = (bf16[6,16,3200]{2,1,0:T(8,128)(2,1)S(1)}, bf16[6,16,3200]{2,1,0:T(8,128)(2,1)S(1)}, u32[]{:S(2)}, u32[]{:S(2)}) collective-permute-start(bf16[6,16,3200]{2,1,0:T(8,128)(2,1)S(1)} %collective-permute-done.1.refs_2_), channel_id=1, source_target_pairs={{0,16},{1,17},{2,18},{3,19},{4,20},{5,21},{6,22},{7,23},{8,24},{9,... | collective-permute-start | bytes 1843208 | tf_op jit(solution)/shard_map/ppermute | solution.py:48
  37.5 2.0 %collective-permute-start.4 = (bf16[6,16,3200]{2,1,0:T(8,128)(2,1)S(1)}, bf16[6,16,3200]{2,1,0:T(8,128)(2,1)S(1)}, u32[]{:S(2)}, u32[]{:S(2)}) collective-permute-start(bf16[6,16,3200]{2,1,0:T(8,128)(2,1)S(1)} %collective-permute-done.3.refs_4_), channel_id=1, source_target_pairs={{0,16},{1,17},{2,18},{3,19},{4,20},{5,21},{6,22},{7,23},{8,24},{9,... | collective-permute-start | bytes 1843208 | tf_op jit(solution)/shard_map/ppermute | solution.py:48
  37.5 2.9 %collective-permute-start.6 = (bf16[6,16,3200]{2,1,0:T(8,128)(2,1)S(1)}, bf16[6,16,3200]{2,1,0:T(8,128)(2,1)S(1)}, u32[]{:S(2)}, u32[]{:S(2)}) collective-permute-start(bf16[6,16,3200]{2,1,0:T(8,128)(2,1)S(1)} %collective-permute-done.5.refs_6_), channel_id=1, source_target_pairs={{0,16},{1,17},{2,18},{3,19},{4,20},{5,21},{6,22},{7,23},{8,24},{9,... | collective-permute-start | bytes 1843208 | tf_op jit(solution)/shard_map/ppermute | solution.py:48
  52.1 38.4 %collective-permute-start.10 = (s16[3136,128]{1,0:T(8,128)(2,1)S(1)}, s16[3136,128]{1,0:T(8,128)(2,1)S(1)}, u32[]{:S(2)}, u32[]{:S(2)}) collective-permute-start(s16[3136,128]{1,0:T(8,128)(2,1)S(1)} %get-tuple-element.36), channel_id=1, source_target_pairs={{0,32},{1,33},{2,34},{3,35},{4,36},{5,37},{6,38},{7,39},{8,40},{9,... | collective-permute-start | bytes 2408456 | tf_op jit(solution)/shard_map/ppermute | solution.py:48
  55.2 47.4 %collective-permute-start.7 = (s16[784,1024]{1,0:T(8,128)(2,1)S(1)}, s16[784,1024]{1,0:T(8,128)(2,1)S(1)}, u32[]{:S(2)}, u32[]{:S(2)}) collective-permute-start(s16[784,1024]{1,0:T(8,128)(2,1)S(1)} %shard_map.40), channel_id=1, source_target_pairs={{0,4},{1,5},{2,6},{3,7},{4,8},{5,9},{6,10},{7,11},{8,12},{9,13},{1... | collective-permute-start | bytes 4816904 | tf_op jit(solution)/shard_map/ppermute | solution.py:48
  56.8 45.9 %collective-permute-start.8 = (s16[784,1024]{1,0:T(8,128)(2,1)S(1)}, s16[784,1024]{1,0:T(8,128)(2,1)S(1)}, u32[]{:S(2)}, u32[]{:S(2)}) collective-permute-start(s16[784,1024]{1,0:T(8,128)(2,1)S(1)} %shard_map.41), channel_id=1, source_target_pairs={{0,8},{1,9},{2,10},{3,11},{4,12},{5,13},{6,14},{7,15},{8,0},{9,1},... | collective-permute-start | bytes 4816904 | tf_op jit(solution)/shard_map/ppermute | solution.py:48
  59.5 43.1 %collective-permute-start.9 = (s16[784,1024]{1,0:T(8,128)(2,1)S(1)}, s16[784,1024]{1,0:T(8,128)(2,1)S(1)}, u32[]{:S(2)}, u32[]{:S(2)}) collective-permute-start(s16[784,1024]{1,0:T(8,128)(2,1)S(1)} %shard_map.42), channel_id=1, source_target_pairs={{0,12},{1,13},{2,14},{3,15},{4,0},{5,1},{6,2},{7,3},{8,4},{9,5},{1... | collective-permute-start | bytes 4816904 | tf_op jit(solution)/shard_map/ppermute | solution.py:48
  61.0 31.9 %collective-permute-start.11 = (s16[3136,128]{1,0:T(8,128)(2,1)S(1)}, s16[3136,128]{1,0:T(8,128)(2,1)S(1)}, u32[]{:S(2)}, u32[]{:S(2)}) collective-permute-start(s16[3136,128]{1,0:T(8,128)(2,1)S(1)} %get-tuple-element.37), channel_id=1, source_target_pairs={{0,64},{1,65},{2,66},{3,67},{4,68},{5,69},{6,70},{7,71},{8,72},{9,... | collective-permute-start | bytes 2408456 | tf_op jit(solution)/shard_map/ppermute | solution.py:48
  90.5 12.2 %collective-permute-start.12 = (s16[3136,128]{1,0:T(8,128)(2,1)S(1)}, s16[3136,128]{1,0:T(8,128)(2,1)S(1)}, u32[]{:S(2)}, u32[]{:S(2)}) collective-permute-start(s16[3136,128]{1,0:T(8,128)(2,1)S(1)} %get-tuple-element.38), channel_id=1, source_target_pairs={{0,96},{1,97},{2,98},{3,99},{4,100},{5,101},{6,102},{7,103},{8,104... | collective-permute-start | bytes 2408456 | tf_op jit(solution)/shard_map/ppermute | solution.py:48
  107.1 12.1 %collective-permute-start.13 = (s16[208,1536]{1,0:T(8,128)(2,1)S(1)}, s16[208,1536]{1,0:T(8,128)(2,1)S(1)}, u32[]{:S(2)}, u32[]{:S(2)}) collective-permute-start(s16[208,1536]{1,0:T(8,128)(2,1)S(1)} %get-tuple-element.40), channel_id=1, source_target_pairs={{0,2},{1,3},{2,0},{3,1},{4,6},{5,7},{6,4},{7,5},{8,10},{9,11},{10,... | collective-permute-start | bytes 1916936 | tf_op jit(solution)/shard_map/ppermute | solution.py:48
  109.4 17.2 %collective-permute-start.14 = (s16[208,1536]{1,0:T(8,128)(2,1)S(1)}, s16[208,1536]{1,0:T(8,128)(2,1)S(1)}, u32[]{:S(2)}, u32[]{:S(2)}) collective-permute-start(s16[208,1536]{1,0:T(8,128)(2,1)S(1)} %get-tuple-element.41), channel_id=1, source_target_pairs={{0,1},{1,2},{2,3},{3,0},{4,5},{5,6},{6,7},{7,4},{8,9},{9,10},{10,1... | collective-permute-start | bytes 1916936 | tf_op jit(solution)/shard_map/ppermute | solution.py:48
  109.4 17.2 %collective-permute-start.15 = (s16[208,1536]{1,0:T(8,128)(2,1)S(1)}, s16[208,1536]{1,0:T(8,128)(2,1)S(1)}, u32[]{:S(2)}, u32[]{:S(2)}) collective-permute-start(s16[208,1536]{1,0:T(8,128)(2,1)S(1)} %get-tuple-element.42), channel_id=1, source_target_pairs={{0,3},{1,0},{2,1},{3,2},{4,7},{5,4},{6,5},{7,6},{8,11},{9,8},{10,9... | collective-permute-start | bytes 1916936 | tf_op jit(solution)/shard_map/ppermute | solution.py:48
  127.9 7.5 %collective-permute-start.19 = (s16[208,128]{1,0:T(8,128)(2,1)S(1)}, s16[208,128]{1,0:T(8,128)(2,1)S(1)}, u32[]{:S(2)}, u32[]{:S(2)}) collective-permute-start(s16[208,128]{1,0:T(8,128)(2,1)S(1)} %get-tuple-element.48), channel_id=1, source_target_pairs={{0,4},{1,5},{2,6},{3,7},{4,8},{5,9},{6,10},{7,11},{8,12},{9,13},{1... | collective-permute-start | bytes 159752 | tf_op jit(solution)/shard_map/ppermute | solution.py:48
  129.4 10.1 %collective-permute-start.16 = (s16[208,256]{1,0:T(8,128)(2,1)S(1)}, s16[208,256]{1,0:T(8,128)(2,1)S(1)}, u32[]{:S(2)}, u32[]{:S(2)}) collective-permute-start(s16[208,256]{1,0:T(8,128)(2,1)S(1)} %get-tuple-element.44), channel_id=1, source_target_pairs={{0,32},{1,33},{2,34},{3,35},{4,36},{5,37},{6,38},{7,39},{8,40},{9,... | collective-permute-start | bytes 319496 | tf_op jit(solution)/shard_map/ppermute | solution.py:48
  129.4 10.1 %collective-permute-start.17 = (s16[208,256]{1,0:T(8,128)(2,1)S(1)}, s16[208,256]{1,0:T(8,128)(2,1)S(1)}, u32[]{:S(2)}, u32[]{:S(2)}) collective-permute-start(s16[208,256]{1,0:T(8,128)(2,1)S(1)} %get-tuple-element.45), channel_id=1, source_target_pairs={{0,64},{1,65},{2,66},{3,67},{4,68},{5,69},{6,70},{7,71},{8,72},{9,... | collective-permute-start | bytes 319496 | tf_op jit(solution)/shard_map/ppermute | solution.py:48
  132.1 7.4 %collective-permute-start.18 = (s16[208,256]{1,0:T(8,128)(2,1)S(1)}, s16[208,256]{1,0:T(8,128)(2,1)S(1)}, u32[]{:S(2)}, u32[]{:S(2)}) collective-permute-start(s16[208,256]{1,0:T(8,128)(2,1)S(1)} %get-tuple-element.46), channel_id=1, source_target_pairs={{0,96},{1,97},{2,98},{3,99},{4,100},{5,101},{6,102},{7,103},{8,104... | collective-permute-start | bytes 319496 | tf_op jit(solution)/shard_map/ppermute | solution.py:48
  132.7 5.6 %collective-permute-start.20 = (s16[208,128]{1,0:T(8,128)(2,1)S(1)}, s16[208,128]{1,0:T(8,128)(2,1)S(1)}, u32[]{:S(2)}, u32[]{:S(2)}) collective-permute-start(s16[208,128]{1,0:T(8,128)(2,1)S(1)} %get-tuple-element.49), channel_id=1, source_target_pairs={{0,8},{1,9},{2,10},{3,11},{4,12},{5,13},{6,14},{7,15},{8,0},{9,1},... | collective-permute-start | bytes 159752 | tf_op jit(solution)/shard_map/ppermute | solution.py:48
  135.4 4.1 %collective-permute-start.21 = (s16[208,128]{1,0:T(8,128)(2,1)S(1)}, s16[208,128]{1,0:T(8,128)(2,1)S(1)}, u32[]{:S(2)}, u32[]{:S(2)}) collective-permute-start(s16[208,128]{1,0:T(8,128)(2,1)S(1)} %get-tuple-element.50), channel_id=1, source_target_pairs={{0,12},{1,13},{2,14},{3,15},{4,0},{5,1},{6,2},{7,3},{8,4},{9,5},{1... | collective-permute-start | bytes 159752 | tf_op jit(solution)/shard_map/ppermute | solution.py:48

commit v2 on v1

v2 whole, which is shorter than its diff:
```python
import functools

import jax
import jax.numpy as jnp
from jax import lax
from jax.experimental import pallas as pl
from jax.experimental.pallas import tpu as pltpu
from jax.sharding import Mesh
from jax.sharding import PartitionSpec as P


AXES = ("z", "c", "x", "y")
BF = jnp.bfloat16
F32 = jnp.float32
I16 = jnp.int16
MIB = 1 << 20
RING = 4
ORDER = (2, 1, 3, 0)
TAIL = 16


def whole():
    return pl.BlockSpec(memory_space=pltpu.VMEM)


def scalars():
    return pl.BlockSpec(memory_space=pltpu.SMEM)


def params(mib):
    return pltpu.CompilerParams(vmem_limit_bytes=mib * MIB)


def cost(flops, moved):
    return pl.CostEstimate(flops=flops, bytes_accessed=moved, transcendentals=0)


def place(z, c, x, y):
    return ((z % 4) * 2 + c) * 16 + (x % 4) * 4 + y % 4


def moves(shift):
    every = [(z, c, x, y) for z in range(4) for c in range(2) for x in range(4) for y in range(4)]
    return [(place(*d), place(*shift(*d))) for d in every]


def send(v, shift):
    return lax.ppermute(v, AXES, moves(shift))


def along_z(k):
    return lambda z, c, x, y: (z + k, c, x, y)


def other_core(z, c, x, y):
    return (z, 1 - c, x, y)


def first_axis(k):
    return lambda z, c, x, y: (z, c, x + k, y) if c == 0 else (z, c, x, y + k)


def second_axis(k):
    return lambda z, c, x, y: (z, c, x, y + k) if c == 0 else (z, c, x + k, y)


def screen_body(at, half, gate, *outs_and_scratch):
    outs, turned = outs_and_scratch[:4], outs_and_scratch[4]
    kept = half[...] * gate[...][None]
    turned[...] = jnp.swapaxes(kept.astype(F32), 0, 1).astype(BF)
    group = outs[0].shape[0]
    for k in range(RING):
        outs[k][...] = turned[pl.ds(lax.rem(at[0] + k, RING) * group, group)]


def screen(at, half, gate):
    aux, occ, ao = half.shape
    lanes = 512
    group = occ // RING
    return pl.pallas_call(
        screen_body,
        grid=(ao // lanes,),
        out_shape=[jax.ShapeDtypeStruct((group, aux, ao), BF)] * RING,
        in_specs=[
            scalars(),
            pl.BlockSpec((aux, occ, lanes), lambda j: (0, 0, j)),
            pl.BlockSpec((1, lanes), lambda j: (0, j)),
        ],
        out_specs=[pl.BlockSpec((group, aux, lanes), lambda j: (0, 0, j))] * RING,
        scratch_shapes=[pltpu.VMEM((occ, aux, lanes), BF)],
        compiler_params=params(16),
        cost_estimate=cost(half.size, half.size * 4),
        name="screen",
    )(at, half, gate)


def join_body(at, *refs):
    metrics, mixed = refs[:4], refs[4]
    aux = mixed.shape[0]
    part = aux // 8
    metric = jnp.concatenate([m[...] for m in metrics], axis=0)
    source = lax.broadcasted_iota(jnp.int32, (aux, aux), 0)
    n = lax.broadcasted_iota(jnp.int32, (aux, aux), 1)
    slot = n // part
    up = lax.rem(at[0] - slot // 2 + RING, RING)
    core = jnp.where(slot % 2 == 0, at[1], 1 - at[1])
    wanted = (up * 2 + core) * part + n % part
    pick = jnp.where(source == wanted, 1.0, 0.0).astype(BF)
    mixed[...] = jnp.dot(metric, pick, preferred_element_type=F32).astype(BF)


def join(at, metrics):
    aux = metrics[0].shape[1]
    return pl.pallas_call(
        join_body,
        out_shape=jax.ShapeDtypeStruct((aux, aux), BF),
        in_specs=[scalars()] + [whole()] * 4,
        out_specs=whole(),
        compiler_params=params(4),
        cost_estimate=cost(2 * aux**3, aux * aux * 4),
        name="join",
    )(at, *metrics)


def fit_body(at, *refs):
    pieces, mixed, (a1, a2, rest, turned, fresh) = refs[:8], refs[8], refs[9:]
    step = pl.program_id(0)
    ao = fresh.shape[1]
    aux = mixed.shape[0]

    screened = jnp.concatenate([p[0] for p in pieces], axis=0)
    fitted = jnp.dot(mixed[...], screened, preferred_element_type=F32).astype(BF)
    fresh[...] = fitted
    narrow = rest.shape[1] // RING
    for n in range(RING):
        column = n * (ao // RING) + at[1] * 3 * narrow
        cut = slice(n * narrow, (n + 1) * narrow)
        a1[:, cut] = fresh[:, pl.ds(pl.multiple_of(column, 128), narrow)]
        a2[:, cut] = fresh[:, pl.ds(pl.multiple_of(column + narrow, 128), narrow)]
        column = lax.rem(at[0] + ORDER[n], RING) * (ao // RING) + at[1] * 3 * narrow + 2 * narrow
        rest[:, cut] = fresh[:, pl.ds(pl.multiple_of(column, 128), narrow)]
    flipped = fitted.T
    cut = pl.ds(pl.multiple_of(step * aux, aux), aux)
    high = ao // (RING * RING)
    for x in range(RING):
        for y in range(RING):
            n = x * RING + y
            to = jnp.where(at[1] == 0, n, y * RING + x) * high
            turned[pl.ds(pl.multiple_of(to, 64), high), cut] = flipped[n * high:(n + 1) * high]


def fit(at, pieces, mixed):
    group, part, ao = pieces[0].shape
    aux = part * 8
    piece = pl.BlockSpec((1, part, ao), lambda i: (i, 0, 0))
    own = pl.BlockSpec((aux, ao // 6), lambda i: (i, 0))
    return pl.pallas_call(
        fit_body,
        grid=(group,),
        out_shape=[jax.ShapeDtypeStruct((group * aux, ao // 6), BF)] * 3
        + [jax.ShapeDtypeStruct((ao, group * aux), BF)],
        in_specs=[scalars()] + [piece] * 8 + [whole()],
        out_specs=[own] * 3 + [pl.BlockSpec((ao, group * aux), lambda i: (0, 0))],
        scratch_shapes=[pltpu.VMEM((aux, ao), BF)],
        compiler_params=params(28),
        cost_estimate=cost(2 * group * aux * aux * ao, group * aux * ao * 6),
        name="fit",
    )(at, *pieces, mixed)


def exponent(top):
    return jnp.floor(14.9 - jnp.log2(jnp.maximum(top, 1e-30)))


def coded(v, e):
    return jnp.round(v * jnp.exp2(e)).astype(jnp.int32).astype(I16)


def marked(e):
    return jnp.broadcast_to(e, (TAIL, e.shape[1])).astype(jnp.int32).astype(I16)


def scale_of(tail):
    return jnp.exp2(-tail.astype(jnp.int32).astype(F32)[:1])


def plain(q):
    return q.astype(jnp.int32).astype(F32)


def write(out, first, block):
    if out.dtype == F32:
        out[first:first + block.shape[0], :] = block
    else:
        e = exponent(jnp.max(jnp.abs(block), axis=0, keepdims=True))
        end = first + block.shape[0]
        out[first:end, :] = coded(block, e)
        out[end:end + TAIL, :] = marked(e)


def bulk_body(shift, at, bulk, turned, out):
    total = turned.shape[0] // RING
    g = lax.rem(jnp.where(at[1] == 0, at[2], at[3]) + shift, RING)
    left = turned[pl.ds(pl.multiple_of(g * total, 256), total), :]
    write(out, 0, jnp.dot(left, bulk[...], preferred_element_type=F32))


def bulk_k(at, bulk, turned, shift):
    depth, columns = bulk.shape
    total = turned.shape[0] // RING
    shape = (total + (TAIL if shift else 0), columns)
    return pl.pallas_call(
        functools.partial(bulk_body, shift),
        out_shape=jax.ShapeDtypeStruct(shape, I16 if shift else F32),
        in_specs=[scalars(), whole(), whole()],
        out_specs=whole(),
        compiler_params=params(28),
        cost_estimate=cost(2 * depth * total * columns, total * columns * 2),
    )(at, bulk, turned)


def rest_body(rest, turned, *outs):
    both = jnp.dot(turned[...], rest[...], preferred_element_type=F32)
    narrow = both.shape[1] // 2
    write(outs[0], 0, both[:, :narrow])
    write(outs[1], 0, both[:, narrow:])


def rest_k(rest, turned, pair):
    depth = rest.shape[0]
    ao = turned.shape[0]
    total, narrow = ao // RING, rest.shape[1] // RING
    each = [total + (TAIL if k else 0) for k in ORDER[2 * pair:2 * pair + 2]]
    return pl.pallas_call(
        rest_body,
        grid=(RING,),
        out_shape=[jax.ShapeDtypeStruct((RING * n, narrow), I16 if n > total else F32) for n in each],
        in_specs=[
            pl.BlockSpec((depth, 2 * narrow), lambda g: (0, pair)),
            pl.BlockSpec((total, depth), lambda g: (g, 0)),
        ],
        out_specs=[pl.BlockSpec((n, narrow), lambda g: (g, 0)) for n in each],
        compiler_params=params(28),
        cost_estimate=cost(4 * depth * ao * narrow, ao * narrow * 4),
    )(rest, turned)


def second_part(at, own, arrived, kept, outs):
    high = kept.shape[0]
    total = own.shape[0]
    h = jnp.where(at[1] == 0, at[3], at[2])
    scales = [scale_of(m[total:, :]) for m in arrived]
    for k in range(RING):
        row = pl.ds(pl.multiple_of(lax.rem(h + k, RING) * high, 64), high)
        v = own[row, :]
        for m, scale in zip(arrived, scales):
            v = v + plain(m[row, :]) * scale
        write(kept if k == 0 else outs[k - 1], 0, v)


def second_body(at, a, a1, a2, a3, kept, *outs):
    second_part(at, a, (a1, a2, a3), kept, outs)


def second_both_body(at, a, a1, a2, a3, b, b1, b2, b3, kept, *outs):
    @pl.when(pl.program_id(0) < 2)
    def _():
        second_part(at, a, (a1, a2, a3), kept, outs)

    @pl.when(pl.program_id(0) >= 2)
    def _():
        narrow = b.shape[1]
        for n in range(2):
            lanes = slice(n * narrow, (n + 1) * narrow)

            def rows(ref):
                return ref.at[n * (ref.shape[0] // 2):(n + 1) * (ref.shape[0] // 2)]

            second_part(at, rows(b), [rows(m) for m in (b1, b2, b3)], kept.at[:, lanes], [o.at[:, lanes] for o in outs])


def second(at, bulk, rest=()):
    total, columns = bulk[0].shape
    wide, high = columns // 2, total // RING
    steps = 4 if rest else 2
    every = steps * wide

    def of_bulk(rows):
        return pl.BlockSpec((rows, wide), lambda j: (0, jnp.minimum(j, 1)))

    def of_rest(rows):
        return pl.BlockSpec((2 * rows, wide // 2), lambda j: (jnp.maximum(j - 2, 0), 0))

    specs = [of_bulk(total)] + [of_bulk(total + TAIL)] * 3
    if rest:
        specs += [of_rest(total)] + [of_rest(total + TAIL)] * 3
    return pl.pallas_call(
        second_both_body if rest else second_body,
        grid=(steps,),
        out_shape=[jax.ShapeDtypeStruct((high, every), F32)]
        + [jax.ShapeDtypeStruct((high + TAIL, every), I16)] * 3,
        in_specs=[scalars()] + specs,
        out_specs=[pl.BlockSpec((n, wide), lambda j: (0, j)) for n in [high] + [high + TAIL] * 3],
        compiler_params=params(24),
        cost_estimate=cost(total * every * 16, total * every * 10),
        name="second_sum",
    )(at, *bulk, *rest)


def third_body(at, p, p1, p2, p3, q, q1, q2, q3, bulk, b1, b2, b3, rest, r1, r2, r3):
    high, step = rest.shape
    g = jnp.where(at[1] == 0, at[2], at[3])
    for own, arrived, base, start, outs in (
        (p, (p1, p2, p3), 0, at[0], [o.at[:, :step] for o in (bulk, b1, b2, b3)]),
        (q, (q1, q2, q3), 0, at[0], [o.at[:, step:] for o in (bulk, b1, b2, b3)]),
        (q, (q1, q2, q3), RING * step, g, (rest, r1, r2, r3)),
    ):
        for k in range(RING):
            cut = pl.ds(pl.multiple_of(base + lax.rem(start + k, RING) * step, 128), step)
            v = own[:, cut]
            for m in arrived:
                v = v + plain(m[:high, cut]) * scale_of(m[high:, cut])
            write(outs[k], 0, v)


def third(at, first, both):
    high, every = both[0].shape
    narrow = every // 8

    def four(lanes):
        return [jax.ShapeDtypeStruct((high, lanes), F32)] + [jax.ShapeDtypeStruct((high + TAIL, lanes), I16)] * 3

    out = pl.pallas_call(
        third_body,
        out_shape=four(2 * narrow) + four(narrow),
        in_specs=[scalars()] + [whole()] * 8,
        out_specs=[whole()] * 8,
        compiler_params=params(16),
        cost_estimate=cost(high * every * 24, high * every * 15),
        name="third_sum",
    )(at, *first, *both)
    return list(out[:4]), list(out[4:])


def finish_body(own, a, b, d, rest, ra, rb, rd, out):
    high, wide = own.shape
    for first, v, arrived in ((0, own[...], (a, b, d)), (wide, rest[...], (ra, rb, rd))):
        for m in arrived:
            v = v + plain(m[:high, :]) * scale_of(m[high:, :])
        out[:, first:first + v.shape[1]] = v


def finish(bulk, rest):
    high = bulk[0].shape[0]
    ao = bulk[0].shape[1] + rest[0].shape[1]
    return pl.pallas_call(
        finish_body,
        out_shape=jax.ShapeDtypeStruct((high, ao), F32),
        in_specs=[whole()] * 8,
        out_specs=whole(),
        compiler_params=params(8),
        cost_estimate=cost(high * ao * 8, high * ao * 14),
    )(*bulk, *rest)


def shards(half, metric, survive):
    _, _, ao = half.shape
    at = jnp.stack([lax.axis_index(a) for a in AXES]).astype(jnp.int32)
    blocks = survive.shape[2]
    gate = jnp.repeat(survive.reshape(1, blocks).astype(BF), ao // blocks, axis=1)

    pair = jnp.concatenate([metric, send(metric, other_core)], axis=0)
    parts = screen(at, half, gate)
    here, metrics = [parts[0]] + [None] * 3, [pair] + [None] * 3
    for k in ORDER[:3]:
        here[k] = send(parts[k], along_z(k))
    for k in ORDER[:3]:
        metrics[k] = send(pair, along_z(k))
    mixed = join(at, metrics)
    there = [send(v, other_core) for v in here]
    *columns, turned = fit(at, [v for both in zip(here, there) for v in both], mixed)

    moved = {}

    def bulk_step(part, k):
        v = bulk_k(at, columns[part], turned, k)
        if k:
            v = send(v, first_axis(k))
        moved[part, k] = v

    def rest_step(pair):
        out = rest_k(columns[2], turned, pair)
        for k, v in zip(ORDER[2 * pair:2 * pair + 2], out):
            moved[2, k] = send(v, along_z(k)) if k else v

    bulk_step(0, 2)
    rest_step(0)
    bulk_step(0, 1)
    bulk_step(0, 3)
    rest_step(1)
    bulk_step(1, 2)
    bulk_step(1, 1)
    bulk_step(1, 3)
    bulk_step(0, 0)
    bulk_step(1, 0)
    early = list(second(at, [moved[0, k] for k in range(4)]))
    for k in ORDER[:3]:
        early[k] = send(early[k], second_axis(k))
    late = list(second(at, [moved[1, k] for k in range(4)], [moved[2, k] for k in range(4)]))
    for k in ORDER[:3]:
        late[k] = send(late[k], second_axis(k))
    bulk, rest = third(at, early, late)
    bulk[1:] = [send(bulk[k], along_z(k)) for k in (1, 2, 3)]
    rest[1:] = [send(rest[k], first_axis(k)) for k in (1, 2, 3)]
    return finish(bulk, rest)


def solution(mesh):
    finer = Mesh(mesh.devices.reshape(4, 2, 4, 4), AXES)
    placed = (P(("z", "c"), ("x", "y"), None), P(("z", "c"), None), P(("z", "c"), ("x", "y"), None))
    return jax.shard_map(
        shards, mesh=finer, in_specs=placed, out_specs=P(("x", "y"), ("z", "c")), check_vma=False
    )
```

time: 141 us -> 167 us (1.18)
  the two profiles are of different devices: /device:TPU:8 before, /device:TPU:1 now
where the time goes in v2:
time: 167 us; the launch traced here: 166 us
  waiting for transfers between devices  87.9 us (53%)
  starting transfers between devices  45 us (27%)
  Pallas kernels  30.1 us (18%)
  local copies, waits for them, and re-layouts  1.77 us (1%)
    ppermute x32, waiting for transfers between devices, send(): return lax.ppermute(v, AXES, moves(shift))  87.9 us
    ppermute x32, starting transfers between devices, send(): return lax.ppermute(v, AXES, moves(shift))  45 us
    pallas_call x8, Pallas kernels, bulk_k(): pl.pallas_call(functools.partial(bulk_body, shift), out_shape=jax.ShapeDt...  12 us
    pallas_call x2, Pallas kernels, rest_k(): pl.pallas_call(rest_body, grid=(RING,), out_shape=[jax.ShapeDtypeStruct((...  4.75 us
    pallas_call x2, Pallas kernels, second(): pl.pallas_call(second_both_body if rest else second_body, grid=(steps,),...  4.46 us
    pallas_call x1, Pallas kernels, fit(): pl.pallas_call(fit_body, grid=(group,), out_shape=[jax.ShapeDtypeStruct((...  3.55 us
  transfers between devices with their start and end apart: 32, of which 14 were waited for; matrix products, arithmetic and copies ran while one was open for 0% of the time, Pallas kernels for 10%

profile of v2, /device:TPU:1, one launch (start us, length us, event | category | flops | bytes accessed | tf_op | source)
XLA Modules:
  0.0 165.8 jit_solution(91883486764373125)
XLA Ops:
  0.8 1.7 %copy-done = bf16[16,24,3072]{2,1,0:T(8,128)(2,1)S(1)} copy-done((bf16[16,24,3072]{2,1,0:T(8,128)(2,1)S(1)}, bf16[16,24,3072]{2,1,0:T(8,128)(2,1)}, u32[]{:S(2)}) %copy-start) | copy-done | bytes 2359320
  2.5 2.5 %screen.1 = (bf16[6,16,3072]{2,1,0:T(8,128)(2,1)S(1)}, bf16[6,16,3072]{2,1,0:T(8,128)(2,1)S(1)}, bf16[6,16,3072]{2,1,0:T(8,128)(2,1)S(1)}, bf16[6,16,3072]{2,1,0:T(8,128)(2,1)S(1)}) custom-call(s32[4]{0:T(128)S(1)} %pad_add_fusion.at, bf16[16,24,3072]{2,1,0:T(8,128)(2,1)S(1)} %copy-done, bf16[1,3072]{1,0:T(2,128)(2,1)S(1)} %bitcast.12), custom_call_target="tpu_custom_call" | custom-call | flops 1179648 | bytes 4718592 | tf_op jit(solution)/shard_map/screen/pallas_call | solution.py:80
  5.0 2.5 %collective-permute-start.1 = (bf16[6,16,3072]{2,1,0:T(8,128)(2,1)S(1)}, bf16[6,16,3072]{2,1,0:T(8,128)(2,1)S(1)}, u32[]{:S(2)}, u32[]{:S(2)}) collective-permute-start(bf16[6,16,3072]{2,1,0:T(8,128)(2,1)S(1)} %get-tuple-element.34), channel_id=1, source_target_pairs={{0,32},{1,33},{2,34},{3,35},{4,36},{5,37},{6,38},{7,39},{8,40},{9,... | collective-permute-start | bytes 1769480 | tf_op jit(solution)/shard_map/ppermute | solution.py:48
  7.5 3.3 %collective-permute-start.3 = (bf16[6,16,3072]{2,1,0:T(8,128)(2,1)S(1)}, bf16[6,16,3072]{2,1,0:T(8,128)(2,1)S(1)}, u32[]{:S(2)}, u32[]{:S(2)}) collective-permute-start(bf16[6,16,3072]{2,1,0:T(8,128)(2,1)S(1)} %get-tuple-element.35), channel_id=1, source_target_pairs={{0,64},{1,65},{2,66},{3,67},{4,68},{5,69},{6,70},{7,71},{8,72},{9,... | collective-permute-start | bytes 1769480 | tf_op jit(solution)/shard_map/ppermute | solution.py:48
  13.1 9.6 %collective-permute-done.1.refs_2_ = bf16[6,16,3072]{2,1,0:T(8,128)(2,1)S(1)} collective-permute-done((bf16[6,16,3072]{2,1,0:T(8,128)(2,1)S(1)}, bf16[6,16,3072]{2,1,0:T(8,128)(2,1)S(1)}, u32[]{:S(2)}, u32[]{:S(2)}) %collective-permute-start.1) | collective-permute-done | bytes 589856 | tf_op jit(solution)/shard_map/ppermute | solution.py:48
  23.9 12.3 %collective-permute-done.3.refs_4_ = bf16[6,16,3072]{2,1,0:T(8,128)(2,1)S(1)} collective-permute-done((bf16[6,16,3072]{2,1,0:T(8,128)(2,1)S(1)}, bf16[6,16,3072]{2,1,0:T(8,128)(2,1)S(1)}, u32[]{:S(2)}, u32[]{:S(2)}) %collective-permute-start.3) | collective-permute-done | bytes 589856 | tf_op jit(solution)/shard_map/ppermute | solution.py:48
  38.3 2.0 %collective-permute-done.7 = bf16[16,128]{1,0:T(8,128)(2,1)S(1)} collective-permute-done((bf16[16,128]{1,0:T(8,128)(2,1)S(1)}, bf16[16,128]{1,0:T(8,128)(2,1)S(1)}, u32[]{:S(2)}, u32[]{:S(2)}) %collective-permute-start.7) | collective-permute-done | bytes 4128 | tf_op jit(solution)/shard_map/ppermute | solution.py:48
  43.9 2.9 %collective-permute-done.9.refs_2_ = bf16[32,128]{1,0:T(8,128)(2,1)S(1)} collective-permute-done((bf16[32,128]{1,0:T(8,128)(2,1)S(1)}, bf16[32,128]{1,0:T(8,128)(2,1)S(1)}, u32[]{:S(2)}, u32[]{:S(2)}) %collective-permute-start.9) | collective-permute-done | bytes 8224 | tf_op jit(solution)/shard_map/ppermute | solution.py:48
  46.9 3.6 %collective-permute-done.8.refs_1_ = bf16[32,128]{1,0:T(8,128)(2,1)S(1)} collective-permute-done((bf16[32,128]{1,0:T(8,128)(2,1)S(1)}, bf16[32,128]{1,0:T(8,128)(2,1)S(1)}, u32[]{:S(2)}, u32[]{:S(2)}) %collective-permute-start.8) | collective-permute-done | bytes 8224 | tf_op jit(solution)/shard_map/ppermute | solution.py:48
  51.2 3.5 %fit.1 = (bf16[768,512]{1,0:T(8,128)(2,1)S(1)}, bf16[768,512]{1,0:T(8,128)(2,1)S(1)}, bf16[768,512]{1,0:T(8,128)(2,1)S(1)}, bf16[3072,768]{1,0:T(8,128)(2,1)S(1)}) custom-call(s32[4]{0:T(128)S(1)} %pad_add_fusion.at, bf16[6,16,3072]{2,1,0:T(8,128)(2,1)S(1)} %get-tuple-element.33.refs_0_, bf16[6,16,3072]{2,1,0:T(8,128)(2,1)S(1)} %collective-permute-done.refs_1_, ...), custom_call_target="tpu_custom_call" | custom-call | flops 603979776 | bytes 14155776 | tf_op jit(solution)/shard_map/fit/pallas_call | solution.py:157
  54.8 1.6 shard_map.39
  56.3 1.6 shard_map.38
  63.6 1.6 shard_map.40
  65.1 2.1 %collective-permute-start.13 = (s16[784,512]{1,0:T(8,128)(2,1)S(1)}, s16[784,512]{1,0:T(8,128)(2,1)S(1)}, u32[]{:S(2)}, u32[]{:S(2)}) collective-permute-start(s16[784,512]{1,0:T(8,128)(2,1)S(1)} %shard_map.40), channel_id=1, source_target_pairs={{0,12},{1,13},{2,14},{3,15},{4,0},{5,1},{6,2},{7,3},{8,4},{9,5},{1... | collective-permute-start | bytes 2408456 | tf_op jit(solution)/shard_map/ppermute | solution.py:48
  67.2 1.6 shard_map.43
  70.8 2.5 %shard_map.46 = (s16[3136,128]{1,0:T(8,128)(2,1)S(1)}, s16[3136,128]{1,0:T(8,128)(2,1)S(1)}) custom-call(bf16[768,512]{1,0:T(8,128)(2,1)S(1)} %get-tuple-element.44.rest, bf16[3072,768]{1,0:T(8,128)(2,1)S(1)} %get-tuple-element.38.turned), custom_call_target="tpu_custom_call" | custom-call | flops 1207959552 | bytes 1572864 | tf_op jit(solution)/shard_map/pallas_call | solution.py:234
  73.2 2.3 %shard_map.45 = (s16[3136,128]{1,0:T(8,128)(2,1)S(1)}, f32[3072,128]{1,0:T(8,128)S(1)}) custom-call(bf16[768,512]{1,0:T(8,128)(2,1)S(1)} %get-tuple-element.44.rest, bf16[3072,768]{1,0:T(8,128)(2,1)S(1)} %get-tuple-element.38.turned), custom_call_target="tpu_custom_call" | custom-call | flops 1207959552 | bytes 1572864 | tf_op jit(solution)/shard_map/pallas_call | solution.py:234
  75.5 1.6 collective-permute-start.19
  77.1 3.6 %collective-permute-done.11.a1 = s16[784,512]{1,0:T(8,128)(2,1)S(1)} collective-permute-done((s16[784,512]{1,0:T(8,128)(2,1)S(1)}, s16[784,512]{1,0:T(8,128)(2,1)S(1)}, u32[]{:S(2)}, u32[]{:S(2)}) %collective-permute-start.11) | collective-permute-done | bytes 802848 | tf_op jit(solution)/shard_map/ppermute | solution.py:48
  80.7 9.8 %collective-permute-done.12.a2 = s16[784,512]{1,0:T(8,128)(2,1)S(1)} collective-permute-done((s16[784,512]{1,0:T(8,128)(2,1)S(1)}, s16[784,512]{1,0:T(8,128)(2,1)S(1)}, u32[]{:S(2)}, u32[]{:S(2)}) %collective-permute-start.12) | collective-permute-done | bytes 802848 | tf_op jit(solution)/shard_map/ppermute | solution.py:48
  94.4 1.7 %second_sum.2 = (f32[192,512]{1,0:T(8,128)S(1)}, s16[208,512]{1,0:T(8,128)(2,1)S(1)}, s16[208,512]{1,0:T(8,128)(2,1)S(1)}, s16[208,512]{1,0:T(8,128)(2,1)S(1)}) custom-call(s32[4]{0:T(128)S(1)} %pad_add_fusion.at, f32[768,512]{1,0:T(8,128)S(1)} %shard_map.37.a, s16[784,512]{1,0:T(8,128)(2,1)S(1)} %collective-permute-done.11.a1, ...), custom_call_target="tpu_custom_call" | custom-call | flops 6291456 | bytes 3932160 | tf_op jit(solution)/shard_map/second_sum/pallas_call | solution.py:297
  96.1 3.0 %collective-permute-done.18.a2 = s16[784,512]{1,0:T(8,128)(2,1)S(1)} collective-permute-done((s16[784,512]{1,0:T(8,128)(2,1)S(1)}, s16[784,512]{1,0:T(8,128)(2,1)S(1)}, u32[]{:S(2)}, u32[]{:S(2)}) %collective-permute-start.18) | collective-permute-done | bytes 802848 | tf_op jit(solution)/shard_map/ppermute | solution.py:48
  100.0 13.5 %collective-permute-done.21.b2 = s16[3136,128]{1,0:T(8,128)(2,1)S(1)} collective-permute-done((s16[3136,128]{1,0:T(8,128)(2,1)S(1)}, s16[3136,128]{1,0:T(8,128)(2,1)S(1)}, u32[]{:S(2)}, u32[]{:S(2)}) %collective-permute-start.21) | collective-permute-done | bytes 802848 | tf_op jit(solution)/shard_map/ppermute | solution.py:48
  113.6 13.0 %collective-permute-done.22.b3 = s16[3136,128]{1,0:T(8,128)(2,1)S(1)} collective-permute-done((s16[3136,128]{1,0:T(8,128)(2,1)S(1)}, s16[3136,128]{1,0:T(8,128)(2,1)S(1)}, u32[]{:S(2)}, u32[]{:S(2)}) %collective-permute-start.22) | collective-permute-done | bytes 802848 | tf_op jit(solution)/shard_map/ppermute | solution.py:48
  126.6 2.8 %second_sum.3 = (f32[192,1024]{1,0:T(8,128)S(1)}, s16[208,1024]{1,0:T(8,128)(2,1)S(1)}, s16[208,1024]{1,0:T(8,128)(2,1)S(1)}, s16[208,1024]{1,0:T(8,128)(2,1)S(1)}) custom-call(s32[4]{0:T(128)S(1)} %pad_add_fusion.at, f32[768,512]{1,0:T(8,128)S(1)} %shard_map.41.a, s16[784,512]{1,0:T(8,128)(2,1)S(1)} %collective-permute-done.17.a1, ...), custom_call_target="tpu_custom_call" | custom-call | flops 12582912 | bytes 7864320 | tf_op jit(solution)/shard_map/second_sum/pallas_call | solution.py:297
  129.5 2.5 %collective-permute-start.24 = (s16[208,1024]{1,0:T(8,128)(2,1)S(1)}, s16[208,1024]{1,0:T(8,128)(2,1)S(1)}, u32[]{:S(2)}, u32[]{:S(2)}) collective-permute-start(s16[208,1024]{1,0:T(8,128)(2,1)S(1)} %get-tuple-element.51), channel_id=1, source_target_pairs={{0,2},{1,3},{2,0},{3,1},{4,6},{5,7},{6,4},{7,5},{8,10},{9,11},{10,... | collective-permute-start | bytes 1277960 | tf_op jit(solution)/shard_map/ppermute | solution.py:48
  132.0 2.0 %collective-permute-start.25 = (s16[208,1024]{1,0:T(8,128)(2,1)S(1)}, s16[208,1024]{1,0:T(8,128)(2,1)S(1)}, u32[]{:S(2)}, u32[]{:S(2)}) collective-permute-start(s16[208,1024]{1,0:T(8,128)(2,1)S(1)} %get-tuple-element.52), channel_id=1, source_target_pairs={{0,3},{1,0},{2,1},{3,2},{4,7},{5,4},{6,5},{7,6},{8,11},{9,8},{10,9... | collective-permute-start | bytes 1277960 | tf_op jit(solution)/shard_map/ppermute | solution.py:48
  135.9 8.7 %collective-permute-done.15.p2 = s16[208,512]{1,0:T(8,128)(2,1)S(1)} collective-permute-done((s16[208,512]{1,0:T(8,128)(2,1)S(1)}, s16[208,512]{1,0:T(8,128)(2,1)S(1)}, u32[]{:S(2)}, u32[]{:S(2)}) %collective-permute-start.15) | collective-permute-done | bytes 213024 | tf_op jit(solution)/shard_map/ppermute | solution.py:48
  144.6 3.1 %collective-permute-done.16.p3 = s16[208,512]{1,0:T(8,128)(2,1)S(1)} collective-permute-done((s16[208,512]{1,0:T(8,128)(2,1)S(1)}, s16[208,512]{1,0:T(8,128)(2,1)S(1)}, u32[]{:S(2)}, u32[]{:S(2)}) %collective-permute-start.16) | collective-permute-done | bytes 213024 | tf_op jit(solution)/shard_map/ppermute | solution.py:48
  150.5 3.2 %collective-permute-start.27 = (s16[208,256]{1,0:T(8,128)(2,1)S(1)}, s16[208,256]{1,0:T(8,128)(2,1)S(1)}, u32[]{:S(2)}, u32[]{:S(2)}) collective-permute-start(s16[208,256]{1,0:T(8,128)(2,1)S(1)} %get-tuple-element.55), channel_id=1, source_target_pairs={{0,64},{1,65},{2,66},{3,67},{4,68},{5,69},{6,70},{7,71},{8,72},{9,... | collective-permute-start | bytes 319496 | tf_op jit(solution)/shard_map/ppermute | solution.py:48
  153.8 7.9 %collective-permute-start.30 = (s16[208,128]{1,0:T(8,128)(2,1)S(1)}, s16[208,128]{1,0:T(8,128)(2,1)S(1)}, u32[]{:S(2)}, u32[]{:S(2)}) collective-permute-start(s16[208,128]{1,0:T(8,128)(2,1)S(1)} %get-tuple-element.59), channel_id=1, source_target_pairs={{0,8},{1,9},{2,10},{3,11},{4,12},{5,13},{6,14},{7,15},{8,0},{9,1},... | collective-permute-start | bytes 159752 | tf_op jit(solution)/shard_map/ppermute | solution.py:48
  161.7 2.0 %collective-permute-start.31 = (s16[208,128]{1,0:T(8,128)(2,1)S(1)}, s16[208,128]{1,0:T(8,128)(2,1)S(1)}, u32[]{:S(2)}, u32[]{:S(2)}) collective-permute-start(s16[208,128]{1,0:T(8,128)(2,1)S(1)} %get-tuple-element.60), channel_id=1, source_target_pairs={{0,12},{1,13},{2,14},{3,15},{4,0},{5,1},{6,2},{7,3},{8,4},{9,5},{1... | collective-permute-start | bytes 159752 | tf_op jit(solution)/shard_map/ppermute | solution.py:48
  (59 shorter events, 30.2 us)
Async XLA Ops:
  5.0 17.7 %collective-permute-start.1 = (bf16[6,16,3072]{2,1,0:T(8,128)(2,1)S(1)}, bf16[6,16,3072]{2,1,0:T(8,128)(2,1)S(1)}, u32[]{:S(2)}, u32[]{:S(2)}) collective-permute-start(bf16[6,16,3072]{2,1,0:T(8,128)(2,1)S(1)} %get-tuple-element.34), channel_id=1, source_target_pairs={{0,32},{1,33},{2,34},{3,35},{4,36},{5,37},{6,38},{7,39},{8,40},{9,... | collective-permute-start | bytes 1769480 | tf_op jit(solution)/shard_map/ppermute | solution.py:48
  7.5 28.7 %collective-permute-start.3 = (bf16[6,16,3072]{2,1,0:T(8,128)(2,1)S(1)}, bf16[6,16,3072]{2,1,0:T(8,128)(2,1)S(1)}, u32[]{:S(2)}, u32[]{:S(2)}) collective-permute-start(bf16[6,16,3072]{2,1,0:T(8,128)(2,1)S(1)} %get-tuple-element.35), channel_id=1, source_target_pairs={{0,64},{1,65},{2,66},{3,67},{4,68},{5,69},{6,70},{7,71},{8,72},{9,... | collective-permute-start | bytes 1769480 | tf_op jit(solution)/shard_map/ppermute | solution.py:48
  10.8 26.9 %collective-permute-start.5 = (bf16[6,16,3072]{2,1,0:T(8,128)(2,1)S(1)}, bf16[6,16,3072]{2,1,0:T(8,128)(2,1)S(1)}, u32[]{:S(2)}, u32[]{:S(2)}) collective-permute-start(bf16[6,16,3072]{2,1,0:T(8,128)(2,1)S(1)} %get-tuple-element.36), channel_id=1, source_target_pairs={{0,96},{1,97},{2,98},{3,99},{4,100},{5,101},{6,102},{7,103},{8,104... | collective-permute-start | bytes 1769480 | tf_op jit(solution)/shard_map/ppermute | solution.py:48
  11.6 39.6 %collective-permute-start = (bf16[6,16,3072]{2,1,0:T(8,128)(2,1)S(1)}, bf16[6,16,3072]{2,1,0:T(8,128)(2,1)S(1)}, u32[]{:S(2)}, u32[]{:S(2)}) collective-permute-start(bf16[6,16,3072]{2,1,0:T(8,128)(2,1)S(1)} %get-tuple-element.33.refs_0_), channel_id=1, source_target_pairs={{0,16},{1,17},{2,18},{3,19},{4,20},{5,21},{6,22},{7,23},{8,24},{9,... | collective-permute-start | bytes 1769480 | tf_op jit(solution)/shard_map/ppermute | solution.py:48
  22.7 28.5 %collective-permute-start.2 = (bf16[6,16,3072]{2,1,0:T(8,128)(2,1)S(1)}, bf16[6,16,3072]{2,1,0:T(8,128)(2,1)S(1)}, u32[]{:S(2)}, u32[]{:S(2)}) collective-permute-start(bf16[6,16,3072]{2,1,0:T(8,128)(2,1)S(1)} %collective-permute-done.1.refs_2_), channel_id=1, source_target_pairs={{0,16},{1,17},{2,18},{3,19},{4,20},{5,21},{6,22},{7,23},{8,24},{9,... | collective-permute-start | bytes 1769480 | tf_op jit(solution)/shard_map/ppermute | solution.py:48
  36.2 15.0 %collective-permute-start.4 = (bf16[6,16,3072]{2,1,0:T(8,128)(2,1)S(1)}, bf16[6,16,3072]{2,1,0:T(8,128)(2,1)S(1)}, u32[]{:S(2)}, u32[]{:S(2)}) collective-permute-start(bf16[6,16,3072]{2,1,0:T(8,128)(2,1)S(1)} %collective-permute-done.3.refs_4_), channel_id=1, source_target_pairs={{0,16},{1,17},{2,18},{3,19},{4,20},{5,21},{6,22},{7,23},{8,24},{9,... | collective-permute-start | bytes 1769480 | tf_op jit(solution)/shard_map/ppermute | solution.py:48
  37.8 13.4 %collective-permute-start.6 = (bf16[6,16,3072]{2,1,0:T(8,128)(2,1)S(1)}, bf16[6,16,3072]{2,1,0:T(8,128)(2,1)S(1)}, u32[]{:S(2)}, u32[]{:S(2)}) collective-permute-start(bf16[6,16,3072]{2,1,0:T(8,128)(2,1)S(1)} %collective-permute-done.5.refs_6_), channel_id=1, source_target_pairs={{0,16},{1,17},{2,18},{3,19},{4,20},{5,21},{6,22},{7,23},{8,24},{9,... | collective-permute-start | bytes 1769480 | tf_op jit(solution)/shard_map/ppermute | solution.py:48
  37.8 2.5 %collective-permute-start.7 = (bf16[16,128]{1,0:T(8,128)(2,1)S(1)}, bf16[16,128]{1,0:T(8,128)(2,1)S(1)}, u32[]{:S(2)}, u32[]{:S(2)}) collective-permute-start(bf16[16,128]{1,0:T(8,128)(2,1)S(1)} %copy-done.1), channel_id=1, source_target_pairs={{0,16},{1,17},{2,18},{3,19},{4,20},{5,21},{6,22},{7,23},{8,24},{9,... | collective-permute-start | bytes 12296 | tf_op jit(solution)/shard_map/ppermute | solution.py:48
  40.2 2.5 %collective-permute-start.10 = (bf16[32,128]{1,0:T(8,128)(2,1)S(1)}, bf16[32,128]{1,0:T(8,128)(2,1)S(1)}, u32[]{:S(2)}, u32[]{:S(2)}) collective-permute-start(bf16[32,128]{1,0:T(8,128)(2,1)S(1)} %constant_dynamic-update-slice_fusion.refs_0_), channel_id=1, source_target_pairs={{0,96},{1,97},{2,98},{3,99},{4,100},{5,101},{6,102},{7,103},{8,104... | collective-permute-start | bytes 24584 | tf_op jit(solution)/shard_map/ppermute | solution.py:48
  42.7 4.0 %collective-permute-start.9 = (bf16[32,128]{1,0:T(8,128)(2,1)S(1)}, bf16[32,128]{1,0:T(8,128)(2,1)S(1)}, u32[]{:S(2)}, u32[]{:S(2)}) collective-permute-start(bf16[32,128]{1,0:T(8,128)(2,1)S(1)} %constant_dynamic-update-slice_fusion.refs_0_), channel_id=1, source_target_pairs={{0,64},{1,65},{2,66},{3,67},{4,68},{5,69},{6,70},{7,71},{8,72},{9,... | collective-permute-start | bytes 24584 | tf_op jit(solution)/shard_map/ppermute | solution.py:48
  46.8 3.7 %collective-permute-start.8 = (bf16[32,128]{1,0:T(8,128)(2,1)S(1)}, bf16[32,128]{1,0:T(8,128)(2,1)S(1)}, u32[]{:S(2)}, u32[]{:S(2)}) collective-permute-start(bf16[32,128]{1,0:T(8,128)(2,1)S(1)} %constant_dynamic-update-slice_fusion.refs_0_), channel_id=1, source_target_pairs={{0,32},{1,33},{2,34},{3,35},{4,36},{5,37},{6,38},{7,39},{8,40},{9,... | collective-permute-start | bytes 24584 | tf_op jit(solution)/shard_map/ppermute | solution.py:48
  59.5 16.0 %collective-permute-start.17 = (s16[784,512]{1,0:T(8,128)(2,1)S(1)}, s16[784,512]{1,0:T(8,128)(2,1)S(1)}, u32[]{:S(2)}, u32[]{:S(2)}) collective-permute-start(s16[784,512]{1,0:T(8,128)(2,1)S(1)} %shard_map.42), channel_id=1, source_target_pairs={{0,4},{1,5},{2,6},{3,7},{4,8},{5,9},{6,10},{7,11},{8,12},{9,13},{1... | collective-permute-start | bytes 2408456 | tf_op jit(solution)/shard_map/ppermute | solution.py:48
  60.8 19.9 %collective-permute-start.11 = (s16[784,512]{1,0:T(8,128)(2,1)S(1)}, s16[784,512]{1,0:T(8,128)(2,1)S(1)}, u32[]{:S(2)}, u32[]{:S(2)}) collective-permute-start(s16[784,512]{1,0:T(8,128)(2,1)S(1)} %shard_map.38), channel_id=1, source_target_pairs={{0,4},{1,5},{2,6},{3,7},{4,8},{5,9},{6,10},{7,11},{8,12},{9,13},{1... | collective-permute-start | bytes 2408456 | tf_op jit(solution)/shard_map/ppermute | solution.py:48
  62.1 28.4 %collective-permute-start.12 = (s16[784,512]{1,0:T(8,128)(2,1)S(1)}, s16[784,512]{1,0:T(8,128)(2,1)S(1)}, u32[]{:S(2)}, u32[]{:S(2)}) collective-permute-start(s16[784,512]{1,0:T(8,128)(2,1)S(1)} %shard_map.39), channel_id=1, source_target_pairs={{0,8},{1,9},{2,10},{3,11},{4,12},{5,13},{6,14},{7,15},{8,0},{9,1},... | collective-permute-start | bytes 2408456 | tf_op jit(solution)/shard_map/ppermute | solution.py:48
  65.1 25.9 %collective-permute-start.13 = (s16[784,512]{1,0:T(8,128)(2,1)S(1)}, s16[784,512]{1,0:T(8,128)(2,1)S(1)}, u32[]{:S(2)}, u32[]{:S(2)}) collective-permute-start(s16[784,512]{1,0:T(8,128)(2,1)S(1)} %shard_map.40), channel_id=1, source_target_pairs={{0,12},{1,13},{2,14},{3,15},{4,0},{5,1},{6,2},{7,3},{8,4},{9,5},{1... | collective-permute-start | bytes 2408456 | tf_op jit(solution)/shard_map/ppermute | solution.py:48
  68.8 30.4 %collective-permute-start.18 = (s16[784,512]{1,0:T(8,128)(2,1)S(1)}, s16[784,512]{1,0:T(8,128)(2,1)S(1)}, u32[]{:S(2)}, u32[]{:S(2)}) collective-permute-start(s16[784,512]{1,0:T(8,128)(2,1)S(1)} %shard_map.43), channel_id=1, source_target_pairs={{0,8},{1,9},{2,10},{3,11},{4,12},{5,13},{6,14},{7,15},{8,0},{9,1},... | collective-permute-start | bytes 2408456 | tf_op jit(solution)/shard_map/ppermute | solution.py:48
  75.5 24.5 %collective-permute-start.19 = (s16[784,512]{1,0:T(8,128)(2,1)S(1)}, s16[784,512]{1,0:T(8,128)(2,1)S(1)}, u32[]{:S(2)}, u32[]{:S(2)}) collective-permute-start(s16[784,512]{1,0:T(8,128)(2,1)S(1)} %shard_map.44), channel_id=1, source_target_pairs={{0,12},{1,13},{2,14},{3,15},{4,0},{5,1},{6,2},{7,3},{8,4},{9,5},{1... | collective-permute-start | bytes 2408456 | tf_op jit(solution)/shard_map/ppermute | solution.py:48
  80.7 19.3 %collective-permute-start.20 = (s16[3136,128]{1,0:T(8,128)(2,1)S(1)}, s16[3136,128]{1,0:T(8,128)(2,1)S(1)}, u32[]{:S(2)}, u32[]{:S(2)}) collective-permute-start(s16[3136,128]{1,0:T(8,128)(2,1)S(1)} %get-tuple-element.46), channel_id=1, source_target_pairs={{0,32},{1,33},{2,34},{3,35},{4,36},{5,37},{6,38},{7,39},{8,40},{9,... | collective-permute-start | bytes 2408456 | tf_op jit(solution)/shard_map/ppermute | solution.py:48
  90.5 23.1 %collective-permute-start.21 = (s16[3136,128]{1,0:T(8,128)(2,1)S(1)}, s16[3136,128]{1,0:T(8,128)(2,1)S(1)}, u32[]{:S(2)}, u32[]{:S(2)}) collective-permute-start(s16[3136,128]{1,0:T(8,128)(2,1)S(1)} %get-tuple-element.47), channel_id=1, source_target_pairs={{0,64},{1,65},{2,66},{3,67},{4,68},{5,69},{6,70},{7,71},{8,72},{9,... | collective-permute-start | bytes 2408456 | tf_op jit(solution)/shard_map/ppermute | solution.py:48
  91.0 35.6 %collective-permute-start.22 = (s16[3136,128]{1,0:T(8,128)(2,1)S(1)}, s16[3136,128]{1,0:T(8,128)(2,1)S(1)}, u32[]{:S(2)}, u32[]{:S(2)}) collective-permute-start(s16[3136,128]{1,0:T(8,128)(2,1)S(1)} %get-tuple-element.48), channel_id=1, source_target_pairs={{0,96},{1,97},{2,98},{3,99},{4,100},{5,101},{6,102},{7,103},{8,104... | collective-permute-start | bytes 2408456 | tf_op jit(solution)/shard_map/ppermute | solution.py:48
  99.1 35.4 %collective-permute-start.14 = (s16[208,512]{1,0:T(8,128)(2,1)S(1)}, s16[208,512]{1,0:T(8,128)(2,1)S(1)}, u32[]{:S(2)}, u32[]{:S(2)}) collective-permute-start(s16[208,512]{1,0:T(8,128)(2,1)S(1)} %get-tuple-element.40), channel_id=1, source_target_pairs={{0,1},{1,2},{2,3},{3,0},{4,5},{5,6},{6,7},{7,4},{8,9},{9,10},{10,1... | collective-permute-start | bytes 638984 | tf_op jit(solution)/shard_map/ppermute | solution.py:48
  129.4 18.3 %collective-permute-start.23 = (s16[208,1024]{1,0:T(8,128)(2,1)S(1)}, s16[208,1024]{1,0:T(8,128)(2,1)S(1)}, u32[]{:S(2)}, u32[]{:S(2)}) collective-permute-start(s16[208,1024]{1,0:T(8,128)(2,1)S(1)} %get-tuple-element.50), channel_id=1, source_target_pairs={{0,1},{1,2},{2,3},{3,0},{4,5},{5,6},{6,7},{7,4},{8,9},{9,10},{10,1... | collective-permute-start | bytes 1277960 | tf_op jit(solution)/shard_map/ppermute | solution.py:48
  129.5 18.3 %collective-permute-start.24 = (s16[208,1024]{1,0:T(8,128)(2,1)S(1)}, s16[208,1024]{1,0:T(8,128)(2,1)S(1)}, u32[]{:S(2)}, u32[]{:S(2)}) collective-permute-start(s16[208,1024]{1,0:T(8,128)(2,1)S(1)} %get-tuple-element.51), channel_id=1, source_target_pairs={{0,2},{1,3},{2,0},{3,1},{4,6},{5,7},{6,4},{7,5},{8,10},{9,11},{10,... | collective-permute-start | bytes 1277960 | tf_op jit(solution)/shard_map/ppermute | solution.py:48
  132.0 15.7 %collective-permute-start.25 = (s16[208,1024]{1,0:T(8,128)(2,1)S(1)}, s16[208,1024]{1,0:T(8,128)(2,1)S(1)}, u32[]{:S(2)}, u32[]{:S(2)}) collective-permute-start(s16[208,1024]{1,0:T(8,128)(2,1)S(1)} %get-tuple-element.52), channel_id=1, source_target_pairs={{0,3},{1,0},{2,1},{3,2},{4,7},{5,4},{6,5},{7,6},{8,11},{9,8},{10,9... | collective-permute-start | bytes 1277960 | tf_op jit(solution)/shard_map/ppermute | solution.py:48
  134.0 10.6 %collective-permute-start.15 = (s16[208,512]{1,0:T(8,128)(2,1)S(1)}, s16[208,512]{1,0:T(8,128)(2,1)S(1)}, u32[]{:S(2)}, u32[]{:S(2)}) collective-permute-start(s16[208,512]{1,0:T(8,128)(2,1)S(1)} %get-tuple-element.41), channel_id=1, source_target_pairs={{0,2},{1,3},{2,0},{3,1},{4,6},{5,7},{6,4},{7,5},{8,10},{9,11},{10,... | collective-permute-start | bytes 638984 | tf_op jit(solution)/shard_map/ppermute | solution.py:48
  134.5 13.2 %collective-permute-start.16 = (s16[208,512]{1,0:T(8,128)(2,1)S(1)}, s16[208,512]{1,0:T(8,128)(2,1)S(1)}, u32[]{:S(2)}, u32[]{:S(2)}) collective-permute-start(s16[208,512]{1,0:T(8,128)(2,1)S(1)} %get-tuple-element.42), channel_id=1, source_target_pairs={{0,3},{1,0},{2,1},{3,2},{4,7},{5,4},{6,5},{7,6},{8,11},{9,8},{10,9... | collective-permute-start | bytes 638984 | tf_op jit(solution)/shard_map/ppermute | solution.py:48
  149.0 12.6 %collective-permute-start.29 = (s16[208,128]{1,0:T(8,128)(2,1)S(1)}, s16[208,128]{1,0:T(8,128)(2,1)S(1)}, u32[]{:S(2)}, u32[]{:S(2)}) collective-permute-start(s16[208,128]{1,0:T(8,128)(2,1)S(1)} %get-tuple-element.58), channel_id=1, source_target_pairs={{0,4},{1,5},{2,6},{3,7},{4,8},{5,9},{6,10},{7,11},{8,12},{9,13},{1... | collective-permute-start | bytes 159752 | tf_op jit(solution)/shard_map/ppermute | solution.py:48
  149.1 15.8 %collective-permute-start.26 = (s16[208,256]{1,0:T(8,128)(2,1)S(1)}, s16[208,256]{1,0:T(8,128)(2,1)S(1)}, u32[]{:S(2)}, u32[]{:S(2)}) collective-permute-start(s16[208,256]{1,0:T(8,128)(2,1)S(1)} %get-tuple-element.54), channel_id=1, source_target_pairs={{0,32},{1,33},{2,34},{3,35},{4,36},{5,37},{6,38},{7,39},{8,40},{9,... | collective-permute-start | bytes 319496 | tf_op jit(solution)/shard_map/ppermute | solution.py:48
  150.5 14.4 %collective-permute-start.27 = (s16[208,256]{1,0:T(8,128)(2,1)S(1)}, s16[208,256]{1,0:T(8,128)(2,1)S(1)}, u32[]{:S(2)}, u32[]{:S(2)}) collective-permute-start(s16[208,256]{1,0:T(8,128)(2,1)S(1)} %get-tuple-element.55), channel_id=1, source_target_pairs={{0,64},{1,65},{2,66},{3,67},{4,68},{5,69},{6,70},{7,71},{8,72},{9,... | collective-permute-start | bytes 319496 | tf_op jit(solution)/shard_map/ppermute | solution.py:48
  153.8 11.2 %collective-permute-start.28 = (s16[208,256]{1,0:T(8,128)(2,1)S(1)}, s16[208,256]{1,0:T(8,128)(2,1)S(1)}, u32[]{:S(2)}, u32[]{:S(2)}) collective-permute-start(s16[208,256]{1,0:T(8,128)(2,1)S(1)} %get-tuple-element.56), channel_id=1, source_target_pairs={{0,96},{1,97},{2,98},{3,99},{4,100},{5,101},{6,102},{7,103},{8,104... | collective-permute-start | bytes 319496 | tf_op jit(solution)/shard_map/ppermute | solution.py:48
  153.8 9.9 %collective-permute-start.30 = (s16[208,128]{1,0:T(8,128)(2,1)S(1)}, s16[208,128]{1,0:T(8,128)(2,1)S(1)}, u32[]{:S(2)}, u32[]{:S(2)}) collective-permute-start(s16[208,128]{1,0:T(8,128)(2,1)S(1)} %get-tuple-element.59), channel_id=1, source_target_pairs={{0,8},{1,9},{2,10},{3,11},{4,12},{5,13},{6,14},{7,15},{8,0},{9,1},... | collective-permute-start | bytes 159752 | tf_op jit(solution)/shard_map/ppermute | solution.py:48
  161.7 3.3 %collective-permute-start.31 = (s16[208,128]{1,0:T(8,128)(2,1)S(1)}, s16[208,128]{1,0:T(8,128)(2,1)S(1)}, u32[]{:S(2)}, u32[]{:S(2)}) collective-permute-start(s16[208,128]{1,0:T(8,128)(2,1)S(1)} %get-tuple-element.60), channel_id=1, source_target_pairs={{0,12},{1,13},{2,14},{3,15},{4,0},{5,1},{6,2},{7,3},{8,4},{9,5},{1... | collective-permute-start | bytes 159752 | tf_op jit(solution)/shard_map/ppermute | solution.py:48
  (2 other events, 39.4 us)

commit v3 on v1

--- a/solution.py
+++ b/solution.py
@@ -188,20 +188,21 @@
     total = turned.shape[0] // RING
     g = lax.rem(jnp.where(at[1] == 0, at[2], at[3]) + shift, RING)
     left = turned[pl.ds(pl.multiple_of(g * total, 256), total), :]
-    write(out, 0, jnp.dot(left, bulk[...], preferred_element_type=F32))
+    half = bulk.shape[1] // 2
+    for n in range(2):
+        lanes = slice(n * half, (n + 1) * half)
+        write(out.at[:, lanes], 0, jnp.dot(left, bulk[:, lanes], preferred_element_type=F32))
 
 
 def bulk_k(at, bulk, turned, shift):
     depth, columns = bulk.shape
     total = turned.shape[0] // RING
     shape = (total + (TAIL if shift else 0), columns)
-    half = columns // 2
     return pl.pallas_call(
         functools.partial(bulk_body, shift),
-        grid=(2,),
         out_shape=jax.ShapeDtypeStruct(shape, I16 if shift else F32),
-        in_specs=[scalars(), pl.BlockSpec((depth, half), lambda j: (0, j)), whole()],
-        out_specs=pl.BlockSpec((shape[0], half), lambda j: (0, j)),
+        in_specs=[scalars(), whole(), whole()],
+        out_specs=whole(),
         compiler_params=params(28),
         cost_estimate=cost(2 * depth * total * columns, total * columns * 2),
     )(at, bulk, turned)
@@ -233,96 +234,84 @@
     )(rest, turned)
 
 
-def second_body(at, bulk, ba, bb, bd, rest, ra, rb, rd, kept, *outs):
+def gathered(own, arrived, first, tail, row, lanes):
+    v = own[pl.ds(pl.multiple_of(first[0] + row, 64), first[2]), lanes]
+    for m in arrived:
+        cut = pl.ds(pl.multiple_of(first[1] + row, 16), first[2])
+        v = v + plain(m[cut, lanes]) * scale_of(m[tail:tail + TAIL, lanes])
+    return v
+
+
+def second_body(groups, at, own, a, b, d, kept, *outs):
     high = kept.shape[0]
-    wide = kept.shape[1]
-    total = bulk.shape[0]
+    total = own.shape[0] // groups
     h = jnp.where(at[1] == 0, at[3], at[2])
-
-    def part(k, own, arrived, first, lanes):
-        row = pl.multiple_of(lax.rem(h + k, RING) * high, 64)
-        v = own[pl.ds(pl.multiple_of(first * total + row, 64), high), :]
-        for m in arrived:
-            start = first * (total + TAIL)
-            v = v + plain(m[pl.ds(pl.multiple_of(start + row, 16), high), :]) * scale_of(
-                m[start + total:start + total + TAIL, :]
-            )
-        if k == 0:
-            kept[:, lanes] = v
-        else:
-            e = exponent(jnp.max(jnp.abs(v), axis=0, keepdims=True))
-            outs[k - 1][:high, lanes] = coded(v, e)
-            outs[k - 1][high:, lanes] = marked(e)
-
-    @pl.when(pl.program_id(0) < RING)
-    def _():
-        for k in range(RING):
-            part(k, bulk, (ba, bb, bd), 0, slice(0, wide))
-
-    @pl.when(pl.program_id(0) >= RING)
-    def _():
-        for k in range(RING):
-            for n in range(2):
-                part(k, rest, (ra, rb, rd), n, slice(n * wide // 2, (n + 1) * wide // 2))
-
-
-def second(at, bulk, rest):
-    total, columns = bulk[0].shape
-    wide, high = columns // RING, total // RING
-    narrow = wide // 2
-    every = columns + RING * narrow
-
-    def of_bulk(rows):
-        return pl.BlockSpec((rows, wide), lambda j: (0, jnp.minimum(j, RING - 1)))
-
-    def of_rest(rows):
-        return pl.BlockSpec((2 * rows, narrow), lambda j: (jnp.maximum(j - RING, 0), 0))
-
-    return pl.pallas_call(
-        second_body,
-        grid=(RING + 2,),
+    step = own.shape[1] if groups > 1 else 256
+    for k in range(RING):
+        row = lax.rem(h + k, RING) * high
+        out = kept if k == 0 else outs[k - 1]
+        for n in range(groups):
+            start = n * (total + TAIL)
+            for lane in range(0, own.shape[1], step):
+                v = gathered(
+                    own, (a, b, d), (n * total, start, high), start + total, row, slice(lane, lane + step)
+                )
+                to = n * own.shape[1] + lane
+                write(out.at[:, to:to + step], 0, v)
+
+
+def second(at, parts, groups):
+    total, columns = parts[0].shape
+    high, every = total // groups // RING, columns * groups
+    return list(pl.pallas_call(
+        functools.partial(second_body, groups),
         out_shape=[jax.ShapeDtypeStruct((high, every), F32)]
         + [jax.ShapeDtypeStruct((high + TAIL, every), I16)] * 3,
-        in_specs=[scalars(), of_bulk(total)] + [of_bulk(total + TAIL)] * 3
-        + [of_rest(total)] + [of_rest(total + TAIL)] * 3,
-        out_specs=[pl.BlockSpec((n, wide), lambda j: (0, j)) for n in [high] + [high + TAIL] * 3],
+        in_specs=[scalars()] + [whole()] * 4,
+        out_specs=[whole()] * 4,
         compiler_params=params(24),
-        cost_estimate=cost(total * every * 16, total * every * 10),
+        cost_estimate=cost(total * columns * 16, total * columns * 10),
         name="second_sum",
-    )(at, *bulk, *rest)
-
-
-def third_body(at, own, a, b, d, bulk, b1, b2, b3, rest, r1, r2, r3):
-    high, wide = bulk.shape
-    narrow = rest.shape[1]
-    g = jnp.where(at[1] == 0, at[2], at[3])
-    for base, step, place_at, outs in (
-        (0, wide, at[0], (bulk, b1, b2, b3)), (RING * wide, narrow, g, (rest, r1, r2, r3))
-    ):
-        for k in range(RING):
-            cut = pl.ds(pl.multiple_of(base + lax.rem(place_at + k, RING) * step, 128), step)
-            v = own[:, cut]
-            for m in (a, b, d):
-                v = v + plain(m[:high, cut]) * scale_of(m[high:, cut])
-            write(outs[k], 0, v)
-
-
-def third(at, own, arrived, wide, narrow):
-    high = own.shape[0]
-
-    def four(lanes):
-        return [jax.ShapeDtypeStruct((high, lanes), F32)] + [jax.ShapeDtypeStruct((high + TAIL, lanes), I16)] * 3
-
-    out = pl.pallas_call(
-        third_body,
-        out_shape=four(wide) + four(narrow),
+    )(at, *parts))
+
+
+def third_body(by_z, at, own, a, b, d, *outs):
+    high, step = outs[0].shape
+    start = at[0] if by_z else jnp.where(at[1] == 0, at[2], at[3])
+    for k in range(RING):
+        cut = pl.ds(pl.multiple_of(lax.rem(start + k, RING) * step, 128), step)
+        write(outs[k], 0, gathered(own, (a, b, d), (0, 0, high), high, 0, cut))
+
+
+def third(at, parts, by_z):
+    high, every = parts[0].shape
+    wide = every // RING
+    return list(pl.pallas_call(
+        functools.partial(third_body, by_z),
+        out_shape=[jax.ShapeDtypeStruct((high, wide), F32)] + [jax.ShapeDtypeStruct((high + TAIL, wide), I16)] * 3,
         in_specs=[scalars()] + [whole()] * 4,
-        out_specs=[whole()] * 8,
+        out_specs=[whole()] * 4,
         compiler_params=params(16),
-        cost_estimate=cost(own.size * 16, own.size * 10),
+        cost_estimate=cost(high * every * 16, high * every * 10),
         name="third_sum",
-    )(at, own, *arrived)
-    return list(out[:4]), list(out[4:])
+    )(at, *parts))
+
+
+def tick_body(at, out):
+    for n in range(RING):
+        out[n] = at[n]
+
+
+def tick(at):
+    return pl.pallas_call(
+        tick_body,
+        out_shape=jax.ShapeDtypeStruct(at.shape, at.dtype),
+        in_specs=[scalars()],
+        out_specs=scalars(),
+        compiler_params=params(1),
+        cost_estimate=cost(1000, 32),
+        name="tick",
+    )(at)
 
 
 def finish_body(own, a, b, d, rest, ra, rb, rd, out):
@@ -351,7 +340,6 @@
     at = jnp.stack([lax.axis_index(a) for a in AXES]).astype(jnp.int32)
     blocks = survive.shape[2]
     gate = jnp.repeat(survive.reshape(1, blocks).astype(BF), ao // blocks, axis=1)
-    wide = ao // 8
 
     parts = screen(at, half, gate, metric)
     here = [parts[0]] + [None] * 3
@@ -372,17 +360,26 @@
         for k, v in zip(ORDER[2 * pair:2 * pair + 2], out):
             rest[k] = send(v, along_z(k)) if k else v
 
+    def onward(parts, shift):
+        for k in ORDER[:3]:
+            parts[k] = send(parts[k], shift(k))
+
+    rest_step(0)
     bulk_step(2)
-    rest_step(0)
+    rest_step(1)
     bulk_step(1)
     bulk_step(3)
-    rest_step(1)
     bulk_step(0)
-    own, *out = second(at, bulk, rest)
-    arrived = [send(out[k - 1], second_axis(k)) for k in (2, 1, 3)]
-    bulk, rest = third(at, own, arrived, wide - wide // 3, wide // 3)
-    bulk[1:] = [send(bulk[k], along_z(k)) for k in (1, 2, 3)]
-    rest[1:] = [send(rest[k], first_axis(k)) for k in (1, 2, 3)]
+    rest = second(at, rest, RING)
+    onward(rest, second_axis)
+    then = tick(at)
+    bulk = second(then, bulk, 1)
+    onward(bulk, second_axis)
+    rest = third(at, rest, False)
+    onward(rest, first_axis)
+    then = tick(then)
+    bulk = third(then, bulk, True)
+    onward(bulk, along_z)
     return finish(bulk, rest)
 
 

time: 141 us -> 140 us (level)
  the two profiles are of different devices: /device:TPU:8 before, /device:TPU:0 now
where the time goes in v3:
time: 140 us
  waiting for transfers between devices  73.8 us (53%)
  starting transfers between devices  34.4 us (25%)
  Pallas kernels  28.3 us (20%)
  local copies, waits for them, and re-layouts  2.44 us (2%)
    ppermute x25, waiting for transfers between devices, send(): return lax.ppermute(v, AXES, moves(shift))  73.8 us
    ppermute x25, starting transfers between devices, send(): return lax.ppermute(v, AXES, moves(shift))  34.4 us
    pallas_call x4, Pallas kernels, bulk_k(): pl.pallas_call(functools.partial(bulk_body, shift), out_shape=jax.ShapeDt...  9.28 us
    pallas_call x2, Pallas kernels, rest_k(): pl.pallas_call(rest_body, grid=(RING,), out_shape=[jax.ShapeDtypeStruct((...  4.73 us
    pallas_call x2, Pallas kernels, second(): pl.pallas_call(functools.partial(second_body, groups), out_shape=[jax.Sha...  3.75 us
    pallas_call x1, Pallas kernels, fit(): pl.pallas_call(fit_body, grid=(group,), out_shape=[jax.ShapeDtypeStruct((...  3.62 us
  transfers between devices with their start and end apart: 25, of which 10 were waited for; matrix products, arithmetic and copies ran while one was open for 0% of the time, Pallas kernels for 10%

profile of v3, /device:TPU:0, one launch (start us, length us, event | category | flops | bytes accessed | tf_op | source)
XLA Modules:
  0.0 139.9 jit_solution(7651604702033884090)
XLA Ops:
  0.8 1.7 %copy-done = bf16[16,24,3072]{2,1,0:T(8,128)(2,1)S(1)} copy-done((bf16[16,24,3072]{2,1,0:T(8,128)(2,1)S(1)}, bf16[16,24,3072]{2,1,0:T(8,128)(2,1)}, u32[]{:S(2)}) %copy-start) | copy-done | bytes 2359320
  3.2 2.0 %shard_map.37 = (bf16[6,16,3200]{2,1,0:T(8,128)(2,1)S(1)}, bf16[6,16,3200]{2,1,0:T(8,128)(2,1)S(1)}, bf16[6,16,3200]{2,1,0:T(8,128)(2,1)S(1)}, bf16[6,16,3200]{2,1,0:T(8,128)(2,1)S(1)}) custom-call(s32[4]{0:T(128)S(1)} %pad_add_fusion.at, bf16[16,24,3072]{2,1,0:T(8,128)(2,1)S(1)} %copy-done, bf16[1,3072]{1,0:T(2,128)(2,1)S(1)} %bitcast.12, ...), custom_call_target="tpu_custom_call" | custom-call | flops 1179648 | bytes 4718592 | tf_op jit(solution)/shard_map/pallas_call | solution.py:89
  5.2 2.1 %collective-permute-start.1 = (bf16[6,16,3200]{2,1,0:T(8,128)(2,1)S(1)}, bf16[6,16,3200]{2,1,0:T(8,128)(2,1)S(1)}, u32[]{:S(2)}, u32[]{:S(2)}) collective-permute-start(bf16[6,16,3200]{2,1,0:T(8,128)(2,1)S(1)} %get-tuple-element.33), channel_id=1, source_target_pairs={{0,32},{1,33},{2,34},{3,35},{4,36},{5,37},{6,38},{7,39},{8,40},{9,... | collective-permute-start | bytes 1843208 | tf_op jit(solution)/shard_map/ppermute | solution.py:48
  7.3 3.6 %collective-permute-start.3 = (bf16[6,16,3200]{2,1,0:T(8,128)(2,1)S(1)}, bf16[6,16,3200]{2,1,0:T(8,128)(2,1)S(1)}, u32[]{:S(2)}, u32[]{:S(2)}) collective-permute-start(bf16[6,16,3200]{2,1,0:T(8,128)(2,1)S(1)} %get-tuple-element.34), channel_id=1, source_target_pairs={{0,64},{1,65},{2,66},{3,67},{4,68},{5,69},{6,70},{7,71},{8,72},{9,... | collective-permute-start | bytes 1843208 | tf_op jit(solution)/shard_map/ppermute | solution.py:48
  11.9 11.4 %collective-permute-done.1.refs_2_ = bf16[6,16,3200]{2,1,0:T(8,128)(2,1)S(1)} collective-permute-done((bf16[6,16,3200]{2,1,0:T(8,128)(2,1)S(1)}, bf16[6,16,3200]{2,1,0:T(8,128)(2,1)S(1)}, u32[]{:S(2)}, u32[]{:S(2)}) %collective-permute-start.1) | collective-permute-done | bytes 614432 | tf_op jit(solution)/shard_map/ppermute | solution.py:48
  23.3 14.3 %collective-permute-done.3.refs_4_ = bf16[6,16,3200]{2,1,0:T(8,128)(2,1)S(1)} collective-permute-done((bf16[6,16,3200]{2,1,0:T(8,128)(2,1)S(1)}, bf16[6,16,3200]{2,1,0:T(8,128)(2,1)S(1)}, u32[]{:S(2)}, u32[]{:S(2)}) %collective-permute-start.3) | collective-permute-done | bytes 614432 | tf_op jit(solution)/shard_map/ppermute | solution.py:48
  38.1 1.5 %collective-permute-done.4.refs_5_ = bf16[6,16,3200]{2,1,0:T(8,128)(2,1)S(1)} collective-permute-done((bf16[6,16,3200]{2,1,0:T(8,128)(2,1)S(1)}, bf16[6,16,3200]{2,1,0:T(8,128)(2,1)S(1)}, u32[]{:S(2)}, u32[]{:S(2)}) %collective-permute-start.4) | collective-permute-done | bytes 614432 | tf_op jit(solution)/shard_map/ppermute | solution.py:48
  40.5 3.6 %shard_map.38 = (bf16[768,1024]{1,0:T(8,128)(2,1)S(1)}, bf16[768,512]{1,0:T(8,128)(2,1)S(1)}, bf16[3072,768]{1,0:T(8,128)(2,1)S(1)}) custom-call(s32[4]{0:T(128)S(1)} %pad_add_fusion.at, bf16[6,16,3200]{2,1,0:T(8,128)(2,1)S(1)} %get-tuple-element.32.refs_0_, bf16[6,16,3200]{2,1,0:T(8,128)(2,1)S(1)} %collective-permute-done.refs_1_, ...), custom_call_target="tpu_custom_call" | custom-call | flops 603979776 | bytes 14155776 | tf_op jit(solution)/shard_map/pallas_call | solution.py:143
  44.2 2.4 %shard_map.42 = s16[784,1024]{1,0:T(8,128)(2,1)S(1)} custom-call(s32[4]{0:T(128)S(1)} %pad_add_fusion.at, bf16[768,1024]{1,0:T(8,128)(2,1)S(1)} %get-tuple-element.36.bulk, bf16[3072,768]{1,0:T(8,128)(2,1)S(1)} %get-tuple-element.37.turned), custom_call_target="tpu_custom_call" | custom-call | flops 1207959552 | bytes 1572864 | tf_op jit(solution)/shard_map/pallas_call | solution.py:201
  46.6 2.5 %shard_map.41 = s16[784,1024]{1,0:T(8,128)(2,1)S(1)} custom-call(s32[4]{0:T(128)S(1)} %pad_add_fusion.at, bf16[768,1024]{1,0:T(8,128)(2,1)S(1)} %get-tuple-element.36.bulk, bf16[3072,768]{1,0:T(8,128)(2,1)S(1)} %get-tuple-element.37.turned), custom_call_target="tpu_custom_call" | custom-call | flops 1207959552 | bytes 1572864 | tf_op jit(solution)/shard_map/pallas_call | solution.py:201
  49.1 2.3 %shard_map.43 = (s16[3136,128]{1,0:T(8,128)(2,1)S(1)}, f32[3072,128]{1,0:T(8,128)S(1)}) custom-call(bf16[768,512]{1,0:T(8,128)(2,1)S(1)} %get-tuple-element.46.rest, bf16[3072,768]{1,0:T(8,128)(2,1)S(1)} %get-tuple-element.37.turned), custom_call_target="tpu_custom_call" | custom-call | flops 1207959552 | bytes 1572864 | tf_op jit(solution)/shard_map/pallas_call | solution.py:223
  51.4 1.4 collective-permute-start.18
  52.7 2.4 %shard_map.40 = s16[784,1024]{1,0:T(8,128)(2,1)S(1)} custom-call(s32[4]{0:T(128)S(1)} %pad_add_fusion.at, bf16[768,1024]{1,0:T(8,128)(2,1)S(1)} %get-tuple-element.36.bulk, bf16[3072,768]{1,0:T(8,128)(2,1)S(1)} %get-tuple-element.37.turned), custom_call_target="tpu_custom_call" | custom-call | flops 1207959552 | bytes 1572864 | tf_op jit(solution)/shard_map/pallas_call | solution.py:201
  55.2 2.8 %collective-permute-start.9 = (s16[784,1024]{1,0:T(8,128)(2,1)S(1)}, s16[784,1024]{1,0:T(8,128)(2,1)S(1)}, u32[]{:S(2)}, u32[]{:S(2)}) collective-permute-start(s16[784,1024]{1,0:T(8,128)(2,1)S(1)} %shard_map.42), channel_id=1, source_target_pairs={{0,12},{1,13},{2,14},{3,15},{4,0},{5,1},{6,2},{7,3},{8,4},{9,5},{1... | collective-permute-start | bytes 4816904 | tf_op jit(solution)/shard_map/ppermute | solution.py:48
  59.7 2.5 %shard_map.44 = (s16[3136,128]{1,0:T(8,128)(2,1)S(1)}, s16[3136,128]{1,0:T(8,128)(2,1)S(1)}) custom-call(bf16[768,512]{1,0:T(8,128)(2,1)S(1)} %get-tuple-element.46.rest, bf16[3072,768]{1,0:T(8,128)(2,1)S(1)} %get-tuple-element.37.turned), custom_call_target="tpu_custom_call" | custom-call | flops 1207959552 | bytes 1572864 | tf_op jit(solution)/shard_map/pallas_call | solution.py:223
  63.0 8.4 %collective-permute-done.18.d = s16[3136,128]{1,0:T(8,128)(2,1)S(1)} collective-permute-done((s16[3136,128]{1,0:T(8,128)(2,1)S(1)}, s16[3136,128]{1,0:T(8,128)(2,1)S(1)}, u32[]{:S(2)}, u32[]{:S(2)}) %collective-permute-start.18) | collective-permute-done | bytes 802848 | tf_op jit(solution)/shard_map/ppermute | solution.py:48
  71.4 1.4 collective-permute-start.17
  73.9 1.9 %shard_map.39.own = f32[768,1024]{1,0:T(8,128)S(1)} custom-call(s32[4]{0:T(128)S(1)} %pad_add_fusion.at, bf16[768,1024]{1,0:T(8,128)(2,1)S(1)} %get-tuple-element.36.bulk, bf16[3072,768]{1,0:T(8,128)(2,1)S(1)} %get-tuple-element.37.turned), custom_call_target="tpu_custom_call" | custom-call | flops 1207959552 | bytes 1572864 | tf_op jit(solution)/shard_map/pallas_call | solution.py:201
  75.8 23.8 %collective-permute-done.16.a = s16[3136,128]{1,0:T(8,128)(2,1)S(1)} collective-permute-done((s16[3136,128]{1,0:T(8,128)(2,1)S(1)}, s16[3136,128]{1,0:T(8,128)(2,1)S(1)}, u32[]{:S(2)}, u32[]{:S(2)}) %collective-permute-start.16) | collective-permute-done | bytes 802848 | tf_op jit(solution)/shard_map/ppermute | solution.py:48
  99.6 1.4 %second_sum.3 = (f32[192,512]{1,0:T(8,128)S(1)}, s16[208,512]{1,0:T(8,128)(2,1)S(1)}, s16[208,512]{1,0:T(8,128)(2,1)S(1)}, s16[208,512]{1,0:T(8,128)(2,1)S(1)}) custom-call(s32[4]{0:T(128)S(1)} %pad_add_fusion.at, f32[3072,128]{1,0:T(8,128)S(1)} %get-tuple-element.47.own, s16[3136,128]{1,0:T(8,128)(2,1)S(1)} %collective-permute-done.16.a, ...), custom_call_target="tpu_custom_call" | custom-call | flops 6291456 | bytes 3932160 | tf_op jit(solution)/shard_map/second_sum/pallas_call | solution.py:266
  101.0 2.1 %collective-permute-start.19 = (s16[208,512]{1,0:T(8,128)(2,1)S(1)}, s16[208,512]{1,0:T(8,128)(2,1)S(1)}, u32[]{:S(2)}, u32[]{:S(2)}) collective-permute-start(s16[208,512]{1,0:T(8,128)(2,1)S(1)} %get-tuple-element.52), channel_id=1, source_target_pairs={{0,1},{1,2},{2,3},{3,0},{4,5},{5,6},{6,7},{7,4},{8,9},{9,10},{10,1... | collective-permute-start | bytes 638984 | tf_op jit(solution)/shard_map/ppermute | solution.py:48
  103.2 2.3 %second_sum.2 = (f32[192,1024]{1,0:T(8,128)S(1)}, s16[208,1024]{1,0:T(8,128)(2,1)S(1)}, s16[208,1024]{1,0:T(8,128)(2,1)S(1)}, s16[208,1024]{1,0:T(8,128)(2,1)S(1)}) custom-call(s32[4]{0:T(128)S(1)} %tick.2.at, f32[768,1024]{1,0:T(8,128)S(1)} %shard_map.39.own, s16[784,1024]{1,0:T(8,128)(2,1)S(1)} %collective-permute-done.7.a, ...), custom_call_target="tpu_custom_call" | custom-call | flops 12582912 | bytes 7864320 | tf_op jit(solution)/shard_map/second_sum/pallas_call | solution.py:266
  105.9 2.5 %collective-permute-start.11 = (s16[208,1024]{1,0:T(8,128)(2,1)S(1)}, s16[208,1024]{1,0:T(8,128)(2,1)S(1)}, u32[]{:S(2)}, u32[]{:S(2)}) collective-permute-start(s16[208,1024]{1,0:T(8,128)(2,1)S(1)} %get-tuple-element.40), channel_id=1, source_target_pairs={{0,2},{1,3},{2,0},{3,1},{4,6},{5,7},{6,4},{7,5},{8,10},{9,11},{10,... | collective-permute-start | bytes 1277960 | tf_op jit(solution)/shard_map/ppermute | solution.py:48
  108.4 1.7 %collective-permute-start.12 = (s16[208,1024]{1,0:T(8,128)(2,1)S(1)}, s16[208,1024]{1,0:T(8,128)(2,1)S(1)}, u32[]{:S(2)}, u32[]{:S(2)}) collective-permute-start(s16[208,1024]{1,0:T(8,128)(2,1)S(1)} %get-tuple-element.41), channel_id=1, source_target_pairs={{0,3},{1,0},{2,1},{3,2},{4,7},{5,4},{6,5},{7,6},{8,11},{9,8},{10,9... | collective-permute-start | bytes 1277960 | tf_op jit(solution)/shard_map/ppermute | solution.py:48
  110.1 1.7 %collective-permute-start.20 = (s16[208,512]{1,0:T(8,128)(2,1)S(1)}, s16[208,512]{1,0:T(8,128)(2,1)S(1)}, u32[]{:S(2)}, u32[]{:S(2)}) collective-permute-start(s16[208,512]{1,0:T(8,128)(2,1)S(1)} %get-tuple-element.53), channel_id=1, source_target_pairs={{0,2},{1,3},{2,0},{3,1},{4,6},{5,7},{6,4},{7,5},{8,10},{9,11},{10,... | collective-permute-start | bytes 638984 | tf_op jit(solution)/shard_map/ppermute | solution.py:48
  114.3 7.2 %collective-permute-done.20.b = s16[208,512]{1,0:T(8,128)(2,1)S(1)} collective-permute-done((s16[208,512]{1,0:T(8,128)(2,1)S(1)}, s16[208,512]{1,0:T(8,128)(2,1)S(1)}, u32[]{:S(2)}, u32[]{:S(2)}) %collective-permute-start.20) | collective-permute-done | bytes 213024 | tf_op jit(solution)/shard_map/ppermute | solution.py:48
  121.5 3.6 %collective-permute-done.21.d = s16[208,512]{1,0:T(8,128)(2,1)S(1)} collective-permute-done((s16[208,512]{1,0:T(8,128)(2,1)S(1)}, s16[208,512]{1,0:T(8,128)(2,1)S(1)}, u32[]{:S(2)}, u32[]{:S(2)}) %collective-permute-start.21) | collective-permute-done | bytes 213024 | tf_op jit(solution)/shard_map/ppermute | solution.py:48
  125.8 1.6 %collective-permute-start.22 = (s16[208,128]{1,0:T(8,128)(2,1)S(1)}, s16[208,128]{1,0:T(8,128)(2,1)S(1)}, u32[]{:S(2)}, u32[]{:S(2)}) collective-permute-start(s16[208,128]{1,0:T(8,128)(2,1)S(1)} %get-tuple-element.56), channel_id=1, source_target_pairs={{0,4},{1,5},{2,6},{3,7},{4,8},{5,9},{6,10},{7,11},{8,12},{9,13},{1... | collective-permute-start | bytes 159752 | tf_op jit(solution)/shard_map/ppermute | solution.py:48
  129.6 2.5 %collective-permute-start.15 = (s16[208,256]{1,0:T(8,128)(2,1)S(1)}, s16[208,256]{1,0:T(8,128)(2,1)S(1)}, u32[]{:S(2)}, u32[]{:S(2)}) collective-permute-start(s16[208,256]{1,0:T(8,128)(2,1)S(1)} %get-tuple-element.45), channel_id=1, source_target_pairs={{0,96},{1,97},{2,98},{3,99},{4,100},{5,101},{6,102},{7,103},{8,104... | collective-permute-start | bytes 319496 | tf_op jit(solution)/shard_map/ppermute | solution.py:48
  132.1 2.7 %collective-permute-start.23 = (s16[208,128]{1,0:T(8,128)(2,1)S(1)}, s16[208,128]{1,0:T(8,128)(2,1)S(1)}, u32[]{:S(2)}, u32[]{:S(2)}) collective-permute-start(s16[208,128]{1,0:T(8,128)(2,1)S(1)} %get-tuple-element.57), channel_id=1, source_target_pairs={{0,8},{1,9},{2,10},{3,11},{4,12},{5,13},{6,14},{7,15},{8,0},{9,1},... | collective-permute-start | bytes 159752 | tf_op jit(solution)/shard_map/ppermute | solution.py:48
  134.9 1.4 %collective-permute-start.24 = (s16[208,128]{1,0:T(8,128)(2,1)S(1)}, s16[208,128]{1,0:T(8,128)(2,1)S(1)}, u32[]{:S(2)}, u32[]{:S(2)}) collective-permute-start(s16[208,128]{1,0:T(8,128)(2,1)S(1)} %get-tuple-element.58), channel_id=1, source_target_pairs={{0,12},{1,13},{2,14},{3,15},{4,0},{5,1},{6,2},{7,3},{8,4},{9,5},{1... | collective-permute-start | bytes 159752 | tf_op jit(solution)/shard_map/ppermute | solution.py:48
  136.3 1.5 %collective-permute-done.23.rb = s16[208,128]{1,0:T(8,128)(2,1)S(1)} collective-permute-done((s16[208,128]{1,0:T(8,128)(2,1)S(1)}, s16[208,128]{1,0:T(8,128)(2,1)S(1)}, u32[]{:S(2)}, u32[]{:S(2)}) %collective-permute-start.23) | collective-permute-done | bytes 53280 | tf_op jit(solution)/shard_map/ppermute | solution.py:48
  (41 shorter events, 15.5 us)
Async XLA Ops:
  0.8 1.7 %copy-start = (bf16[16,24,3072]{2,1,0:T(8,128)(2,1)S(1)}, bf16[16,24,3072]{2,1,0:T(8,128)(2,1)}, u32[]{:S(2)}) copy-start(bf16[16,24,3072]{2,1,0:T(8,128)(2,1)} %half.1) | copy-start | bytes 7077892
  2.5 0.7 copy-start.1
  5.2 18.1 %collective-permute-start.1 = (bf16[6,16,3200]{2,1,0:T(8,128)(2,1)S(1)}, bf16[6,16,3200]{2,1,0:T(8,128)(2,1)S(1)}, u32[]{:S(2)}, u32[]{:S(2)}) collective-permute-start(bf16[6,16,3200]{2,1,0:T(8,128)(2,1)S(1)} %get-tuple-element.33), channel_id=1, source_target_pairs={{0,32},{1,33},{2,34},{3,35},{4,36},{5,37},{6,38},{7,39},{8,40},{9,... | collective-permute-start | bytes 1843208 | tf_op jit(solution)/shard_map/ppermute | solution.py:48
  7.3 30.3 %collective-permute-start.3 = (bf16[6,16,3200]{2,1,0:T(8,128)(2,1)S(1)}, bf16[6,16,3200]{2,1,0:T(8,128)(2,1)S(1)}, u32[]{:S(2)}, u32[]{:S(2)}) collective-permute-start(bf16[6,16,3200]{2,1,0:T(8,128)(2,1)S(1)} %get-tuple-element.34), channel_id=1, source_target_pairs={{0,64},{1,65},{2,66},{3,67},{4,68},{5,69},{6,70},{7,71},{8,72},{9,... | collective-permute-start | bytes 1843208 | tf_op jit(solution)/shard_map/ppermute | solution.py:48
  10.9 26.7 %collective-permute-start.5 = (bf16[6,16,3200]{2,1,0:T(8,128)(2,1)S(1)}, bf16[6,16,3200]{2,1,0:T(8,128)(2,1)S(1)}, u32[]{:S(2)}, u32[]{:S(2)}) collective-permute-start(bf16[6,16,3200]{2,1,0:T(8,128)(2,1)S(1)} %get-tuple-element.35), channel_id=1, source_target_pairs={{0,96},{1,97},{2,98},{3,99},{4,100},{5,101},{6,102},{7,103},{8,104... | collective-permute-start | bytes 1843208 | tf_op jit(solution)/shard_map/ppermute | solution.py:48
  11.9 26.2 %collective-permute-start = (bf16[6,16,3200]{2,1,0:T(8,128)(2,1)S(1)}, bf16[6,16,3200]{2,1,0:T(8,128)(2,1)S(1)}, u32[]{:S(2)}, u32[]{:S(2)}) collective-permute-start(bf16[6,16,3200]{2,1,0:T(8,128)(2,1)S(1)} %get-tuple-element.32.refs_0_), channel_id=1, source_target_pairs={{0,16},{1,17},{2,18},{3,19},{4,20},{5,21},{6,22},{7,23},{8,24},{9,... | collective-permute-start | bytes 1843208 | tf_op jit(solution)/shard_map/ppermute | solution.py:48
  23.3 14.9 %collective-permute-start.2 = (bf16[6,16,3200]{2,1,0:T(8,128)(2,1)S(1)}, bf16[6,16,3200]{2,1,0:T(8,128)(2,1)S(1)}, u32[]{:S(2)}, u32[]{:S(2)}) collective-permute-start(bf16[6,16,3200]{2,1,0:T(8,128)(2,1)S(1)} %collective-permute-done.1.refs_2_), channel_id=1, source_target_pairs={{0,16},{1,17},{2,18},{3,19},{4,20},{5,21},{6,22},{7,23},{8,24},{9,... | collective-permute-start | bytes 1843208 | tf_op jit(solution)/shard_map/ppermute | solution.py:48
  37.6 2.0 %collective-permute-start.4 = (bf16[6,16,3200]{2,1,0:T(8,128)(2,1)S(1)}, bf16[6,16,3200]{2,1,0:T(8,128)(2,1)S(1)}, u32[]{:S(2)}, u32[]{:S(2)}) collective-permute-start(bf16[6,16,3200]{2,1,0:T(8,128)(2,1)S(1)} %collective-permute-done.3.refs_4_), channel_id=1, source_target_pairs={{0,16},{1,17},{2,18},{3,19},{4,20},{5,21},{6,22},{7,23},{8,24},{9,... | collective-permute-start | bytes 1843208 | tf_op jit(solution)/shard_map/ppermute | solution.py:48
  37.6 2.9 %collective-permute-start.6 = (bf16[6,16,3200]{2,1,0:T(8,128)(2,1)S(1)}, bf16[6,16,3200]{2,1,0:T(8,128)(2,1)S(1)}, u32[]{:S(2)}, u32[]{:S(2)}) collective-permute-start(bf16[6,16,3200]{2,1,0:T(8,128)(2,1)S(1)} %collective-permute-done.5.refs_6_), channel_id=1, source_target_pairs={{0,16},{1,17},{2,18},{3,19},{4,20},{5,21},{6,22},{7,23},{8,24},{9,... | collective-permute-start | bytes 1843208 | tf_op jit(solution)/shard_map/ppermute | solution.py:48
  51.4 20.0 %collective-permute-start.18 = (s16[3136,128]{1,0:T(8,128)(2,1)S(1)}, s16[3136,128]{1,0:T(8,128)(2,1)S(1)}, u32[]{:S(2)}, u32[]{:S(2)}) collective-permute-start(s16[3136,128]{1,0:T(8,128)(2,1)S(1)} %get-tuple-element.50), channel_id=1, source_target_pairs={{0,96},{1,97},{2,98},{3,99},{4,100},{5,101},{6,102},{7,103},{8,104... | collective-permute-start | bytes 2408456 | tf_op jit(solution)/shard_map/ppermute | solution.py:48
  55.2 48.0 %collective-permute-start.9 = (s16[784,1024]{1,0:T(8,128)(2,1)S(1)}, s16[784,1024]{1,0:T(8,128)(2,1)S(1)}, u32[]{:S(2)}, u32[]{:S(2)}) collective-permute-start(s16[784,1024]{1,0:T(8,128)(2,1)S(1)} %shard_map.42), channel_id=1, source_target_pairs={{0,12},{1,13},{2,14},{3,15},{4,0},{5,1},{6,2},{7,3},{8,4},{9,5},{1... | collective-permute-start | bytes 4816904 | tf_op jit(solution)/shard_map/ppermute | solution.py:48
  58.0 45.2 %collective-permute-start.8 = (s16[784,1024]{1,0:T(8,128)(2,1)S(1)}, s16[784,1024]{1,0:T(8,128)(2,1)S(1)}, u32[]{:S(2)}, u32[]{:S(2)}) collective-permute-start(s16[784,1024]{1,0:T(8,128)(2,1)S(1)} %shard_map.41), channel_id=1, source_target_pairs={{0,8},{1,9},{2,10},{3,11},{4,12},{5,13},{6,14},{7,15},{8,0},{9,1},... | collective-permute-start | bytes 4816904 | tf_op jit(solution)/shard_map/ppermute | solution.py:48
  58.8 44.4 %collective-permute-start.7 = (s16[784,1024]{1,0:T(8,128)(2,1)S(1)}, s16[784,1024]{1,0:T(8,128)(2,1)S(1)}, u32[]{:S(2)}, u32[]{:S(2)}) collective-permute-start(s16[784,1024]{1,0:T(8,128)(2,1)S(1)} %shard_map.40), channel_id=1, source_target_pairs={{0,4},{1,5},{2,6},{3,7},{4,8},{5,9},{6,10},{7,11},{8,12},{9,13},{1... | collective-permute-start | bytes 4816904 | tf_op jit(solution)/shard_map/ppermute | solution.py:48
  62.2 37.5 %collective-permute-start.16 = (s16[3136,128]{1,0:T(8,128)(2,1)S(1)}, s16[3136,128]{1,0:T(8,128)(2,1)S(1)}, u32[]{:S(2)}, u32[]{:S(2)}) collective-permute-start(s16[3136,128]{1,0:T(8,128)(2,1)S(1)} %get-tuple-element.48), channel_id=1, source_target_pairs={{0,32},{1,33},{2,34},{3,35},{4,36},{5,37},{6,38},{7,39},{8,40},{9,... | collective-permute-start | bytes 2408456 | tf_op jit(solution)/shard_map/ppermute | solution.py:48
  71.4 28.3 %collective-permute-start.17 = (s16[3136,128]{1,0:T(8,128)(2,1)S(1)}, s16[3136,128]{1,0:T(8,128)(2,1)S(1)}, u32[]{:S(2)}, u32[]{:S(2)}) collective-permute-start(s16[3136,128]{1,0:T(8,128)(2,1)S(1)} %get-tuple-element.49), channel_id=1, source_target_pairs={{0,64},{1,65},{2,66},{3,67},{4,68},{5,69},{6,70},{7,71},{8,72},{9,... | collective-permute-start | bytes 2408456 | tf_op jit(solution)/shard_map/ppermute | solution.py:48
  101.0 10.7 %collective-permute-start.19 = (s16[208,512]{1,0:T(8,128)(2,1)S(1)}, s16[208,512]{1,0:T(8,128)(2,1)S(1)}, u32[]{:S(2)}, u32[]{:S(2)}) collective-permute-start(s16[208,512]{1,0:T(8,128)(2,1)S(1)} %get-tuple-element.52), channel_id=1, source_target_pairs={{0,1},{1,2},{2,3},{3,0},{4,5},{5,6},{6,7},{7,4},{8,9},{9,10},{10,1... | collective-permute-start | bytes 638984 | tf_op jit(solution)/shard_map/ppermute | solution.py:48
  105.5 21.8 %collective-permute-start.10 = (s16[208,1024]{1,0:T(8,128)(2,1)S(1)}, s16[208,1024]{1,0:T(8,128)(2,1)S(1)}, u32[]{:S(2)}, u32[]{:S(2)}) collective-permute-start(s16[208,1024]{1,0:T(8,128)(2,1)S(1)} %get-tuple-element.39), channel_id=1, source_target_pairs={{0,1},{1,2},{2,3},{3,0},{4,5},{5,6},{6,7},{7,4},{8,9},{9,10},{10,1... | collective-permute-start | bytes 1277960 | tf_op jit(solution)/shard_map/ppermute | solution.py:48
  105.9 21.5 %collective-permute-start.11 = (s16[208,1024]{1,0:T(8,128)(2,1)S(1)}, s16[208,1024]{1,0:T(8,128)(2,1)S(1)}, u32[]{:S(2)}, u32[]{:S(2)}) collective-permute-start(s16[208,1024]{1,0:T(8,128)(2,1)S(1)} %get-tuple-element.40), channel_id=1, source_target_pairs={{0,2},{1,3},{2,0},{3,1},{4,6},{5,7},{6,4},{7,5},{8,10},{9,11},{10,... | collective-permute-start | bytes 1277960 | tf_op jit(solution)/shard_map/ppermute | solution.py:48
  108.4 19.0 %collective-permute-start.12 = (s16[208,1024]{1,0:T(8,128)(2,1)S(1)}, s16[208,1024]{1,0:T(8,128)(2,1)S(1)}, u32[]{:S(2)}, u32[]{:S(2)}) collective-permute-start(s16[208,1024]{1,0:T(8,128)(2,1)S(1)} %get-tuple-element.41), channel_id=1, source_target_pairs={{0,3},{1,0},{2,1},{3,2},{4,7},{5,4},{6,5},{7,6},{8,11},{9,8},{10,9... | collective-permute-start | bytes 1277960 | tf_op jit(solution)/shard_map/ppermute | solution.py:48
  110.1 11.4 %collective-permute-start.20 = (s16[208,512]{1,0:T(8,128)(2,1)S(1)}, s16[208,512]{1,0:T(8,128)(2,1)S(1)}, u32[]{:S(2)}, u32[]{:S(2)}) collective-permute-start(s16[208,512]{1,0:T(8,128)(2,1)S(1)} %get-tuple-element.53), channel_id=1, source_target_pairs={{0,2},{1,3},{2,0},{3,1},{4,6},{5,7},{6,4},{7,5},{8,10},{9,11},{10,... | collective-permute-start | bytes 638984 | tf_op jit(solution)/shard_map/ppermute | solution.py:48
  111.8 13.2 %collective-permute-start.21 = (s16[208,512]{1,0:T(8,128)(2,1)S(1)}, s16[208,512]{1,0:T(8,128)(2,1)S(1)}, u32[]{:S(2)}, u32[]{:S(2)}) collective-permute-start(s16[208,512]{1,0:T(8,128)(2,1)S(1)} %get-tuple-element.54), channel_id=1, source_target_pairs={{0,3},{1,0},{2,1},{3,2},{4,7},{5,4},{6,5},{7,6},{8,11},{9,8},{10,9... | collective-permute-start | bytes 638984 | tf_op jit(solution)/shard_map/ppermute | solution.py:48
  125.8 9.1 %collective-permute-start.22 = (s16[208,128]{1,0:T(8,128)(2,1)S(1)}, s16[208,128]{1,0:T(8,128)(2,1)S(1)}, u32[]{:S(2)}, u32[]{:S(2)}) collective-permute-start(s16[208,128]{1,0:T(8,128)(2,1)S(1)} %get-tuple-element.56), channel_id=1, source_target_pairs={{0,4},{1,5},{2,6},{3,7},{4,8},{5,9},{6,10},{7,11},{8,12},{9,13},{1... | collective-permute-start | bytes 159752 | tf_op jit(solution)/shard_map/ppermute | solution.py:48
  128.4 10.6 %collective-permute-start.13 = (s16[208,256]{1,0:T(8,128)(2,1)S(1)}, s16[208,256]{1,0:T(8,128)(2,1)S(1)}, u32[]{:S(2)}, u32[]{:S(2)}) collective-permute-start(s16[208,256]{1,0:T(8,128)(2,1)S(1)} %get-tuple-element.43), channel_id=1, source_target_pairs={{0,32},{1,33},{2,34},{3,35},{4,36},{5,37},{6,38},{7,39},{8,40},{9,... | collective-permute-start | bytes 319496 | tf_op jit(solution)/shard_map/ppermute | solution.py:48
  128.5 10.5 %collective-permute-start.14 = (s16[208,256]{1,0:T(8,128)(2,1)S(1)}, s16[208,256]{1,0:T(8,128)(2,1)S(1)}, u32[]{:S(2)}, u32[]{:S(2)}) collective-permute-start(s16[208,256]{1,0:T(8,128)(2,1)S(1)} %get-tuple-element.44), channel_id=1, source_target_pairs={{0,64},{1,65},{2,66},{3,67},{4,68},{5,69},{6,70},{7,71},{8,72},{9,... | collective-permute-start | bytes 319496 | tf_op jit(solution)/shard_map/ppermute | solution.py:48
  129.6 9.4 %collective-permute-start.15 = (s16[208,256]{1,0:T(8,128)(2,1)S(1)}, s16[208,256]{1,0:T(8,128)(2,1)S(1)}, u32[]{:S(2)}, u32[]{:S(2)}) collective-permute-start(s16[208,256]{1,0:T(8,128)(2,1)S(1)} %get-tuple-element.45), channel_id=1, source_target_pairs={{0,96},{1,97},{2,98},{3,99},{4,100},{5,101},{6,102},{7,103},{8,104... | collective-permute-start | bytes 319496 | tf_op jit(solution)/shard_map/ppermute | solution.py:48
  132.1 5.6 %collective-permute-start.23 = (s16[208,128]{1,0:T(8,128)(2,1)S(1)}, s16[208,128]{1,0:T(8,128)(2,1)S(1)}, u32[]{:S(2)}, u32[]{:S(2)}) collective-permute-start(s16[208,128]{1,0:T(8,128)(2,1)S(1)} %get-tuple-element.57), channel_id=1, source_target_pairs={{0,8},{1,9},{2,10},{3,11},{4,12},{5,13},{6,14},{7,15},{8,0},{9,1},... | collective-permute-start | bytes 159752 | tf_op jit(solution)/shard_map/ppermute | solution.py:48
  134.9 4.1 %collective-permute-start.24 = (s16[208,128]{1,0:T(8,128)(2,1)S(1)}, s16[208,128]{1,0:T(8,128)(2,1)S(1)}, u32[]{:S(2)}, u32[]{:S(2)}) collective-permute-start(s16[208,128]{1,0:T(8,128)(2,1)S(1)} %get-tuple-element.58), channel_id=1, source_target_pairs={{0,12},{1,13},{2,14},{3,15},{4,0},{5,1},{6,2},{7,3},{8,4},{9,5},{1... | collective-permute-start | bytes 159752 | tf_op jit(solution)/shard_map/ppermute | solution.py:48

commit v4 on v3

--- a/solution.py
+++ b/solution.py
@@ -27,6 +27,10 @@
     return pl.BlockSpec(memory_space=pltpu.SMEM)
 
 
+def position():
+    return [lax.axis_index(a) for a in AXES]
+
+
 def params(mib):
     return pltpu.CompilerParams(vmem_limit_bytes=mib * MIB)
 
@@ -64,40 +68,61 @@
     return lambda z, c, x, y: (z, c, x, y + k) if c == 0 else (z, c, x + k, y)
 
 
-def screen_body(at, half, gate, metric, *outs_and_scratch):
-    outs, turned = outs_and_scratch[:4], outs_and_scratch[4]
-    lanes = 512
-
-    def step(n, carry):
-        cut = pl.ds(pl.multiple_of(n * lanes, lanes), lanes)
-        kept = half[:, :, cut] * gate[:, cut][None]
-        turned[:, :, cut] = jnp.swapaxes(kept.astype(F32), 0, 1).astype(BF)
-        return carry
-
+def screen_body(survive, half, metric, *rest):
+    outs, (held, own, turned, sems) = rest[:4], rest[4:]
+    at = position()
     ao = half.shape[2]
-    lax.fori_loop(0, ao // lanes, step, 0)
+    block = ao // survive.shape[2]
+    chunks = sems.shape[0] - 1
+    lanes = ao // chunks
+    copies = [
+        pltpu.make_async_copy(half.at[:, :, cut], held.at[:, :, cut], sems.at[n])
+        for n, cut in enumerate(slice(n * lanes, (n + 1) * lanes) for n in range(chunks))
+    ] + [pltpu.make_async_copy(metric, own, sems.at[chunks])]
+    for copy in copies:
+        copy.start()
+    for n in range(chunks):
+        copies[n].wait()
+
+        def step(m, carry):
+            m = n * (lanes // block) + m
+            cut = pl.ds(pl.multiple_of(m * block, block), block)
+            keep = survive[0, 0, m].astype(F32)
+            turned[:, :, cut] = jnp.swapaxes(held[:, :, cut].astype(F32) * keep, 0, 1).astype(BF)
+            return carry
+
+        lax.fori_loop(0, lanes // block, step, 0, unroll=True)
+    copies[chunks].wait()
     group = outs[0].shape[0]
     for k in range(RING):
         first = lax.rem(at[0] + k, RING) * group
         outs[k][:, :, :ao] = turned[pl.ds(first, group)]
-        outs[k][:, :, ao:] = jnp.broadcast_to(metric[...][None], (group,) + metric.shape)
-
-
-def screen(at, half, gate, metric):
+        outs[k][:, :, ao:] = jnp.broadcast_to(own[...][None], (group,) + metric.shape)
+
+
+def screen(survive, half, metric):
     aux, occ, ao = half.shape
     out = jax.ShapeDtypeStruct((occ // RING, aux, ao + metric.shape[1]), BF)
+    in_hbm = pl.BlockSpec(memory_space=pltpu.HBM)
     return pl.pallas_call(
         screen_body,
         out_shape=[out] * RING,
-        in_specs=[scalars(), whole(), whole(), whole()],
+        in_specs=[scalars(), in_hbm, in_hbm],
         out_specs=[whole()] * RING,
-        scratch_shapes=[pltpu.VMEM((occ, aux, ao), BF)],
-        compiler_params=params(16),
+        scratch_shapes=[
+            pltpu.VMEM(half.shape, BF),
+            pltpu.VMEM(metric.shape, BF),
+            pltpu.VMEM((occ, aux, ao), BF),
+            pltpu.SemaphoreType.DMA((5,)),
+        ],
+        compiler_params=params(50),
         cost_estimate=cost(half.size, half.size * 4),
-    )(at, half, gate, metric)
-
-
-def fit_body(at, *refs):
+        name="screen",
+    )(survive, half, metric)
+
+
+def fit_body(*refs):
+    at = position()
     pieces, (bulk, rest, turned, mixed, fresh) = refs[:8], refs[8:]
     step = pl.program_id(0)
     ao = fresh.shape[1]
@@ -135,7 +160,7 @@
             turned[pl.ds(pl.multiple_of(to, 64), high), cut] = flipped[n * high:(n + 1) * high]
 
 
-def fit(at, pieces):
+def fit(pieces):
     group, part, wide = pieces[0].shape
     aux = part * 8
     ao = wide - aux
@@ -145,13 +170,13 @@
         grid=(group,),
         out_shape=[jax.ShapeDtypeStruct((group * aux, n), BF) for n in (ao // 3, ao // 6)]
         + [jax.ShapeDtypeStruct((ao, group * aux), BF)],
-        in_specs=[scalars()] + [piece] * 8,
+        in_specs=[piece] * 8,
         out_specs=[pl.BlockSpec((aux, n), lambda i: (i, 0)) for n in (ao // 3, ao // 6)]
         + [pl.BlockSpec((ao, group * aux), lambda i: (0, 0))],
         scratch_shapes=[pltpu.VMEM((aux, aux), BF), pltpu.VMEM((aux, ao), BF)],
         compiler_params=params(28),
         cost_estimate=cost(2 * group * aux * aux * ao, group * aux * ao * 6),
-    )(at, *pieces)
+    )(*pieces)
 
 
 def exponent(top):
@@ -184,7 +209,8 @@
         out[end:end + TAIL, :] = marked(e)
 
 
-def bulk_body(shift, at, bulk, turned, out):
+def bulk_body(shift, bulk, turned, out):
+    at = position()
     total = turned.shape[0] // RING
     g = lax.rem(jnp.where(at[1] == 0, at[2], at[3]) + shift, RING)
     left = turned[pl.ds(pl.multiple_of(g * total, 256), total), :]
@@ -194,18 +220,18 @@
         write(out.at[:, lanes], 0, jnp.dot(left, bulk[:, lanes], preferred_element_type=F32))
 
 
-def bulk_k(at, bulk, turned, shift):
+def bulk_k(bulk, turned, shift):
     depth, columns = bulk.shape
     total = turned.shape[0] // RING
     shape = (total + (TAIL if shift else 0), columns)
     return pl.pallas_call(
         functools.partial(bulk_body, shift),
         out_shape=jax.ShapeDtypeStruct(shape, I16 if shift else F32),
-        in_specs=[scalars(), whole(), whole()],
+        in_specs=[whole(), whole()],
         out_specs=whole(),
         compiler_params=params(28),
         cost_estimate=cost(2 * depth * total * columns, total * columns * 2),
-    )(at, bulk, turned)
+    )(bulk, turned)
 
 
 def rest_body(rest, turned, *outs):
@@ -242,7 +268,8 @@
     return v
 
 
-def second_body(groups, at, own, a, b, d, kept, *outs):
+def second_body(groups, own, a, b, d, after, kept, *outs):
+    at = position()
     high = kept.shape[0]
     total = own.shape[0] // groups
     h = jnp.where(at[1] == 0, at[3], at[2])
@@ -260,22 +287,23 @@
                 write(out.at[:, to:to + step], 0, v)
 
 
-def second(at, parts, groups):
+def second(parts, groups, after):
     total, columns = parts[0].shape
     high, every = total // groups // RING, columns * groups
     return list(pl.pallas_call(
         functools.partial(second_body, groups),
         out_shape=[jax.ShapeDtypeStruct((high, every), F32)]
         + [jax.ShapeDtypeStruct((high + TAIL, every), I16)] * 3,
-        in_specs=[scalars()] + [whole()] * 4,
+        in_specs=[whole()] * 5,
         out_specs=[whole()] * 4,
         compiler_params=params(24),
         cost_estimate=cost(total * columns * 16, total * columns * 10),
         name="second_sum",
-    )(at, *parts))
-
-
-def third_body(by_z, at, own, a, b, d, *outs):
+    )(*parts, after))
+
+
+def third_body(by_z, own, a, b, d, after, *outs):
+    at = position()
     high, step = outs[0].shape
     start = at[0] if by_z else jnp.where(at[1] == 0, at[2], at[3])
     for k in range(RING):
@@ -283,35 +311,34 @@
         write(outs[k], 0, gathered(own, (a, b, d), (0, 0, high), high, 0, cut))
 
 
-def third(at, parts, by_z):
+def third(parts, by_z, after):
     high, every = parts[0].shape
     wide = every // RING
     return list(pl.pallas_call(
         functools.partial(third_body, by_z),
         out_shape=[jax.ShapeDtypeStruct((high, wide), F32)] + [jax.ShapeDtypeStruct((high + TAIL, wide), I16)] * 3,
-        in_specs=[scalars()] + [whole()] * 4,
+        in_specs=[whole()] * 5,
         out_specs=[whole()] * 4,
         compiler_params=params(16),
         cost_estimate=cost(high * every * 16, high * every * 10),
         name="third_sum",
-    )(at, *parts))
-
-
-def tick_body(at, out):
-    for n in range(RING):
-        out[n] = at[n]
-
-
-def tick(at):
+    )(*parts, after))
+
+
+def tick_body(v, out):
+    out[...] = v[...]
+
+
+def tick(v):
     return pl.pallas_call(
         tick_body,
-        out_shape=jax.ShapeDtypeStruct(at.shape, at.dtype),
-        in_specs=[scalars()],
-        out_specs=scalars(),
+        out_shape=jax.ShapeDtypeStruct(v.shape, v.dtype),
+        in_specs=[whole()],
+        out_specs=whole(),
         compiler_params=params(1),
         cost_estimate=cost(1000, 32),
         name="tick",
-    )(at)
+    )(v)
 
 
 def finish_body(own, a, b, d, rest, ra, rb, rd, out):
@@ -336,22 +363,17 @@
 
 
 def shards(half, metric, survive):
-    _, _, ao = half.shape
-    at = jnp.stack([lax.axis_index(a) for a in AXES]).astype(jnp.int32)
-    blocks = survive.shape[2]
-    gate = jnp.repeat(survive.reshape(1, blocks).astype(BF), ao // blocks, axis=1)
-
-    parts = screen(at, half, gate, metric)
+    parts = screen(survive, half, metric)
     here = [parts[0]] + [None] * 3
     for k in (2, 1, 3):
         here[k] = send(parts[k], along_z(k))
     there = [send(v, other_core) for v in here]
-    bulk_rows, rest_rows, turned = fit(at, [v for pair in zip(here, there) for v in pair])
+    bulk_rows, rest_rows, turned = fit([v for pair in zip(here, there) for v in pair])
 
     bulk, rest = [None] * 4, [None] * 4
 
     def bulk_step(k):
-        bulk[k] = bulk_k(at, bulk_rows, turned, k)
+        bulk[k] = bulk_k(bulk_rows, turned, k)
         if k:
             bulk[k] = send(bulk[k], first_axis(k))
 
@@ -370,15 +392,15 @@
     bulk_step(1)
     bulk_step(3)
     bulk_step(0)
-    rest = second(at, rest, RING)
+    rest = second(rest, RING, metric)
     onward(rest, second_axis)
-    then = tick(at)
-    bulk = second(then, bulk, 1)
+    then = tick(metric)
+    bulk = second(bulk, 1, then)
     onward(bulk, second_axis)
-    rest = third(at, rest, False)
+    rest = third(rest, False, metric)
     onward(rest, first_axis)
     then = tick(then)
-    bulk = third(then, bulk, True)
+    bulk = third(bulk, True, then)
     onward(bulk, along_z)
     return finish(bulk, rest)
 

time: 140 us -> 135 us (0.964)
  Pallas kernels: 28.3 us -> 22.7 us
  waiting for transfers between devices: 73.8 us -> 76.7 us
    ppermute x25, waiting for transfers between devices: 73.8 us -> 76.7 us  [send(): return lax.ppermute(v, AXES, moves(shift))]
    pallas_call x2, Pallas kernels: 2.27 us -> 0.01 us  [tick(): pl.pallas_call(tick_body, out_shape=jax.ShapeDtypeStruct(v.shape, v.dtype...]
    pallas_call x4, Pallas kernels: 9.28 us -> 7.07 us  [bulk_k(): pl.pallas_call(functools.partial(bulk_body, shift), out_shape=jax.ShapeDt...]
  transfers between devices with their start and end apart: 25 -> 25, of which waited for: 10 -> 10; matrix products, arithmetic and copies ran while one was open for 0% -> 0% of each run, Pallas kernels for 10% -> 7%
where the time goes in v4:
time: 135 us
  waiting for transfers between devices  76.7 us (57%)
  starting transfers between devices  34.2 us (25%)
  Pallas kernels  22.7 us (17%)
  local copies, waits for them, and re-layouts  1.35 us (1%)
    ppermute x25, waiting for transfers between devices, send(): return lax.ppermute(v, AXES, moves(shift))  76.7 us
    ppermute x25, starting transfers between devices, send(): return lax.ppermute(v, AXES, moves(shift))  34.2 us
    pallas_call x4, Pallas kernels, bulk_k(): pl.pallas_call(functools.partial(bulk_body, shift), out_shape=jax.ShapeDt...  7.07 us
    pallas_call x2, Pallas kernels, rest_k(): pl.pallas_call(rest_body, grid=(RING,), out_shape=[jax.ShapeDtypeStruct((...  4.72 us
    pallas_call x1, Pallas kernels, fit(): pl.pallas_call(fit_body, grid=(group,), out_shape=[jax.ShapeDtypeStruct((...  3.56 us
    pallas_call x1, Pallas kernels, screen(): pl.pallas_call(screen_body, out_shape=[out] * RING, in_specs=[scalars(),...  3.07 us
  transfers between devices with their start and end apart: 25, of which 10 were waited for; matrix products, arithmetic and copies ran while one was open for 0% of the time, Pallas kernels for 7%

profile of v4, /device:TPU:0, one launch (start us, length us, event | category | flops | bytes accessed | tf_op | source)
XLA Modules:
  0.0 135.0 jit_solution(16712338795976564709)
XLA Ops:
  1.3 3.1 %screen.1 = (bf16[6,16,3200]{2,1,0:T(8,128)(2,1)S(1)}, bf16[6,16,3200]{2,1,0:T(8,128)(2,1)S(1)}, bf16[6,16,3200]{2,1,0:T(8,128)(2,1)S(1)}, bf16[6,16,3200]{2,1,0:T(8,128)(2,1)S(1)}) custom-call(s32[1,1,24]{2,1,0:T(1,128)S(1)} %copy-done.2, bf16[16,24,3072]{2,1,0:T(8,128)(2,1)} %half.1, bf16[16,128]{1,0:T(8,128)(2,1)S(1)} %copy-done), custom_call_target="tpu_custom_call" | custom-call | flops 1179648 | bytes 4718592 | tf_op jit(solution)/shard_map/screen/pallas_call | solution.py:107
  4.4 2.1 %collective-permute-start.1 = (bf16[6,16,3200]{2,1,0:T(8,128)(2,1)S(1)}, bf16[6,16,3200]{2,1,0:T(8,128)(2,1)S(1)}, u32[]{:S(2)}, u32[]{:S(2)}) collective-permute-start(bf16[6,16,3200]{2,1,0:T(8,128)(2,1)S(1)} %get-tuple-element.33), channel_id=1, source_target_pairs={{0,32},{1,33},{2,34},{3,35},{4,36},{5,37},{6,38},{7,39},{8,40},{9,... | collective-permute-start | bytes 1843208 | tf_op jit(solution)/shard_map/ppermute | solution.py:52
  6.5 3.6 %collective-permute-start.3 = (bf16[6,16,3200]{2,1,0:T(8,128)(2,1)S(1)}, bf16[6,16,3200]{2,1,0:T(8,128)(2,1)S(1)}, u32[]{:S(2)}, u32[]{:S(2)}) collective-permute-start(bf16[6,16,3200]{2,1,0:T(8,128)(2,1)S(1)} %get-tuple-element.34), channel_id=1, source_target_pairs={{0,64},{1,65},{2,66},{3,67},{4,68},{5,69},{6,70},{7,71},{8,72},{9,... | collective-permute-start | bytes 1843208 | tf_op jit(solution)/shard_map/ppermute | solution.py:52
  11.1 11.4 %collective-permute-done.1.refs_2_ = bf16[6,16,3200]{2,1,0:T(8,128)(2,1)S(1)} collective-permute-done((bf16[6,16,3200]{2,1,0:T(8,128)(2,1)S(1)}, bf16[6,16,3200]{2,1,0:T(8,128)(2,1)S(1)}, u32[]{:S(2)}, u32[]{:S(2)}) %collective-permute-start.1) | collective-permute-done | bytes 614432 | tf_op jit(solution)/shard_map/ppermute | solution.py:52
  22.5 14.3 %collective-permute-done.3.refs_4_ = bf16[6,16,3200]{2,1,0:T(8,128)(2,1)S(1)} collective-permute-done((bf16[6,16,3200]{2,1,0:T(8,128)(2,1)S(1)}, bf16[6,16,3200]{2,1,0:T(8,128)(2,1)S(1)}, u32[]{:S(2)}, u32[]{:S(2)}) %collective-permute-start.3) | collective-permute-done | bytes 614432 | tf_op jit(solution)/shard_map/ppermute | solution.py:52
  37.4 1.5 %collective-permute-done.4.refs_5_ = bf16[6,16,3200]{2,1,0:T(8,128)(2,1)S(1)} collective-permute-done((bf16[6,16,3200]{2,1,0:T(8,128)(2,1)S(1)}, bf16[6,16,3200]{2,1,0:T(8,128)(2,1)S(1)}, u32[]{:S(2)}, u32[]{:S(2)}) %collective-permute-start.4) | collective-permute-done | bytes 614432 | tf_op jit(solution)/shard_map/ppermute | solution.py:52
  39.8 3.6 %shard_map.37 = (bf16[768,1024]{1,0:T(8,128)(2,1)S(1)}, bf16[768,512]{1,0:T(8,128)(2,1)S(1)}, bf16[3072,768]{1,0:T(8,128)(2,1)S(1)}) custom-call(bf16[6,16,3200]{2,1,0:T(8,128)(2,1)S(1)} %get-tuple-element.32.refs_0_, bf16[6,16,3200]{2,1,0:T(8,128)(2,1)S(1)} %collective-permute-done.refs_1_, bf16[6,16,3200]{2,1,0:T(8,128)(2,1)S(1)} %collective-permute-done.1.refs_2_, ...), custom_call_target="tpu_custom_call" | custom-call | flops 603979776 | bytes 14155776 | tf_op jit(solution)/shard_map/pallas_call | solution.py:168
  43.3 1.9 %shard_map.41 = s16[784,1024]{1,0:T(8,128)(2,1)S(1)} custom-call(bf16[768,1024]{1,0:T(8,128)(2,1)S(1)} %get-tuple-element.36.bulk, bf16[3072,768]{1,0:T(8,128)(2,1)S(1)} %get-tuple-element.37.turned), custom_call_target="tpu_custom_call" | custom-call | flops 1207959552 | bytes 1572864 | tf_op jit(solution)/shard_map/pallas_call | solution.py:227
  45.2 1.9 %shard_map.40 = s16[784,1024]{1,0:T(8,128)(2,1)S(1)} custom-call(bf16[768,1024]{1,0:T(8,128)(2,1)S(1)} %get-tuple-element.36.bulk, bf16[3072,768]{1,0:T(8,128)(2,1)S(1)} %get-tuple-element.37.turned), custom_call_target="tpu_custom_call" | custom-call | flops 1207959552 | bytes 1572864 | tf_op jit(solution)/shard_map/pallas_call | solution.py:227
  47.1 2.3 %shard_map.42 = (s16[3136,128]{1,0:T(8,128)(2,1)S(1)}, f32[3072,128]{1,0:T(8,128)S(1)}) custom-call(bf16[768,512]{1,0:T(8,128)(2,1)S(1)} %get-tuple-element.46.rest, bf16[3072,768]{1,0:T(8,128)(2,1)S(1)} %get-tuple-element.37.turned), custom_call_target="tpu_custom_call" | custom-call | flops 1207959552 | bytes 1572864 | tf_op jit(solution)/shard_map/pallas_call | solution.py:249
  49.4 1.4 collective-permute-start.18
  50.8 1.9 %shard_map.39 = s16[784,1024]{1,0:T(8,128)(2,1)S(1)} custom-call(bf16[768,1024]{1,0:T(8,128)(2,1)S(1)} %get-tuple-element.36.bulk, bf16[3072,768]{1,0:T(8,128)(2,1)S(1)} %get-tuple-element.37.turned), custom_call_target="tpu_custom_call" | custom-call | flops 1207959552 | bytes 1572864 | tf_op jit(solution)/shard_map/pallas_call | solution.py:227
  52.7 2.8 %collective-permute-start.9 = (s16[784,1024]{1,0:T(8,128)(2,1)S(1)}, s16[784,1024]{1,0:T(8,128)(2,1)S(1)}, u32[]{:S(2)}, u32[]{:S(2)}) collective-permute-start(s16[784,1024]{1,0:T(8,128)(2,1)S(1)} %shard_map.41), channel_id=1, source_target_pairs={{0,12},{1,13},{2,14},{3,15},{4,0},{5,1},{6,2},{7,3},{8,4},{9,5},{1... | collective-permute-start | bytes 4816904 | tf_op jit(solution)/shard_map/ppermute | solution.py:52
  57.2 2.4 %shard_map.43 = (s16[3136,128]{1,0:T(8,128)(2,1)S(1)}, s16[3136,128]{1,0:T(8,128)(2,1)S(1)}) custom-call(bf16[768,512]{1,0:T(8,128)(2,1)S(1)} %get-tuple-element.46.rest, bf16[3072,768]{1,0:T(8,128)(2,1)S(1)} %get-tuple-element.37.turned), custom_call_target="tpu_custom_call" | custom-call | flops 1207959552 | bytes 1572864 | tf_op jit(solution)/shard_map/pallas_call | solution.py:249
  60.5 9.0 %collective-permute-done.18.d = s16[3136,128]{1,0:T(8,128)(2,1)S(1)} collective-permute-done((s16[3136,128]{1,0:T(8,128)(2,1)S(1)}, s16[3136,128]{1,0:T(8,128)(2,1)S(1)}, u32[]{:S(2)}, u32[]{:S(2)}) %collective-permute-start.18) | collective-permute-done | bytes 802848 | tf_op jit(solution)/shard_map/ppermute | solution.py:52
  69.4 1.4 %collective-permute-start.17 = (s16[3136,128]{1,0:T(8,128)(2,1)S(1)}, s16[3136,128]{1,0:T(8,128)(2,1)S(1)}, u32[]{:S(2)}, u32[]{:S(2)}) collective-permute-start(s16[3136,128]{1,0:T(8,128)(2,1)S(1)} %get-tuple-element.49), channel_id=1, source_target_pairs={{0,64},{1,65},{2,66},{3,67},{4,68},{5,69},{6,70},{7,71},{8,72},{9,... | collective-permute-start | bytes 2408456 | tf_op jit(solution)/shard_map/ppermute | solution.py:52
  70.8 1.4 %shard_map.38.own = f32[768,1024]{1,0:T(8,128)S(1)} custom-call(bf16[768,1024]{1,0:T(8,128)(2,1)S(1)} %get-tuple-element.36.bulk, bf16[3072,768]{1,0:T(8,128)(2,1)S(1)} %get-tuple-element.37.turned), custom_call_target="tpu_custom_call" | custom-call | flops 1207959552 | bytes 1572864 | tf_op jit(solution)/shard_map/pallas_call | solution.py:227
  72.2 24.9 %collective-permute-done.16.a = s16[3136,128]{1,0:T(8,128)(2,1)S(1)} collective-permute-done((s16[3136,128]{1,0:T(8,128)(2,1)S(1)}, s16[3136,128]{1,0:T(8,128)(2,1)S(1)}, u32[]{:S(2)}, u32[]{:S(2)}) %collective-permute-start.16) | collective-permute-done | bytes 802848 | tf_op jit(solution)/shard_map/ppermute | solution.py:52
  98.0 2.0 %collective-permute-start.19 = (s16[208,512]{1,0:T(8,128)(2,1)S(1)}, s16[208,512]{1,0:T(8,128)(2,1)S(1)}, u32[]{:S(2)}, u32[]{:S(2)}) collective-permute-start(s16[208,512]{1,0:T(8,128)(2,1)S(1)} %get-tuple-element.52), channel_id=1, source_target_pairs={{0,1},{1,2},{2,3},{3,0},{4,5},{5,6},{6,7},{7,4},{8,9},{9,10},{10,1... | collective-permute-start | bytes 638984 | tf_op jit(solution)/shard_map/ppermute | solution.py:52
  100.0 1.8 %second_sum.2 = (f32[192,1024]{1,0:T(8,128)S(1)}, s16[208,1024]{1,0:T(8,128)(2,1)S(1)}, s16[208,1024]{1,0:T(8,128)(2,1)S(1)}, s16[208,1024]{1,0:T(8,128)(2,1)S(1)}) custom-call(f32[768,1024]{1,0:T(8,128)S(1)} %shard_map.38.own, s16[784,1024]{1,0:T(8,128)(2,1)S(1)} %collective-permute-done.7.a, s16[784,1024]{1,0:T(8,128)(2,1)S(1)} %collective-permute-done.8.b, ...), custom_call_target="tpu_custom_call" | custom-call | flops 12582912 | bytes 7864320 | tf_op jit(solution)/shard_map/second_sum/pallas_call | solution.py:293
  102.2 2.5 %collective-permute-start.11 = (s16[208,1024]{1,0:T(8,128)(2,1)S(1)}, s16[208,1024]{1,0:T(8,128)(2,1)S(1)}, u32[]{:S(2)}, u32[]{:S(2)}) collective-permute-start(s16[208,1024]{1,0:T(8,128)(2,1)S(1)} %get-tuple-element.40), channel_id=1, source_target_pairs={{0,2},{1,3},{2,0},{3,1},{4,6},{5,7},{6,4},{7,5},{8,10},{9,11},{10,... | collective-permute-start | bytes 1277960 | tf_op jit(solution)/shard_map/ppermute | solution.py:52
  104.7 1.7 %collective-permute-start.12 = (s16[208,1024]{1,0:T(8,128)(2,1)S(1)}, s16[208,1024]{1,0:T(8,128)(2,1)S(1)}, u32[]{:S(2)}, u32[]{:S(2)}) collective-permute-start(s16[208,1024]{1,0:T(8,128)(2,1)S(1)} %get-tuple-element.41), channel_id=1, source_target_pairs={{0,3},{1,0},{2,1},{3,2},{4,7},{5,4},{6,5},{7,6},{8,11},{9,8},{10,9... | collective-permute-start | bytes 1277960 | tf_op jit(solution)/shard_map/ppermute | solution.py:52
  106.3 1.7 %collective-permute-start.20 = (s16[208,512]{1,0:T(8,128)(2,1)S(1)}, s16[208,512]{1,0:T(8,128)(2,1)S(1)}, u32[]{:S(2)}, u32[]{:S(2)}) collective-permute-start(s16[208,512]{1,0:T(8,128)(2,1)S(1)} %get-tuple-element.53), channel_id=1, source_target_pairs={{0,2},{1,3},{2,0},{3,1},{4,6},{5,7},{6,4},{7,5},{8,10},{9,11},{10,... | collective-permute-start | bytes 638984 | tf_op jit(solution)/shard_map/ppermute | solution.py:52
  108.0 1.3 collective-permute-start.21
  109.4 8.3 %collective-permute-done.20.b = s16[208,512]{1,0:T(8,128)(2,1)S(1)} collective-permute-done((s16[208,512]{1,0:T(8,128)(2,1)S(1)}, s16[208,512]{1,0:T(8,128)(2,1)S(1)}, u32[]{:S(2)}, u32[]{:S(2)}) %collective-permute-start.20) | collective-permute-done | bytes 213024 | tf_op jit(solution)/shard_map/ppermute | solution.py:52
  117.7 3.6 %collective-permute-done.21.d = s16[208,512]{1,0:T(8,128)(2,1)S(1)} collective-permute-done((s16[208,512]{1,0:T(8,128)(2,1)S(1)}, s16[208,512]{1,0:T(8,128)(2,1)S(1)}, u32[]{:S(2)}, u32[]{:S(2)}) %collective-permute-start.21) | collective-permute-done | bytes 213024 | tf_op jit(solution)/shard_map/ppermute | solution.py:52
  121.5 1.6 %collective-permute-start.22 = (s16[208,128]{1,0:T(8,128)(2,1)S(1)}, s16[208,128]{1,0:T(8,128)(2,1)S(1)}, u32[]{:S(2)}, u32[]{:S(2)}) collective-permute-start(s16[208,128]{1,0:T(8,128)(2,1)S(1)} %get-tuple-element.56), channel_id=1, source_target_pairs={{0,4},{1,5},{2,6},{3,7},{4,8},{5,9},{6,10},{7,11},{8,12},{9,13},{1... | collective-permute-start | bytes 159752 | tf_op jit(solution)/shard_map/ppermute | solution.py:52
  124.8 2.5 %collective-permute-start.15 = (s16[208,256]{1,0:T(8,128)(2,1)S(1)}, s16[208,256]{1,0:T(8,128)(2,1)S(1)}, u32[]{:S(2)}, u32[]{:S(2)}) collective-permute-start(s16[208,256]{1,0:T(8,128)(2,1)S(1)} %get-tuple-element.45), channel_id=1, source_target_pairs={{0,96},{1,97},{2,98},{3,99},{4,100},{5,101},{6,102},{7,103},{8,104... | collective-permute-start | bytes 319496 | tf_op jit(solution)/shard_map/ppermute | solution.py:52
  127.3 2.7 %collective-permute-start.23 = (s16[208,128]{1,0:T(8,128)(2,1)S(1)}, s16[208,128]{1,0:T(8,128)(2,1)S(1)}, u32[]{:S(2)}, u32[]{:S(2)}) collective-permute-start(s16[208,128]{1,0:T(8,128)(2,1)S(1)} %get-tuple-element.57), channel_id=1, source_target_pairs={{0,8},{1,9},{2,10},{3,11},{4,12},{5,13},{6,14},{7,15},{8,0},{9,1},... | collective-permute-start | bytes 159752 | tf_op jit(solution)/shard_map/ppermute | solution.py:52
  130.0 1.4 %collective-permute-start.24 = (s16[208,128]{1,0:T(8,128)(2,1)S(1)}, s16[208,128]{1,0:T(8,128)(2,1)S(1)}, u32[]{:S(2)}, u32[]{:S(2)}) collective-permute-start(s16[208,128]{1,0:T(8,128)(2,1)S(1)} %get-tuple-element.58), channel_id=1, source_target_pairs={{0,12},{1,13},{2,14},{3,15},{4,0},{5,1},{6,2},{7,3},{8,4},{9,5},{1... | collective-permute-start | bytes 159752 | tf_op jit(solution)/shard_map/ppermute | solution.py:52
  131.5 1.5 %collective-permute-done.23.rb = s16[208,128]{1,0:T(8,128)(2,1)S(1)} collective-permute-done((s16[208,128]{1,0:T(8,128)(2,1)S(1)}, s16[208,128]{1,0:T(8,128)(2,1)S(1)}, u32[]{:S(2)}, u32[]{:S(2)}) %collective-permute-start.23) | collective-permute-done | bytes 53280 | tf_op jit(solution)/shard_map/ppermute | solution.py:52
  133.0 1.2 collective-permute-done.24.rd
  (39 shorter events, 10.3 us)
Async XLA Ops:
  0.0 0.7 copy-start
  0.7 0.7 copy-start.2
  4.4 18.1 %collective-permute-start.1 = (bf16[6,16,3200]{2,1,0:T(8,128)(2,1)S(1)}, bf16[6,16,3200]{2,1,0:T(8,128)(2,1)S(1)}, u32[]{:S(2)}, u32[]{:S(2)}) collective-permute-start(bf16[6,16,3200]{2,1,0:T(8,128)(2,1)S(1)} %get-tuple-element.33), channel_id=1, source_target_pairs={{0,32},{1,33},{2,34},{3,35},{4,36},{5,37},{6,38},{7,39},{8,40},{9,... | collective-permute-start | bytes 1843208 | tf_op jit(solution)/shard_map/ppermute | solution.py:52
  6.5 30.3 %collective-permute-start.3 = (bf16[6,16,3200]{2,1,0:T(8,128)(2,1)S(1)}, bf16[6,16,3200]{2,1,0:T(8,128)(2,1)S(1)}, u32[]{:S(2)}, u32[]{:S(2)}) collective-permute-start(bf16[6,16,3200]{2,1,0:T(8,128)(2,1)S(1)} %get-tuple-element.34), channel_id=1, source_target_pairs={{0,64},{1,65},{2,66},{3,67},{4,68},{5,69},{6,70},{7,71},{8,72},{9,... | collective-permute-start | bytes 1843208 | tf_op jit(solution)/shard_map/ppermute | solution.py:52
  10.1 26.7 %collective-permute-start.5 = (bf16[6,16,3200]{2,1,0:T(8,128)(2,1)S(1)}, bf16[6,16,3200]{2,1,0:T(8,128)(2,1)S(1)}, u32[]{:S(2)}, u32[]{:S(2)}) collective-permute-start(bf16[6,16,3200]{2,1,0:T(8,128)(2,1)S(1)} %get-tuple-element.35), channel_id=1, source_target_pairs={{0,96},{1,97},{2,98},{3,99},{4,100},{5,101},{6,102},{7,103},{8,104... | collective-permute-start | bytes 1843208 | tf_op jit(solution)/shard_map/ppermute | solution.py:52
  11.1 26.2 %collective-permute-start = (bf16[6,16,3200]{2,1,0:T(8,128)(2,1)S(1)}, bf16[6,16,3200]{2,1,0:T(8,128)(2,1)S(1)}, u32[]{:S(2)}, u32[]{:S(2)}) collective-permute-start(bf16[6,16,3200]{2,1,0:T(8,128)(2,1)S(1)} %get-tuple-element.32.refs_0_), channel_id=1, source_target_pairs={{0,16},{1,17},{2,18},{3,19},{4,20},{5,21},{6,22},{7,23},{8,24},{9,... | collective-permute-start | bytes 1843208 | tf_op jit(solution)/shard_map/ppermute | solution.py:52
  22.5 14.9 %collective-permute-start.2 = (bf16[6,16,3200]{2,1,0:T(8,128)(2,1)S(1)}, bf16[6,16,3200]{2,1,0:T(8,128)(2,1)S(1)}, u32[]{:S(2)}, u32[]{:S(2)}) collective-permute-start(bf16[6,16,3200]{2,1,0:T(8,128)(2,1)S(1)} %collective-permute-done.1.refs_2_), channel_id=1, source_target_pairs={{0,16},{1,17},{2,18},{3,19},{4,20},{5,21},{6,22},{7,23},{8,24},{9,... | collective-permute-start | bytes 1843208 | tf_op jit(solution)/shard_map/ppermute | solution.py:52
  36.8 2.0 %collective-permute-start.4 = (bf16[6,16,3200]{2,1,0:T(8,128)(2,1)S(1)}, bf16[6,16,3200]{2,1,0:T(8,128)(2,1)S(1)}, u32[]{:S(2)}, u32[]{:S(2)}) collective-permute-start(bf16[6,16,3200]{2,1,0:T(8,128)(2,1)S(1)} %collective-permute-done.3.refs_4_), channel_id=1, source_target_pairs={{0,16},{1,17},{2,18},{3,19},{4,20},{5,21},{6,22},{7,23},{8,24},{9,... | collective-permute-start | bytes 1843208 | tf_op jit(solution)/shard_map/ppermute | solution.py:52
  36.8 2.9 %collective-permute-start.6 = (bf16[6,16,3200]{2,1,0:T(8,128)(2,1)S(1)}, bf16[6,16,3200]{2,1,0:T(8,128)(2,1)S(1)}, u32[]{:S(2)}, u32[]{:S(2)}) collective-permute-start(bf16[6,16,3200]{2,1,0:T(8,128)(2,1)S(1)} %collective-permute-done.5.refs_6_), channel_id=1, source_target_pairs={{0,16},{1,17},{2,18},{3,19},{4,20},{5,21},{6,22},{7,23},{8,24},{9,... | collective-permute-start | bytes 1843208 | tf_op jit(solution)/shard_map/ppermute | solution.py:52
  49.4 20.0 %collective-permute-start.18 = (s16[3136,128]{1,0:T(8,128)(2,1)S(1)}, s16[3136,128]{1,0:T(8,128)(2,1)S(1)}, u32[]{:S(2)}, u32[]{:S(2)}) collective-permute-start(s16[3136,128]{1,0:T(8,128)(2,1)S(1)} %get-tuple-element.50), channel_id=1, source_target_pairs={{0,96},{1,97},{2,98},{3,99},{4,100},{5,101},{6,102},{7,103},{8,104... | collective-permute-start | bytes 2408456 | tf_op jit(solution)/shard_map/ppermute | solution.py:52
  52.7 18.2 %copy-start.1 = (bf16[16,128]{1,0:T(8,128)(2,1)S(1)}, bf16[16,128]{1,0:T(8,128)(2,1)}, u32[]{:S(2)}) copy-start(bf16[16,128]{1,0:T(8,128)(2,1)} %after.3) | copy-start | bytes 12292
  52.7 47.3 %collective-permute-start.9 = (s16[784,1024]{1,0:T(8,128)(2,1)S(1)}, s16[784,1024]{1,0:T(8,128)(2,1)S(1)}, u32[]{:S(2)}, u32[]{:S(2)}) collective-permute-start(s16[784,1024]{1,0:T(8,128)(2,1)S(1)} %shard_map.41), channel_id=1, source_target_pairs={{0,12},{1,13},{2,14},{3,15},{4,0},{5,1},{6,2},{7,3},{8,4},{9,5},{1... | collective-permute-start | bytes 4816904 | tf_op jit(solution)/shard_map/ppermute | solution.py:52
  55.5 44.5 %collective-permute-start.8 = (s16[784,1024]{1,0:T(8,128)(2,1)S(1)}, s16[784,1024]{1,0:T(8,128)(2,1)S(1)}, u32[]{:S(2)}, u32[]{:S(2)}) collective-permute-start(s16[784,1024]{1,0:T(8,128)(2,1)S(1)} %shard_map.40), channel_id=1, source_target_pairs={{0,8},{1,9},{2,10},{3,11},{4,12},{5,13},{6,14},{7,15},{8,0},{9,1},... | collective-permute-start | bytes 4816904 | tf_op jit(solution)/shard_map/ppermute | solution.py:52
  56.3 43.7 %collective-permute-start.7 = (s16[784,1024]{1,0:T(8,128)(2,1)S(1)}, s16[784,1024]{1,0:T(8,128)(2,1)S(1)}, u32[]{:S(2)}, u32[]{:S(2)}) collective-permute-start(s16[784,1024]{1,0:T(8,128)(2,1)S(1)} %shard_map.39), channel_id=1, source_target_pairs={{0,4},{1,5},{2,6},{3,7},{4,8},{5,9},{6,10},{7,11},{8,12},{9,13},{1... | collective-permute-start | bytes 4816904 | tf_op jit(solution)/shard_map/ppermute | solution.py:52
  59.6 37.5 %collective-permute-start.16 = (s16[3136,128]{1,0:T(8,128)(2,1)S(1)}, s16[3136,128]{1,0:T(8,128)(2,1)S(1)}, u32[]{:S(2)}, u32[]{:S(2)}) collective-permute-start(s16[3136,128]{1,0:T(8,128)(2,1)S(1)} %get-tuple-element.48), channel_id=1, source_target_pairs={{0,32},{1,33},{2,34},{3,35},{4,36},{5,37},{6,38},{7,39},{8,40},{9,... | collective-permute-start | bytes 2408456 | tf_op jit(solution)/shard_map/ppermute | solution.py:52
  69.4 27.7 %collective-permute-start.17 = (s16[3136,128]{1,0:T(8,128)(2,1)S(1)}, s16[3136,128]{1,0:T(8,128)(2,1)S(1)}, u32[]{:S(2)}, u32[]{:S(2)}) collective-permute-start(s16[3136,128]{1,0:T(8,128)(2,1)S(1)} %get-tuple-element.49), channel_id=1, source_target_pairs={{0,64},{1,65},{2,66},{3,67},{4,68},{5,69},{6,70},{7,71},{8,72},{9,... | collective-permute-start | bytes 2408456 | tf_op jit(solution)/shard_map/ppermute | solution.py:52
  98.0 10.0 %collective-permute-start.19 = (s16[208,512]{1,0:T(8,128)(2,1)S(1)}, s16[208,512]{1,0:T(8,128)(2,1)S(1)}, u32[]{:S(2)}, u32[]{:S(2)}) collective-permute-start(s16[208,512]{1,0:T(8,128)(2,1)S(1)} %get-tuple-element.52), channel_id=1, source_target_pairs={{0,1},{1,2},{2,3},{3,0},{4,5},{5,6},{6,7},{7,4},{8,9},{9,10},{10,1... | collective-permute-start | bytes 638984 | tf_op jit(solution)/shard_map/ppermute | solution.py:52
  101.8 21.3 %collective-permute-start.10 = (s16[208,1024]{1,0:T(8,128)(2,1)S(1)}, s16[208,1024]{1,0:T(8,128)(2,1)S(1)}, u32[]{:S(2)}, u32[]{:S(2)}) collective-permute-start(s16[208,1024]{1,0:T(8,128)(2,1)S(1)} %get-tuple-element.39), channel_id=1, source_target_pairs={{0,1},{1,2},{2,3},{3,0},{4,5},{5,6},{6,7},{7,4},{8,9},{9,10},{10,1... | collective-permute-start | bytes 1277960 | tf_op jit(solution)/shard_map/ppermute | solution.py:52
  102.2 21.0 %collective-permute-start.11 = (s16[208,1024]{1,0:T(8,128)(2,1)S(1)}, s16[208,1024]{1,0:T(8,128)(2,1)S(1)}, u32[]{:S(2)}, u32[]{:S(2)}) collective-permute-start(s16[208,1024]{1,0:T(8,128)(2,1)S(1)} %get-tuple-element.40), channel_id=1, source_target_pairs={{0,2},{1,3},{2,0},{3,1},{4,6},{5,7},{6,4},{7,5},{8,10},{9,11},{10,... | collective-permute-start | bytes 1277960 | tf_op jit(solution)/shard_map/ppermute | solution.py:52
  104.7 18.4 %collective-permute-start.12 = (s16[208,1024]{1,0:T(8,128)(2,1)S(1)}, s16[208,1024]{1,0:T(8,128)(2,1)S(1)}, u32[]{:S(2)}, u32[]{:S(2)}) collective-permute-start(s16[208,1024]{1,0:T(8,128)(2,1)S(1)} %get-tuple-element.41), channel_id=1, source_target_pairs={{0,3},{1,0},{2,1},{3,2},{4,7},{5,4},{6,5},{7,6},{8,11},{9,8},{10,9... | collective-permute-start | bytes 1277960 | tf_op jit(solution)/shard_map/ppermute | solution.py:52
  106.3 11.4 %collective-permute-start.20 = (s16[208,512]{1,0:T(8,128)(2,1)S(1)}, s16[208,512]{1,0:T(8,128)(2,1)S(1)}, u32[]{:S(2)}, u32[]{:S(2)}) collective-permute-start(s16[208,512]{1,0:T(8,128)(2,1)S(1)} %get-tuple-element.53), channel_id=1, source_target_pairs={{0,2},{1,3},{2,0},{3,1},{4,6},{5,7},{6,4},{7,5},{8,10},{9,11},{10,... | collective-permute-start | bytes 638984 | tf_op jit(solution)/shard_map/ppermute | solution.py:52
  108.0 13.2 %collective-permute-start.21 = (s16[208,512]{1,0:T(8,128)(2,1)S(1)}, s16[208,512]{1,0:T(8,128)(2,1)S(1)}, u32[]{:S(2)}, u32[]{:S(2)}) collective-permute-start(s16[208,512]{1,0:T(8,128)(2,1)S(1)} %get-tuple-element.54), channel_id=1, source_target_pairs={{0,3},{1,0},{2,1},{3,2},{4,7},{5,4},{6,5},{7,6},{8,11},{9,8},{10,9... | collective-permute-start | bytes 638984 | tf_op jit(solution)/shard_map/ppermute | solution.py:52
  121.5 8.5 %collective-permute-start.22 = (s16[208,128]{1,0:T(8,128)(2,1)S(1)}, s16[208,128]{1,0:T(8,128)(2,1)S(1)}, u32[]{:S(2)}, u32[]{:S(2)}) collective-permute-start(s16[208,128]{1,0:T(8,128)(2,1)S(1)} %get-tuple-element.56), channel_id=1, source_target_pairs={{0,4},{1,5},{2,6},{3,7},{4,8},{5,9},{6,10},{7,11},{8,12},{9,13},{1... | collective-permute-start | bytes 159752 | tf_op jit(solution)/shard_map/ppermute | solution.py:52
  123.6 10.6 %collective-permute-start.13 = (s16[208,256]{1,0:T(8,128)(2,1)S(1)}, s16[208,256]{1,0:T(8,128)(2,1)S(1)}, u32[]{:S(2)}, u32[]{:S(2)}) collective-permute-start(s16[208,256]{1,0:T(8,128)(2,1)S(1)} %get-tuple-element.43), channel_id=1, source_target_pairs={{0,32},{1,33},{2,34},{3,35},{4,36},{5,37},{6,38},{7,39},{8,40},{9,... | collective-permute-start | bytes 319496 | tf_op jit(solution)/shard_map/ppermute | solution.py:52
  123.7 10.5 %collective-permute-start.14 = (s16[208,256]{1,0:T(8,128)(2,1)S(1)}, s16[208,256]{1,0:T(8,128)(2,1)S(1)}, u32[]{:S(2)}, u32[]{:S(2)}) collective-permute-start(s16[208,256]{1,0:T(8,128)(2,1)S(1)} %get-tuple-element.44), channel_id=1, source_target_pairs={{0,64},{1,65},{2,66},{3,67},{4,68},{5,69},{6,70},{7,71},{8,72},{9,... | collective-permute-start | bytes 319496 | tf_op jit(solution)/shard_map/ppermute | solution.py:52
  124.8 9.4 %collective-permute-start.15 = (s16[208,256]{1,0:T(8,128)(2,1)S(1)}, s16[208,256]{1,0:T(8,128)(2,1)S(1)}, u32[]{:S(2)}, u32[]{:S(2)}) collective-permute-start(s16[208,256]{1,0:T(8,128)(2,1)S(1)} %get-tuple-element.45), channel_id=1, source_target_pairs={{0,96},{1,97},{2,98},{3,99},{4,100},{5,101},{6,102},{7,103},{8,104... | collective-permute-start | bytes 319496 | tf_op jit(solution)/shard_map/ppermute | solution.py:52
  127.3 5.6 %collective-permute-start.23 = (s16[208,128]{1,0:T(8,128)(2,1)S(1)}, s16[208,128]{1,0:T(8,128)(2,1)S(1)}, u32[]{:S(2)}, u32[]{:S(2)}) collective-permute-start(s16[208,128]{1,0:T(8,128)(2,1)S(1)} %get-tuple-element.57), channel_id=1, source_target_pairs={{0,8},{1,9},{2,10},{3,11},{4,12},{5,13},{6,14},{7,15},{8,0},{9,1},... | collective-permute-start | bytes 159752 | tf_op jit(solution)/shard_map/ppermute | solution.py:52
  130.0 4.1 %collective-permute-start.24 = (s16[208,128]{1,0:T(8,128)(2,1)S(1)}, s16[208,128]{1,0:T(8,128)(2,1)S(1)}, u32[]{:S(2)}, u32[]{:S(2)}) collective-permute-start(s16[208,128]{1,0:T(8,128)(2,1)S(1)} %get-tuple-element.58), channel_id=1, source_target_pairs={{0,12},{1,13},{2,14},{3,15},{4,0},{5,1},{6,2},{7,3},{8,4},{9,5},{1... | collective-permute-start | bytes 159752 | tf_op jit(solution)/shard_map/ppermute | solution.py:52

commit v5 on v4

--- a/solution.py
+++ b/solution.py
@@ -68,17 +68,17 @@
     return lambda z, c, x, y: (z, c, x, y + k) if c == 0 else (z, c, x + k, y)
 
 
-def screen_body(survive, half, metric, *rest):
-    outs, (held, own, turned, sems) = rest[:4], rest[4:]
+def screen_body(survive, half, *rest):
+    outs, (held, turned, sems) = rest[:4], rest[4:]
     at = position()
     ao = half.shape[2]
     block = ao // survive.shape[2]
-    chunks = sems.shape[0] - 1
+    chunks = sems.shape[0]
     lanes = ao // chunks
     copies = [
         pltpu.make_async_copy(half.at[:, :, cut], held.at[:, :, cut], sems.at[n])
         for n, cut in enumerate(slice(n * lanes, (n + 1) * lanes) for n in range(chunks))
-    ] + [pltpu.make_async_copy(metric, own, sems.at[chunks])]
+    ]
     for copy in copies:
         copy.start()
     for n in range(chunks):
@@ -92,56 +92,68 @@
             return carry
 
         lax.fori_loop(0, lanes // block, step, 0, unroll=True)
-    copies[chunks].wait()
     group = outs[0].shape[0]
     for k in range(RING):
         first = lax.rem(at[0] + k, RING) * group
-        outs[k][:, :, :ao] = turned[pl.ds(first, group)]
-        outs[k][:, :, ao:] = jnp.broadcast_to(own[...][None], (group,) + metric.shape)
-
-
-def screen(survive, half, metric):
+        outs[k][...] = turned[pl.ds(first, group)]
+
+
+def screen(survive, half):
     aux, occ, ao = half.shape
-    out = jax.ShapeDtypeStruct((occ // RING, aux, ao + metric.shape[1]), BF)
+    out = jax.ShapeDtypeStruct((occ // RING, aux, ao), BF)
     in_hbm = pl.BlockSpec(memory_space=pltpu.HBM)
     return pl.pallas_call(
         screen_body,
         out_shape=[out] * RING,
-        in_specs=[scalars(), in_hbm, in_hbm],
+        in_specs=[scalars(), in_hbm],
         out_specs=[whole()] * RING,
         scratch_shapes=[
             pltpu.VMEM(half.shape, BF),
-            pltpu.VMEM(metric.shape, BF),
             pltpu.VMEM((occ, aux, ao), BF),
-            pltpu.SemaphoreType.DMA((5,)),
+            pltpu.SemaphoreType.DMA((4,)),
         ],
         compiler_params=params(50),
         cost_estimate=cost(half.size, half.size * 4),
         name="screen",
-    )(survive, half, metric)
+    )(survive, half)
+
+
+def join_body(*refs):
+    metrics, mixed = refs[:4], refs[4]
+    at = position()
+    aux = mixed.shape[0]
+    part = aux // 8
+    metric = jnp.concatenate([m[...] for m in metrics], axis=0)
+    source = lax.broadcasted_iota(jnp.int32, (aux, aux), 0)
+    n = lax.broadcasted_iota(jnp.int32, (aux, aux), 1)
+    slot = n // part
+    up = lax.rem(at[0] - slot // 2 + RING, RING)
+    core = jnp.where(slot % 2 == 0, at[1], 1 - at[1])
+    wanted = (up * 2 + core) * part + n % part
+    pick = jnp.where(source == wanted, 1.0, 0.0).astype(BF)
+    mixed[...] = jnp.dot(metric, pick, preferred_element_type=F32).astype(BF)
+
+
+def join(metrics):
+    aux = metrics[0].shape[1]
+    return pl.pallas_call(
+        join_body,
+        out_shape=jax.ShapeDtypeStruct((aux, aux), BF),
+        in_specs=[whole()] * 4,
+        out_specs=whole(),
+        compiler_params=params(4),
+        cost_estimate=cost(2 * aux**3, aux * aux * 4),
+        name="join",
+    )(*metrics)
 
 
 def fit_body(*refs):
-    at = position()
-    pieces, (bulk, rest, turned, mixed, fresh) = refs[:8], refs[8:]
+    pieces, mixed, (bulk, rest, turned, fresh) = refs[:8], refs[8], refs[9:]
+    at = position()
     step = pl.program_id(0)
     ao = fresh.shape[1]
     aux = mixed.shape[0]
-    part = aux // 8
-
-    @pl.when(step == 0)
-    def _():
-        metric = jnp.concatenate([p[0][:, ao:] for p in pieces], axis=0)
-        source = lax.broadcasted_iota(jnp.int32, (aux, aux), 0)
-        n = lax.broadcasted_iota(jnp.int32, (aux, aux), 1)
-        slot = n // part
-        up = lax.rem(at[0] - slot // 2 + RING, RING)
-        core = jnp.where(slot % 2 == 0, at[1], 1 - at[1])
-        wanted = (up * 2 + core) * part + n % part
-        pick = jnp.where(source == wanted, 1.0, 0.0).astype(BF)
-        mixed[...] = jnp.dot(metric, pick, preferred_element_type=F32).astype(BF)
-
-    screened = jnp.concatenate([p[0][:, :ao] for p in pieces], axis=0)
+    screened = jnp.concatenate([p[0] for p in pieces], axis=0)
     fitted = jnp.dot(mixed[...], screened, preferred_element_type=F32).astype(BF)
     fresh[...] = fitted
     wide, narrow = bulk.shape[1] // RING, rest.shape[1] // RING
@@ -160,23 +172,23 @@
             turned[pl.ds(pl.multiple_of(to, 64), high), cut] = flipped[n * high:(n + 1) * high]
 
 
-def fit(pieces):
-    group, part, wide = pieces[0].shape
+def fit(pieces, mixed):
+    group, part, ao = pieces[0].shape
     aux = part * 8
-    ao = wide - aux
-    piece = pl.BlockSpec((1, part, wide), lambda i: (i, 0, 0))
+    piece = pl.BlockSpec((1, part, ao), lambda i: (i, 0, 0))
     return pl.pallas_call(
         fit_body,
         grid=(group,),
         out_shape=[jax.ShapeDtypeStruct((group * aux, n), BF) for n in (ao // 3, ao // 6)]
         + [jax.ShapeDtypeStruct((ao, group * aux), BF)],
-        in_specs=[piece] * 8,
+        in_specs=[piece] * 8 + [whole()],
         out_specs=[pl.BlockSpec((aux, n), lambda i: (i, 0)) for n in (ao // 3, ao // 6)]
         + [pl.BlockSpec((ao, group * aux), lambda i: (0, 0))],
-        scratch_shapes=[pltpu.VMEM((aux, aux), BF), pltpu.VMEM((aux, ao), BF)],
+        scratch_shapes=[pltpu.VMEM((aux, ao), BF)],
         compiler_params=params(28),
         cost_estimate=cost(2 * group * aux * aux * ao, group * aux * ao * 6),
-    )(*pieces)
+        name="fit",
+    )(*pieces, mixed)
 
 
 def exponent(top):
@@ -234,29 +246,30 @@
     )(bulk, turned)
 
 
-def rest_body(rest, turned, *outs):
-    both = jnp.dot(turned[...], rest[...], preferred_element_type=F32)
-    narrow = both.shape[1] // 2
-    write(outs[0], 0, both[:, :narrow])
-    write(outs[1], 0, both[:, narrow:])
-
-
-def rest_k(rest, turned, pair):
+def rest_body(first, rest, turned, *outs):
+    narrow = rest.shape[1] // RING
+    total = turned.shape[0] // RING
+    right = rest[:, first * narrow:(first + len(outs)) * narrow]
+    for g in range(RING):
+        block = jnp.dot(turned[g * total:(g + 1) * total, :], right, preferred_element_type=F32)
+        for n, out in enumerate(outs):
+            write(out, g * (out.shape[0] // RING), block[:, n * narrow:(n + 1) * narrow])
+
+
+def rest_k(rest, turned, first, last):
     depth = rest.shape[0]
     ao = turned.shape[0]
-    total, narrow = ao // RING, rest.shape[1] // RING
-    each = [total + (TAIL if k else 0) for k in ORDER[2 * pair:2 * pair + 2]]
-    return pl.pallas_call(
-        rest_body,
-        grid=(RING,),
-        out_shape=[jax.ShapeDtypeStruct((RING * n, narrow), I16 if n > total else F32) for n in each],
-        in_specs=[
-            pl.BlockSpec((depth, 2 * narrow), lambda g: (0, pair)),
-            pl.BlockSpec((total, depth), lambda g: (g, 0)),
+    narrow = rest.shape[1] // RING
+    shifts = ORDER[first:last]
+    return pl.pallas_call(
+        functools.partial(rest_body, first),
+        out_shape=[
+            jax.ShapeDtypeStruct((ao + (RING * TAIL if k else 0), narrow), I16 if k else F32) for k in shifts
         ],
-        out_specs=[pl.BlockSpec((n, narrow), lambda g: (g, 0)) for n in each],
+        in_specs=[whole()] * 2,
+        out_specs=[whole()] * len(shifts),
         compiler_params=params(28),
-        cost_estimate=cost(4 * depth * ao * narrow, ao * narrow * 4),
+        cost_estimate=cost(2 * len(shifts) * depth * ao * narrow, ao * narrow * 4),
     )(rest, turned)
 
 
@@ -363,12 +376,17 @@
 
 
 def shards(half, metric, survive):
-    parts = screen(survive, half, metric)
+    parts = screen(survive, half)
     here = [parts[0]] + [None] * 3
-    for k in (2, 1, 3):
+    for k in ORDER[:3]:
         here[k] = send(parts[k], along_z(k))
+    pair = jnp.concatenate([metric, send(metric, other_core)], axis=0)
+    metrics = [pair] + [None] * 3
+    for k in ORDER[:3]:
+        metrics[k] = send(pair, along_z(k))
+    mixed = join(metrics)
     there = [send(v, other_core) for v in here]
-    bulk_rows, rest_rows, turned = fit([v for pair in zip(here, there) for v in pair])
+    bulk_rows, rest_rows, turned = fit([v for both in zip(here, there) for v in both], mixed)
 
     bulk, rest = [None] * 4, [None] * 4
 
@@ -377,20 +395,21 @@
         if k:
             bulk[k] = send(bulk[k], first_axis(k))
 
-    def rest_step(pair):
-        out = rest_k(rest_rows, turned, pair)
-        for k, v in zip(ORDER[2 * pair:2 * pair + 2], out):
+    def rest_step(first, last):
+        out = rest_k(rest_rows, turned, first, last)
+        for k, v in zip(ORDER[first:last], out):
             rest[k] = send(v, along_z(k)) if k else v
 
     def onward(parts, shift):
         for k in ORDER[:3]:
             parts[k] = send(parts[k], shift(k))
 
-    rest_step(0)
+    rest_step(0, 1)
     bulk_step(2)
-    rest_step(1)
+    rest_step(1, 3)
     bulk_step(1)
     bulk_step(3)
+    rest_step(3, 4)
     bulk_step(0)
     rest = second(rest, RING, metric)
     onward(rest, second_axis)

time: 135 us -> 147 us (1.089)
  the two profiles are of different devices: /device:TPU:0 before, /device:TPU:16 now
where the time goes in v5:
time: 147 us
  waiting for transfers between devices  89.7 us (61%)
  starting transfers between devices  34 us (23%)
  Pallas kernels  22.8 us (16%)
    ppermute x29, waiting for transfers between devices, send(): return lax.ppermute(v, AXES, moves(shift))  89.7 us
    ppermute x29, starting transfers between devices, send(): return lax.ppermute(v, AXES, moves(shift))  34 us
    pallas_call x4, Pallas kernels, bulk_k(): pl.pallas_call(functools.partial(bulk_body, shift), out_shape=jax.ShapeDt...  7.08 us
    pallas_call x3, Pallas kernels, rest_k(): pl.pallas_call(functools.partial(rest_body, first), out_shape=[jax.ShapeD...  4.87 us
    pallas_call x1, Pallas kernels, fit(): pl.pallas_call(fit_body, grid=(group,), out_shape=[jax.ShapeDtypeStruct((...  3.31 us
    pallas_call x1, Pallas kernels, screen(): pl.pallas_call(screen_body, out_shape=[out] * RING, in_specs=[scalars(),...  3.12 us
  transfers between devices with their start and end apart: 29, of which 13 were waited for; matrix products, arithmetic and copies ran while one was open for 0% of the time, Pallas kernels for 7%

profile of v5, /device:TPU:16, one launch (start us, length us, event | category | flops | bytes accessed | tf_op | source)
XLA Modules:
  0.0 147.3 jit_solution(7268745166831655207)
XLA Ops:
  0.7 3.1 %screen.1 = (bf16[6,16,3072]{2,1,0:T(8,128)(2,1)S(1)}, bf16[6,16,3072]{2,1,0:T(8,128)(2,1)S(1)}, bf16[6,16,3072]{2,1,0:T(8,128)(2,1)S(1)}, bf16[6,16,3072]{2,1,0:T(8,128)(2,1)S(1)}) custom-call(s32[1,1,24]{2,1,0:T(1,128)S(1)} %copy-done.1, bf16[16,24,3072]{2,1,0:T(8,128)(2,1)} %half.1), custom_call_target="tpu_custom_call" | custom-call | flops 1179648 | bytes 4718592 | tf_op jit(solution)/shard_map/screen/pallas_call | solution.py:105
  3.8 2.0 %collective-permute-start.1 = (bf16[6,16,3072]{2,1,0:T(8,128)(2,1)S(1)}, bf16[6,16,3072]{2,1,0:T(8,128)(2,1)S(1)}, u32[]{:S(2)}, u32[]{:S(2)}) collective-permute-start(bf16[6,16,3072]{2,1,0:T(8,128)(2,1)S(1)} %get-tuple-element.31), channel_id=1, source_target_pairs={{0,32},{1,33},{2,34},{3,35},{4,36},{5,37},{6,38},{7,39},{8,40},{9,... | collective-permute-start | bytes 1769480 | tf_op jit(solution)/shard_map/ppermute | solution.py:52
  5.8 3.6 %collective-permute-start.3 = (bf16[6,16,3072]{2,1,0:T(8,128)(2,1)S(1)}, bf16[6,16,3072]{2,1,0:T(8,128)(2,1)S(1)}, u32[]{:S(2)}, u32[]{:S(2)}) collective-permute-start(bf16[6,16,3072]{2,1,0:T(8,128)(2,1)S(1)} %get-tuple-element.32), channel_id=1, source_target_pairs={{0,64},{1,65},{2,66},{3,67},{4,68},{5,69},{6,70},{7,71},{8,72},{9,... | collective-permute-start | bytes 1769480 | tf_op jit(solution)/shard_map/ppermute | solution.py:52
  10.4 10.9 %collective-permute-done.1.refs_2_ = bf16[6,16,3072]{2,1,0:T(8,128)(2,1)S(1)} collective-permute-done((bf16[6,16,3072]{2,1,0:T(8,128)(2,1)S(1)}, bf16[6,16,3072]{2,1,0:T(8,128)(2,1)S(1)}, u32[]{:S(2)}, u32[]{:S(2)}) %collective-permute-start.1) | collective-permute-done | bytes 589856 | tf_op jit(solution)/shard_map/ppermute | solution.py:52
  21.2 13.8 %collective-permute-done.3.refs_4_ = bf16[6,16,3072]{2,1,0:T(8,128)(2,1)S(1)} collective-permute-done((bf16[6,16,3072]{2,1,0:T(8,128)(2,1)S(1)}, bf16[6,16,3072]{2,1,0:T(8,128)(2,1)S(1)}, u32[]{:S(2)}, u32[]{:S(2)}) %collective-permute-start.3) | collective-permute-done | bytes 589856 | tf_op jit(solution)/shard_map/ppermute | solution.py:52
  35.6 2.2 %collective-permute-done.7 = bf16[16,128]{1,0:T(8,128)(2,1)S(1)} collective-permute-done((bf16[16,128]{1,0:T(8,128)(2,1)S(1)}, bf16[16,128]{1,0:T(8,128)(2,1)S(1)}, u32[]{:S(2)}, u32[]{:S(2)}) %collective-permute-start.7) | collective-permute-done | bytes 4128 | tf_op jit(solution)/shard_map/ppermute | solution.py:52
  37.9 1.3 collective-permute-start.10
  39.2 2.3 %collective-permute-done.10.refs_3_ = bf16[32,128]{1,0:T(8,128)(2,1)S(1)} collective-permute-done((bf16[32,128]{1,0:T(8,128)(2,1)S(1)}, bf16[32,128]{1,0:T(8,128)(2,1)S(1)}, u32[]{:S(2)}, u32[]{:S(2)}) %collective-permute-start.10) | collective-permute-done | bytes 8224 | tf_op jit(solution)/shard_map/ppermute | solution.py:52
  41.9 4.5 %collective-permute-done.8.refs_1_ = bf16[32,128]{1,0:T(8,128)(2,1)S(1)} collective-permute-done((bf16[32,128]{1,0:T(8,128)(2,1)S(1)}, bf16[32,128]{1,0:T(8,128)(2,1)S(1)}, u32[]{:S(2)}, u32[]{:S(2)}) %collective-permute-start.8) | collective-permute-done | bytes 8224 | tf_op jit(solution)/shard_map/ppermute | solution.py:52
  46.9 4.7 %collective-permute-done.9.refs_2_ = bf16[32,128]{1,0:T(8,128)(2,1)S(1)} collective-permute-done((bf16[32,128]{1,0:T(8,128)(2,1)S(1)}, bf16[32,128]{1,0:T(8,128)(2,1)S(1)}, u32[]{:S(2)}, u32[]{:S(2)}) %collective-permute-start.9) | collective-permute-done | bytes 8224 | tf_op jit(solution)/shard_map/ppermute | solution.py:52
  51.8 3.3 %fit.1 = (bf16[768,1024]{1,0:T(8,128)(2,1)S(1)}, bf16[768,512]{1,0:T(8,128)(2,1)S(1)}, bf16[3072,768]{1,0:T(8,128)(2,1)S(1)}) custom-call(bf16[6,16,3072]{2,1,0:T(8,128)(2,1)S(1)} %get-tuple-element.30.refs_0_, bf16[6,16,3072]{2,1,0:T(8,128)(2,1)S(1)} %collective-permute-done.refs_1_, bf16[6,16,3072]{2,1,0:T(8,128)(2,1)S(1)} %collective-permute-done.1.refs_2_, ...), custom_call_target="tpu_custom_call" | custom-call | flops 603979776 | bytes 14155776 | tf_op jit(solution)/shard_map/fit/pallas_call | solution.py:179
  55.1 1.9 %shard_map.40 = s16[784,1024]{1,0:T(8,128)(2,1)S(1)} custom-call(bf16[768,1024]{1,0:T(8,128)(2,1)S(1)} %get-tuple-element.34.bulk, bf16[3072,768]{1,0:T(8,128)(2,1)S(1)} %get-tuple-element.35.turned), custom_call_target="tpu_custom_call" | custom-call | flops 1207959552 | bytes 1572864 | tf_op jit(solution)/shard_map/pallas_call | solution.py:239
  57.0 1.9 %shard_map.39 = s16[784,1024]{1,0:T(8,128)(2,1)S(1)} custom-call(bf16[768,1024]{1,0:T(8,128)(2,1)S(1)} %get-tuple-element.34.bulk, bf16[3072,768]{1,0:T(8,128)(2,1)S(1)} %get-tuple-element.35.turned), custom_call_target="tpu_custom_call" | custom-call | flops 1207959552 | bytes 1572864 | tf_op jit(solution)/shard_map/pallas_call | solution.py:239
  58.9 1.9 %shard_map.42 = (s16[3136,128]{1,0:T(8,128)(2,1)S(1)}, s16[3136,128]{1,0:T(8,128)(2,1)S(1)}) custom-call(bf16[768,512]{1,0:T(8,128)(2,1)S(1)} %get-tuple-element.44.rest, bf16[3072,768]{1,0:T(8,128)(2,1)S(1)} %get-tuple-element.35.turned), custom_call_target="tpu_custom_call" | custom-call | flops 1207959552 | bytes 1572864 | tf_op jit(solution)/shard_map/pallas_call | solution.py:264
  60.9 1.9 %shard_map.38 = s16[784,1024]{1,0:T(8,128)(2,1)S(1)} custom-call(bf16[768,1024]{1,0:T(8,128)(2,1)S(1)} %get-tuple-element.34.bulk, bf16[3072,768]{1,0:T(8,128)(2,1)S(1)} %get-tuple-element.35.turned), custom_call_target="tpu_custom_call" | custom-call | flops 1207959552 | bytes 1572864 | tf_op jit(solution)/shard_map/pallas_call | solution.py:239
  62.8 2.8 %collective-permute-start.13 = (s16[784,1024]{1,0:T(8,128)(2,1)S(1)}, s16[784,1024]{1,0:T(8,128)(2,1)S(1)}, u32[]{:S(2)}, u32[]{:S(2)}) collective-permute-start(s16[784,1024]{1,0:T(8,128)(2,1)S(1)} %shard_map.40), channel_id=1, source_target_pairs={{0,12},{1,13},{2,14},{3,15},{4,0},{5,1},{6,2},{7,3},{8,4},{9,5},{1... | collective-permute-start | bytes 4816904 | tf_op jit(solution)/shard_map/ppermute | solution.py:52
  67.3 3.2 %collective-permute-start.22 = (s16[3136,128]{1,0:T(8,128)(2,1)S(1)}, s16[3136,128]{1,0:T(8,128)(2,1)S(1)}, u32[]{:S(2)}, u32[]{:S(2)}) collective-permute-start(s16[3136,128]{1,0:T(8,128)(2,1)S(1)} %get-tuple-element.46), channel_id=1, source_target_pairs={{0,96},{1,97},{2,98},{3,99},{4,100},{5,101},{6,102},{7,103},{8,104... | collective-permute-start | bytes 2408456 | tf_op jit(solution)/shard_map/ppermute | solution.py:52
  70.5 1.6 %shard_map.43 = s16[3136,128]{1,0:T(8,128)(2,1)S(1)} custom-call(bf16[768,512]{1,0:T(8,128)(2,1)S(1)} %get-tuple-element.44.rest, bf16[3072,768]{1,0:T(8,128)(2,1)S(1)} %get-tuple-element.35.turned), custom_call_target="tpu_custom_call" | custom-call | flops 603979776 | bytes 1572864 | tf_op jit(solution)/shard_map/pallas_call | solution.py:264
  72.1 6.5 %collective-permute-done.20.a = s16[3136,128]{1,0:T(8,128)(2,1)S(1)} collective-permute-done((s16[3136,128]{1,0:T(8,128)(2,1)S(1)}, s16[3136,128]{1,0:T(8,128)(2,1)S(1)}, u32[]{:S(2)}, u32[]{:S(2)}) %collective-permute-start.20) | collective-permute-done | bytes 802848 | tf_op jit(solution)/shard_map/ppermute | solution.py:52
  78.6 1.4 shard_map.41.own
  80.0 1.4 shard_map.37.own
  81.4 18.5 %collective-permute-done.22.d = s16[3136,128]{1,0:T(8,128)(2,1)S(1)} collective-permute-done((s16[3136,128]{1,0:T(8,128)(2,1)S(1)}, s16[3136,128]{1,0:T(8,128)(2,1)S(1)}, u32[]{:S(2)}, u32[]{:S(2)}) %collective-permute-start.22) | collective-permute-done | bytes 802848 | tf_op jit(solution)/shard_map/ppermute | solution.py:52
  100.7 1.6 %collective-permute-start.23 = (s16[208,512]{1,0:T(8,128)(2,1)S(1)}, s16[208,512]{1,0:T(8,128)(2,1)S(1)}, u32[]{:S(2)}, u32[]{:S(2)}) collective-permute-start(s16[208,512]{1,0:T(8,128)(2,1)S(1)} %get-tuple-element.48), channel_id=1, source_target_pairs={{0,1},{1,2},{2,3},{3,0},{4,5},{5,6},{6,7},{7,4},{8,9},{9,10},{10,1... | collective-permute-start | bytes 638984 | tf_op jit(solution)/shard_map/ppermute | solution.py:52
  102.3 8.4 %collective-permute-done.11.a = s16[784,1024]{1,0:T(8,128)(2,1)S(1)} collective-permute-done((s16[784,1024]{1,0:T(8,128)(2,1)S(1)}, s16[784,1024]{1,0:T(8,128)(2,1)S(1)}, u32[]{:S(2)}, u32[]{:S(2)}) %collective-permute-start.11) | collective-permute-done | bytes 1605664 | tf_op jit(solution)/shard_map/ppermute | solution.py:52
  110.7 1.8 %second_sum.2 = (f32[192,1024]{1,0:T(8,128)S(1)}, s16[208,1024]{1,0:T(8,128)(2,1)S(1)}, s16[208,1024]{1,0:T(8,128)(2,1)S(1)}, s16[208,1024]{1,0:T(8,128)(2,1)S(1)}) custom-call(f32[768,1024]{1,0:T(8,128)S(1)} %shard_map.37.own, s16[784,1024]{1,0:T(8,128)(2,1)S(1)} %collective-permute-done.11.a, s16[784,1024]{1,0:T(8,128)(2,1)S(1)} %collective-permute-done.12.b, ...), custom_call_target="tpu_custom_call" | custom-call | flops 12582912 | bytes 7864320 | tf_op jit(solution)/shard_map/second_sum/pallas_call | solution.py:306
  112.5 1.2 collective-permute-start.14
  115.3 3.5 %collective-permute-start.24 = (s16[208,512]{1,0:T(8,128)(2,1)S(1)}, s16[208,512]{1,0:T(8,128)(2,1)S(1)}, u32[]{:S(2)}, u32[]{:S(2)}) collective-permute-start(s16[208,512]{1,0:T(8,128)(2,1)S(1)} %get-tuple-element.49), channel_id=1, source_target_pairs={{0,2},{1,3},{2,0},{3,1},{4,6},{5,7},{6,4},{7,5},{8,10},{9,11},{10,... | collective-permute-start | bytes 638984 | tf_op jit(solution)/shard_map/ppermute | solution.py:52
  118.8 9.2 %collective-permute-done.24.b = s16[208,512]{1,0:T(8,128)(2,1)S(1)} collective-permute-done((s16[208,512]{1,0:T(8,128)(2,1)S(1)}, s16[208,512]{1,0:T(8,128)(2,1)S(1)}, u32[]{:S(2)}, u32[]{:S(2)}) %collective-permute-start.24) | collective-permute-done | bytes 213024 | tf_op jit(solution)/shard_map/ppermute | solution.py:52
  128.0 5.2 %collective-permute-done.25.d = s16[208,512]{1,0:T(8,128)(2,1)S(1)} collective-permute-done((s16[208,512]{1,0:T(8,128)(2,1)S(1)}, s16[208,512]{1,0:T(8,128)(2,1)S(1)}, u32[]{:S(2)}, u32[]{:S(2)}) %collective-permute-start.25) | collective-permute-done | bytes 213024 | tf_op jit(solution)/shard_map/ppermute | solution.py:52
  134.1 4.9 %collective-permute-start.18 = (s16[208,256]{1,0:T(8,128)(2,1)S(1)}, s16[208,256]{1,0:T(8,128)(2,1)S(1)}, u32[]{:S(2)}, u32[]{:S(2)}) collective-permute-start(s16[208,256]{1,0:T(8,128)(2,1)S(1)} %get-tuple-element.42), channel_id=1, source_target_pairs={{0,64},{1,65},{2,66},{3,67},{4,68},{5,69},{6,70},{7,71},{8,72},{9,... | collective-permute-start | bytes 319496 | tf_op jit(solution)/shard_map/ppermute | solution.py:52
  140.8 2.1 %collective-permute-start.28 = (s16[208,128]{1,0:T(8,128)(2,1)S(1)}, s16[208,128]{1,0:T(8,128)(2,1)S(1)}, u32[]{:S(2)}, u32[]{:S(2)}) collective-permute-start(s16[208,128]{1,0:T(8,128)(2,1)S(1)} %get-tuple-element.54), channel_id=1, source_target_pairs={{0,12},{1,13},{2,14},{3,15},{4,0},{5,1},{6,2},{7,3},{8,4},{9,5},{1... | collective-permute-start | bytes 159752 | tf_op jit(solution)/shard_map/ppermute | solution.py:52
  143.0 2.4 %collective-permute-done.27.rb = s16[208,128]{1,0:T(8,128)(2,1)S(1)} collective-permute-done((s16[208,128]{1,0:T(8,128)(2,1)S(1)}, s16[208,128]{1,0:T(8,128)(2,1)S(1)}, u32[]{:S(2)}, u32[]{:S(2)}) %collective-permute-start.27) | collective-permute-done | bytes 53280 | tf_op jit(solution)/shard_map/ppermute | solution.py:52
  (49 shorter events, 12.2 us)
Async XLA Ops:
  0.0 0.7 copy-start.1
  0.7 34.9 %copy-start = (bf16[16,128]{1,0:T(8,128)(2,1)S(1)}, bf16[16,128]{1,0:T(8,128)(2,1)}, u32[]{:S(2)}) copy-start(bf16[16,128]{1,0:T(8,128)(2,1)} %after.3) | copy-start | bytes 12292
  3.8 17.4 %collective-permute-start.1 = (bf16[6,16,3072]{2,1,0:T(8,128)(2,1)S(1)}, bf16[6,16,3072]{2,1,0:T(8,128)(2,1)S(1)}, u32[]{:S(2)}, u32[]{:S(2)}) collective-permute-start(bf16[6,16,3072]{2,1,0:T(8,128)(2,1)S(1)} %get-tuple-element.31), channel_id=1, source_target_pairs={{0,32},{1,33},{2,34},{3,35},{4,36},{5,37},{6,38},{7,39},{8,40},{9,... | collective-permute-start | bytes 1769480 | tf_op jit(solution)/shard_map/ppermute | solution.py:52
  5.8 29.3 %collective-permute-start.3 = (bf16[6,16,3072]{2,1,0:T(8,128)(2,1)S(1)}, bf16[6,16,3072]{2,1,0:T(8,128)(2,1)S(1)}, u32[]{:S(2)}, u32[]{:S(2)}) collective-permute-start(bf16[6,16,3072]{2,1,0:T(8,128)(2,1)S(1)} %get-tuple-element.32), channel_id=1, source_target_pairs={{0,64},{1,65},{2,66},{3,67},{4,68},{5,69},{6,70},{7,71},{8,72},{9,... | collective-permute-start | bytes 1769480 | tf_op jit(solution)/shard_map/ppermute | solution.py:52
  9.4 25.7 %collective-permute-start.5 = (bf16[6,16,3072]{2,1,0:T(8,128)(2,1)S(1)}, bf16[6,16,3072]{2,1,0:T(8,128)(2,1)S(1)}, u32[]{:S(2)}, u32[]{:S(2)}) collective-permute-start(bf16[6,16,3072]{2,1,0:T(8,128)(2,1)S(1)} %get-tuple-element.33), channel_id=1, source_target_pairs={{0,96},{1,97},{2,98},{3,99},{4,100},{5,101},{6,102},{7,103},{8,104... | collective-permute-start | bytes 1769480 | tf_op jit(solution)/shard_map/ppermute | solution.py:52
  10.4 41.4 %collective-permute-start = (bf16[6,16,3072]{2,1,0:T(8,128)(2,1)S(1)}, bf16[6,16,3072]{2,1,0:T(8,128)(2,1)S(1)}, u32[]{:S(2)}, u32[]{:S(2)}) collective-permute-start(bf16[6,16,3072]{2,1,0:T(8,128)(2,1)S(1)} %get-tuple-element.30.refs_0_), channel_id=1, source_target_pairs={{0,16},{1,17},{2,18},{3,19},{4,20},{5,21},{6,22},{7,23},{8,24},{9,... | collective-permute-start | bytes 1769480 | tf_op jit(solution)/shard_map/ppermute | solution.py:52
  21.2 30.5 %collective-permute-start.2 = (bf16[6,16,3072]{2,1,0:T(8,128)(2,1)S(1)}, bf16[6,16,3072]{2,1,0:T(8,128)(2,1)S(1)}, u32[]{:S(2)}, u32[]{:S(2)}) collective-permute-start(bf16[6,16,3072]{2,1,0:T(8,128)(2,1)S(1)} %collective-permute-done.1.refs_2_), channel_id=1, source_target_pairs={{0,16},{1,17},{2,18},{3,19},{4,20},{5,21},{6,22},{7,23},{8,24},{9,... | collective-permute-start | bytes 1769480 | tf_op jit(solution)/shard_map/ppermute | solution.py:52
  35.0 16.7 %collective-permute-start.4 = (bf16[6,16,3072]{2,1,0:T(8,128)(2,1)S(1)}, bf16[6,16,3072]{2,1,0:T(8,128)(2,1)S(1)}, u32[]{:S(2)}, u32[]{:S(2)}) collective-permute-start(bf16[6,16,3072]{2,1,0:T(8,128)(2,1)S(1)} %collective-permute-done.3.refs_4_), channel_id=1, source_target_pairs={{0,16},{1,17},{2,18},{3,19},{4,20},{5,21},{6,22},{7,23},{8,24},{9,... | collective-permute-start | bytes 1769480 | tf_op jit(solution)/shard_map/ppermute | solution.py:52
  35.0 16.7 %collective-permute-start.6 = (bf16[6,16,3072]{2,1,0:T(8,128)(2,1)S(1)}, bf16[6,16,3072]{2,1,0:T(8,128)(2,1)S(1)}, u32[]{:S(2)}, u32[]{:S(2)}) collective-permute-start(bf16[6,16,3072]{2,1,0:T(8,128)(2,1)S(1)} %collective-permute-done.5.refs_6_), channel_id=1, source_target_pairs={{0,16},{1,17},{2,18},{3,19},{4,20},{5,21},{6,22},{7,23},{8,24},{9,... | collective-permute-start | bytes 1769480 | tf_op jit(solution)/shard_map/ppermute | solution.py:52
  35.6 2.3 %collective-permute-start.7 = (bf16[16,128]{1,0:T(8,128)(2,1)S(1)}, bf16[16,128]{1,0:T(8,128)(2,1)S(1)}, u32[]{:S(2)}, u32[]{:S(2)}) collective-permute-start(bf16[16,128]{1,0:T(8,128)(2,1)S(1)} %copy-done), channel_id=1, source_target_pairs={{0,16},{1,17},{2,18},{3,19},{4,20},{5,21},{6,22},{7,23},{8,24},{9,... | collective-permute-start | bytes 12296 | tf_op jit(solution)/shard_map/ppermute | solution.py:52
  37.9 3.7 %collective-permute-start.10 = (bf16[32,128]{1,0:T(8,128)(2,1)S(1)}, bf16[32,128]{1,0:T(8,128)(2,1)S(1)}, u32[]{:S(2)}, u32[]{:S(2)}) collective-permute-start(bf16[32,128]{1,0:T(8,128)(2,1)S(1)} %constant_dynamic-update-slice_fusion.refs_0_), channel_id=1, source_target_pairs={{0,96},{1,97},{2,98},{3,99},{4,100},{5,101},{6,102},{7,103},{8,104... | collective-permute-start | bytes 24584 | tf_op jit(solution)/shard_map/ppermute | solution.py:52
  41.6 4.9 %collective-permute-start.8 = (bf16[32,128]{1,0:T(8,128)(2,1)S(1)}, bf16[32,128]{1,0:T(8,128)(2,1)S(1)}, u32[]{:S(2)}, u32[]{:S(2)}) collective-permute-start(bf16[32,128]{1,0:T(8,128)(2,1)S(1)} %constant_dynamic-update-slice_fusion.refs_0_), channel_id=1, source_target_pairs={{0,32},{1,33},{2,34},{3,35},{4,36},{5,37},{6,38},{7,39},{8,40},{9,... | collective-permute-start | bytes 24584 | tf_op jit(solution)/shard_map/ppermute | solution.py:52
  46.4 5.2 %collective-permute-start.9 = (bf16[32,128]{1,0:T(8,128)(2,1)S(1)}, bf16[32,128]{1,0:T(8,128)(2,1)S(1)}, u32[]{:S(2)}, u32[]{:S(2)}) collective-permute-start(bf16[32,128]{1,0:T(8,128)(2,1)S(1)} %constant_dynamic-update-slice_fusion.refs_0_), channel_id=1, source_target_pairs={{0,64},{1,65},{2,66},{3,67},{4,68},{5,69},{6,70},{7,71},{8,72},{9,... | collective-permute-start | bytes 24584 | tf_op jit(solution)/shard_map/ppermute | solution.py:52
  60.8 17.8 %collective-permute-start.20 = (s16[3136,128]{1,0:T(8,128)(2,1)S(1)}, s16[3136,128]{1,0:T(8,128)(2,1)S(1)}, u32[]{:S(2)}, u32[]{:S(2)}) collective-permute-start(s16[3136,128]{1,0:T(8,128)(2,1)S(1)} %get-tuple-element.45), channel_id=1, source_target_pairs={{0,32},{1,33},{2,34},{3,35},{4,36},{5,37},{6,38},{7,39},{8,40},{9,... | collective-permute-start | bytes 2408456 | tf_op jit(solution)/shard_map/ppermute | solution.py:52
  62.8 39.5 %collective-permute-start.13 = (s16[784,1024]{1,0:T(8,128)(2,1)S(1)}, s16[784,1024]{1,0:T(8,128)(2,1)S(1)}, u32[]{:S(2)}, u32[]{:S(2)}) collective-permute-start(s16[784,1024]{1,0:T(8,128)(2,1)S(1)} %shard_map.40), channel_id=1, source_target_pairs={{0,12},{1,13},{2,14},{3,15},{4,0},{5,1},{6,2},{7,3},{8,4},{9,5},{1... | collective-permute-start | bytes 4816904 | tf_op jit(solution)/shard_map/ppermute | solution.py:52
  65.6 36.7 %collective-permute-start.12 = (s16[784,1024]{1,0:T(8,128)(2,1)S(1)}, s16[784,1024]{1,0:T(8,128)(2,1)S(1)}, u32[]{:S(2)}, u32[]{:S(2)}) collective-permute-start(s16[784,1024]{1,0:T(8,128)(2,1)S(1)} %shard_map.39), channel_id=1, source_target_pairs={{0,8},{1,9},{2,10},{3,11},{4,12},{5,13},{6,14},{7,15},{8,0},{9,1},... | collective-permute-start | bytes 4816904 | tf_op jit(solution)/shard_map/ppermute | solution.py:52
  66.4 44.3 %collective-permute-start.11 = (s16[784,1024]{1,0:T(8,128)(2,1)S(1)}, s16[784,1024]{1,0:T(8,128)(2,1)S(1)}, u32[]{:S(2)}, u32[]{:S(2)}) collective-permute-start(s16[784,1024]{1,0:T(8,128)(2,1)S(1)} %shard_map.38), channel_id=1, source_target_pairs={{0,4},{1,5},{2,6},{3,7},{4,8},{5,9},{6,10},{7,11},{8,12},{9,13},{1... | collective-permute-start | bytes 4816904 | tf_op jit(solution)/shard_map/ppermute | solution.py:52
  67.3 32.5 %collective-permute-start.22 = (s16[3136,128]{1,0:T(8,128)(2,1)S(1)}, s16[3136,128]{1,0:T(8,128)(2,1)S(1)}, u32[]{:S(2)}, u32[]{:S(2)}) collective-permute-start(s16[3136,128]{1,0:T(8,128)(2,1)S(1)} %get-tuple-element.46), channel_id=1, source_target_pairs={{0,96},{1,97},{2,98},{3,99},{4,100},{5,101},{6,102},{7,103},{8,104... | collective-permute-start | bytes 2408456 | tf_op jit(solution)/shard_map/ppermute | solution.py:52
  78.6 21.2 %collective-permute-start.21 = (s16[3136,128]{1,0:T(8,128)(2,1)S(1)}, s16[3136,128]{1,0:T(8,128)(2,1)S(1)}, u32[]{:S(2)}, u32[]{:S(2)}) collective-permute-start(s16[3136,128]{1,0:T(8,128)(2,1)S(1)} %shard_map.43), channel_id=1, source_target_pairs={{0,64},{1,65},{2,66},{3,67},{4,68},{5,69},{6,70},{7,71},{8,72},{9,... | collective-permute-start | bytes 2408456 | tf_op jit(solution)/shard_map/ppermute | solution.py:52
  100.7 18.0 %collective-permute-start.23 = (s16[208,512]{1,0:T(8,128)(2,1)S(1)}, s16[208,512]{1,0:T(8,128)(2,1)S(1)}, u32[]{:S(2)}, u32[]{:S(2)}) collective-permute-start(s16[208,512]{1,0:T(8,128)(2,1)S(1)} %get-tuple-element.48), channel_id=1, source_target_pairs={{0,1},{1,2},{2,3},{3,0},{4,5},{5,6},{6,7},{7,4},{8,9},{9,10},{10,1... | collective-permute-start | bytes 638984 | tf_op jit(solution)/shard_map/ppermute | solution.py:52
  112.5 21.0 %collective-permute-start.14 = (s16[208,1024]{1,0:T(8,128)(2,1)S(1)}, s16[208,1024]{1,0:T(8,128)(2,1)S(1)}, u32[]{:S(2)}, u32[]{:S(2)}) collective-permute-start(s16[208,1024]{1,0:T(8,128)(2,1)S(1)} %get-tuple-element.37), channel_id=1, source_target_pairs={{0,1},{1,2},{2,3},{3,0},{4,5},{5,6},{6,7},{7,4},{8,9},{9,10},{10,1... | collective-permute-start | bytes 1277960 | tf_op jit(solution)/shard_map/ppermute | solution.py:52
  113.7 19.8 %collective-permute-start.15 = (s16[208,1024]{1,0:T(8,128)(2,1)S(1)}, s16[208,1024]{1,0:T(8,128)(2,1)S(1)}, u32[]{:S(2)}, u32[]{:S(2)}) collective-permute-start(s16[208,1024]{1,0:T(8,128)(2,1)S(1)} %get-tuple-element.38), channel_id=1, source_target_pairs={{0,2},{1,3},{2,0},{3,1},{4,6},{5,7},{6,4},{7,5},{8,10},{9,11},{10,... | collective-permute-start | bytes 1277960 | tf_op jit(solution)/shard_map/ppermute | solution.py:52
  114.4 19.1 %collective-permute-start.16 = (s16[208,1024]{1,0:T(8,128)(2,1)S(1)}, s16[208,1024]{1,0:T(8,128)(2,1)S(1)}, u32[]{:S(2)}, u32[]{:S(2)}) collective-permute-start(s16[208,1024]{1,0:T(8,128)(2,1)S(1)} %get-tuple-element.39), channel_id=1, source_target_pairs={{0,3},{1,0},{2,1},{3,2},{4,7},{5,4},{6,5},{7,6},{8,11},{9,8},{10,9... | collective-permute-start | bytes 1277960 | tf_op jit(solution)/shard_map/ppermute | solution.py:52
  115.3 12.7 %collective-permute-start.24 = (s16[208,512]{1,0:T(8,128)(2,1)S(1)}, s16[208,512]{1,0:T(8,128)(2,1)S(1)}, u32[]{:S(2)}, u32[]{:S(2)}) collective-permute-start(s16[208,512]{1,0:T(8,128)(2,1)S(1)} %get-tuple-element.49), channel_id=1, source_target_pairs={{0,2},{1,3},{2,0},{3,1},{4,6},{5,7},{6,4},{7,5},{8,10},{9,11},{10,... | collective-permute-start | bytes 638984 | tf_op jit(solution)/shard_map/ppermute | solution.py:52
  118.8 14.4 %collective-permute-start.25 = (s16[208,512]{1,0:T(8,128)(2,1)S(1)}, s16[208,512]{1,0:T(8,128)(2,1)S(1)}, u32[]{:S(2)}, u32[]{:S(2)}) collective-permute-start(s16[208,512]{1,0:T(8,128)(2,1)S(1)} %get-tuple-element.50), channel_id=1, source_target_pairs={{0,3},{1,0},{2,1},{3,2},{4,7},{5,4},{6,5},{7,6},{8,11},{9,8},{10,9... | collective-permute-start | bytes 638984 | tf_op jit(solution)/shard_map/ppermute | solution.py:52
  133.4 7.4 %collective-permute-start.26 = (s16[208,128]{1,0:T(8,128)(2,1)S(1)}, s16[208,128]{1,0:T(8,128)(2,1)S(1)}, u32[]{:S(2)}, u32[]{:S(2)}) collective-permute-start(s16[208,128]{1,0:T(8,128)(2,1)S(1)} %get-tuple-element.52), channel_id=1, source_target_pairs={{0,4},{1,5},{2,6},{3,7},{4,8},{5,9},{6,10},{7,11},{8,12},{9,13},{1... | collective-permute-start | bytes 159752 | tf_op jit(solution)/shard_map/ppermute | solution.py:52
  134.0 12.5 %collective-permute-start.17 = (s16[208,256]{1,0:T(8,128)(2,1)S(1)}, s16[208,256]{1,0:T(8,128)(2,1)S(1)}, u32[]{:S(2)}, u32[]{:S(2)}) collective-permute-start(s16[208,256]{1,0:T(8,128)(2,1)S(1)} %get-tuple-element.41), channel_id=1, source_target_pairs={{0,32},{1,33},{2,34},{3,35},{4,36},{5,37},{6,38},{7,39},{8,40},{9,... | collective-permute-start | bytes 319496 | tf_op jit(solution)/shard_map/ppermute | solution.py:52
  134.1 12.4 %collective-permute-start.18 = (s16[208,256]{1,0:T(8,128)(2,1)S(1)}, s16[208,256]{1,0:T(8,128)(2,1)S(1)}, u32[]{:S(2)}, u32[]{:S(2)}) collective-permute-start(s16[208,256]{1,0:T(8,128)(2,1)S(1)} %get-tuple-element.42), channel_id=1, source_target_pairs={{0,64},{1,65},{2,66},{3,67},{4,68},{5,69},{6,70},{7,71},{8,72},{9,... | collective-permute-start | bytes 319496 | tf_op jit(solution)/shard_map/ppermute | solution.py:52
  139.0 7.5 %collective-permute-start.19 = (s16[208,256]{1,0:T(8,128)(2,1)S(1)}, s16[208,256]{1,0:T(8,128)(2,1)S(1)}, u32[]{:S(2)}, u32[]{:S(2)}) collective-permute-start(s16[208,256]{1,0:T(8,128)(2,1)S(1)} %get-tuple-element.43), channel_id=1, source_target_pairs={{0,96},{1,97},{2,98},{3,99},{4,100},{5,101},{6,102},{7,103},{8,104... | collective-permute-start | bytes 319496 | tf_op jit(solution)/shard_map/ppermute | solution.py:52
  139.7 5.6 %collective-permute-start.27 = (s16[208,128]{1,0:T(8,128)(2,1)S(1)}, s16[208,128]{1,0:T(8,128)(2,1)S(1)}, u32[]{:S(2)}, u32[]{:S(2)}) collective-permute-start(s16[208,128]{1,0:T(8,128)(2,1)S(1)} %get-tuple-element.53), channel_id=1, source_target_pairs={{0,8},{1,9},{2,10},{3,11},{4,12},{5,13},{6,14},{7,15},{8,0},{9,1},... | collective-permute-start | bytes 159752 | tf_op jit(solution)/shard_map/ppermute | solution.py:52
  140.8 5.6 %collective-permute-start.28 = (s16[208,128]{1,0:T(8,128)(2,1)S(1)}, s16[208,128]{1,0:T(8,128)(2,1)S(1)}, u32[]{:S(2)}, u32[]{:S(2)}) collective-permute-start(s16[208,128]{1,0:T(8,128)(2,1)S(1)} %get-tuple-element.54), channel_id=1, source_target_pairs={{0,12},{1,13},{2,14},{3,15},{4,0},{5,1},{6,2},{7,3},{8,4},{9,5},{1... | collective-permute-start | bytes 159752 | tf_op jit(solution)/shard_map/ppermute | solution.py:52

commit v6 on v5

--- a/solution.py
+++ b/solution.py
@@ -221,29 +221,41 @@
         out[end:end + TAIL, :] = marked(e)
 
 
-def bulk_body(shift, bulk, turned, out):
+def bulk_body(blocks, bulk, turned, *refs):
     at = position()
     total = turned.shape[0] // RING
-    g = lax.rem(jnp.where(at[1] == 0, at[2], at[3]) + shift, RING)
-    left = turned[pl.ds(pl.multiple_of(g * total, 256), total), :]
-    half = bulk.shape[1] // 2
-    for n in range(2):
-        lanes = slice(n * half, (n + 1) * half)
-        write(out.at[:, lanes], 0, jnp.dot(left, bulk[:, lanes], preferred_element_type=F32))
-
-
-def bulk_k(bulk, turned, shift):
+    own = jnp.where(at[1] == 0, at[2], at[3])
+    outs = refs[len(refs) - len(blocks):]
+    arrived = iter(refs)
+    wide = bulk.shape[1] // 2
+    for (shift, half, adds), out in zip(blocks, outs):
+        rows = total if half is None else total // 2
+        first = lax.rem(own + shift, RING) * total + (0 if half is None else half * rows)
+        left = turned[pl.ds(pl.multiple_of(first, 128), rows), :]
+        part = next(arrived) if adds else None
+        for n in range(2):
+            lanes = slice(n * wide, (n + 1) * wide)
+            block = jnp.dot(left, bulk[:, lanes], preferred_element_type=F32)
+            if adds:
+                block = block + plain(part[:rows, lanes]) * scale_of(part[rows:, lanes])
+            write(out.at[:, lanes], 0, block)
+
+
+def bulk_k(bulk, turned, blocks, arrived=()):
     depth, columns = bulk.shape
     total = turned.shape[0] // RING
-    shape = (total + (TAIL if shift else 0), columns)
-    return pl.pallas_call(
-        functools.partial(bulk_body, shift),
-        out_shape=jax.ShapeDtypeStruct(shape, I16 if shift else F32),
-        in_specs=[whole(), whole()],
-        out_specs=whole(),
+    sizes = [total if half is None else total // 2 for _, half, _ in blocks]
+    return pl.pallas_call(
+        functools.partial(bulk_body, blocks),
+        out_shape=[
+            jax.ShapeDtypeStruct((n + (TAIL if shift else 0), columns), I16 if shift else F32)
+            for n, (shift, _, _) in zip(sizes, blocks)
+        ],
+        in_specs=[whole()] * (2 + len(arrived)),
+        out_specs=[whole()] * len(blocks),
         compiler_params=params(28),
-        cost_estimate=cost(2 * depth * total * columns, total * columns * 2),
-    )(bulk, turned)
+        cost_estimate=cost(2 * depth * sum(sizes) * columns, sum(sizes) * columns * 2),
+    )(bulk, turned, *arrived)
 
 
 def rest_body(first, rest, turned, *outs):
@@ -315,6 +327,47 @@
     )(*parts, after))
 
 
+def bulk_second_body(own, a, b, d, e, after, kept, *outs):
+    at = position()
+    high = kept.shape[0]
+    h = jnp.where(at[1] == 0, at[3], at[2])
+    half = own.shape[0] // 2
+    step = 256
+    for k in range(RING):
+        block = lax.rem(h + k, RING)
+        out = kept if k == 0 else outs[k - 1]
+
+        def part(upper, arrived, block=block, out=out):
+            @pl.when((block < RING // 2) == upper)
+            def _():
+                row = pl.multiple_of(lax.rem(block, RING // 2) * high, 64)
+                first = pl.multiple_of(block * high, 64)
+                for lane in range(0, own.shape[1], step):
+                    lanes = slice(lane, lane + step)
+                    v = own[pl.ds(first, high), lanes]
+                    for m in arrived:
+                        v = v + plain(m[pl.ds(row, high), lanes]) * scale_of(m[half:, lanes])
+                    write(out.at[:, lanes], 0, v)
+
+        part(True, (a, b))
+        part(False, (d, e))
+
+
+def bulk_second(own, upper, lower, after):
+    total, columns = own.shape
+    high = total // RING
+    return list(pl.pallas_call(
+        bulk_second_body,
+        out_shape=[jax.ShapeDtypeStruct((high, columns), F32)]
+        + [jax.ShapeDtypeStruct((high + TAIL, columns), I16)] * 3,
+        in_specs=[whole()] * 6,
+        out_specs=[whole()] * 4,
+        compiler_params=params(24),
+        cost_estimate=cost(total * columns * 12, total * columns * 8),
+        name="bulk_second_sum",
+    )(own, *upper, *lower, after))
+
+
 def third_body(by_z, own, a, b, d, after, *outs):
     at = position()
     high, step = outs[0].shape
@@ -388,12 +441,15 @@
     there = [send(v, other_core) for v in here]
     bulk_rows, rest_rows, turned = fit([v for both in zip(here, there) for v in both], mixed)
 
-    bulk, rest = [None] * 4, [None] * 4
-
-    def bulk_step(k):
-        bulk[k] = bulk_k(bulk_rows, turned, k)
-        if k:
-            bulk[k] = send(bulk[k], first_axis(k))
+    rest = [None] * 4
+
+    def bulk_step(*blocks, arrived=()):
+        return bulk_k(bulk_rows, turned, blocks, arrived)
+
+    def near(up, down):
+        up = send(up, first_axis(1))
+        down = send(down, first_axis(3))
+        return up, down
 
     def rest_step(first, last):
         out = rest_k(rest_rows, turned, first, last)
@@ -404,23 +460,24 @@
         for k in ORDER[:3]:
             parts[k] = send(parts[k], shift(k))
 
+    far = near(*bulk_step((2, 0, False), (2, 1, False)))
     rest_step(0, 1)
-    bulk_step(2)
+    lower_up, upper_down = near(*bulk_step((1, 1, False), (3, 0, False)))
     rest_step(1, 3)
-    bulk_step(1)
-    bulk_step(3)
+    upper_up, lower_down = near(*bulk_step((1, 0, True), (3, 1, True), arrived=far))
     rest_step(3, 4)
-    bulk_step(0)
-    rest = second(rest, RING, metric)
+    own = bulk_step((0, None, False))[0]
+    bulk = bulk_second(own, (upper_up, upper_down), (lower_up, lower_down), metric)
+    onward(bulk, second_axis)
+    then = tick(metric)
+    rest = second(rest, RING, then)
     onward(rest, second_axis)
-    then = tick(metric)
-    bulk = second(bulk, 1, then)
-    onward(bulk, second_axis)
-    rest = third(rest, False, metric)
-    onward(rest, first_axis)
     then = tick(then)
     bulk = third(bulk, True, then)
     onward(bulk, along_z)
+    then = tick(then)
+    rest = third(rest, False, then)
+    onward(rest, first_axis)
     return finish(bulk, rest)
 
 

time: 147 us -> 139 us (0.946)
  the two profiles are of different devices: /device:TPU:16 before, /device:TPU:48 now
where the time goes in v6:
time: 139 us
  waiting for transfers between devices  62.3 us (45%)
  starting transfers between devices  54.2 us (39%)
  Pallas kernels  21.8 us (16%)
    ppermute x32, waiting for transfers between devices, send(): return lax.ppermute(v, AXES, moves(shift))  62.3 us
    ppermute x32, starting transfers between devices, send(): return lax.ppermute(v, AXES, moves(shift))  54.2 us
    pallas_call x4, Pallas kernels, bulk_k(): pl.pallas_call(functools.partial(bulk_body, blocks), out_shape=[jax.Shape...  6.57 us
    pallas_call x3, Pallas kernels, rest_k(): pl.pallas_call(functools.partial(rest_body, first), out_shape=[jax.ShapeD...  4.86 us
    pallas_call x1, Pallas kernels, fit(): pl.pallas_call(fit_body, grid=(group,), out_shape=[jax.ShapeDtypeStruct((...  3.31 us
    pallas_call x1, Pallas kernels, screen(): pl.pallas_call(screen_body, out_shape=[out] * RING, in_specs=[scalars(),...  3.12 us
  transfers between devices with their start and end apart: 32, of which 13 were waited for; matrix products, arithmetic and copies ran while one was open for 0% of the time, Pallas kernels for 9%

profile of v6, /device:TPU:48, one launch (start us, length us, event | category | flops | bytes accessed | tf_op | source)
XLA Modules:
  0.0 139.2 jit_solution(8198549248582573521)
XLA Ops:
  0.7 3.1 %screen.1 = (bf16[6,16,3072]{2,1,0:T(8,128)(2,1)S(1)}, bf16[6,16,3072]{2,1,0:T(8,128)(2,1)S(1)}, bf16[6,16,3072]{2,1,0:T(8,128)(2,1)S(1)}, bf16[6,16,3072]{2,1,0:T(8,128)(2,1)S(1)}) custom-call(s32[1,1,24]{2,1,0:T(1,128)S(1)} %copy-done.1, bf16[16,24,3072]{2,1,0:T(8,128)(2,1)} %half.1), custom_call_target="tpu_custom_call" | custom-call | flops 1179648 | bytes 4718592 | tf_op jit(solution)/shard_map/screen/pallas_call | solution.py:105
  3.8 2.0 %collective-permute-start.1 = (bf16[6,16,3072]{2,1,0:T(8,128)(2,1)S(1)}, bf16[6,16,3072]{2,1,0:T(8,128)(2,1)S(1)}, u32[]{:S(2)}, u32[]{:S(2)}) collective-permute-start(bf16[6,16,3072]{2,1,0:T(8,128)(2,1)S(1)} %get-tuple-element.37), channel_id=1, source_target_pairs={{0,32},{1,33},{2,34},{3,35},{4,36},{5,37},{6,38},{7,39},{8,40},{9,... | collective-permute-start | bytes 1769480 | tf_op jit(solution)/shard_map/ppermute | solution.py:52
  6.9 2.5 %collective-permute-start.5 = (bf16[6,16,3072]{2,1,0:T(8,128)(2,1)S(1)}, bf16[6,16,3072]{2,1,0:T(8,128)(2,1)S(1)}, u32[]{:S(2)}, u32[]{:S(2)}) collective-permute-start(bf16[6,16,3072]{2,1,0:T(8,128)(2,1)S(1)} %get-tuple-element.39), channel_id=1, source_target_pairs={{0,96},{1,97},{2,98},{3,99},{4,100},{5,101},{6,102},{7,103},{8,104... | collective-permute-start | bytes 1769480 | tf_op jit(solution)/shard_map/ppermute | solution.py:52
  9.5 21.6 %collective-permute-done.1.refs_2_ = bf16[6,16,3072]{2,1,0:T(8,128)(2,1)S(1)} collective-permute-done((bf16[6,16,3072]{2,1,0:T(8,128)(2,1)S(1)}, bf16[6,16,3072]{2,1,0:T(8,128)(2,1)S(1)}, u32[]{:S(2)}, u32[]{:S(2)}) %collective-permute-start.1) | collective-permute-done | bytes 589856 | tf_op jit(solution)/shard_map/ppermute | solution.py:52
  31.6 2.8 %collective-permute-done.5.refs_6_ = bf16[6,16,3072]{2,1,0:T(8,128)(2,1)S(1)} collective-permute-done((bf16[6,16,3072]{2,1,0:T(8,128)(2,1)S(1)}, bf16[6,16,3072]{2,1,0:T(8,128)(2,1)S(1)}, u32[]{:S(2)}, u32[]{:S(2)}) %collective-permute-start.5) | collective-permute-done | bytes 589856 | tf_op jit(solution)/shard_map/ppermute | solution.py:52
  36.4 1.6 %collective-permute-start.10 = (bf16[32,128]{1,0:T(8,128)(2,1)S(1)}, bf16[32,128]{1,0:T(8,128)(2,1)S(1)}, u32[]{:S(2)}, u32[]{:S(2)}) collective-permute-start(bf16[32,128]{1,0:T(8,128)(2,1)S(1)} %constant_dynamic-update-slice_fusion.refs_0_), channel_id=1, source_target_pairs={{0,96},{1,97},{2,98},{3,99},{4,100},{5,101},{6,102},{7,103},{8,104... | collective-permute-start | bytes 24584 | tf_op jit(solution)/shard_map/ppermute | solution.py:52
  38.0 2.0 %collective-permute-done.10.refs_3_ = bf16[32,128]{1,0:T(8,128)(2,1)S(1)} collective-permute-done((bf16[32,128]{1,0:T(8,128)(2,1)S(1)}, bf16[32,128]{1,0:T(8,128)(2,1)S(1)}, u32[]{:S(2)}, u32[]{:S(2)}) %collective-permute-start.10) | collective-permute-done | bytes 8224 | tf_op jit(solution)/shard_map/ppermute | solution.py:52
  41.0 2.7 %collective-permute-done.8.refs_1_ = bf16[32,128]{1,0:T(8,128)(2,1)S(1)} collective-permute-done((bf16[32,128]{1,0:T(8,128)(2,1)S(1)}, bf16[32,128]{1,0:T(8,128)(2,1)S(1)}, u32[]{:S(2)}, u32[]{:S(2)}) %collective-permute-start.8) | collective-permute-done | bytes 8224 | tf_op jit(solution)/shard_map/ppermute | solution.py:52
  43.7 3.0 %collective-permute-start.9 = (bf16[32,128]{1,0:T(8,128)(2,1)S(1)}, bf16[32,128]{1,0:T(8,128)(2,1)S(1)}, u32[]{:S(2)}, u32[]{:S(2)}) collective-permute-start(bf16[32,128]{1,0:T(8,128)(2,1)S(1)} %constant_dynamic-update-slice_fusion.refs_0_), channel_id=1, source_target_pairs={{0,64},{1,65},{2,66},{3,67},{4,68},{5,69},{6,70},{7,71},{8,72},{9,... | collective-permute-start | bytes 24584 | tf_op jit(solution)/shard_map/ppermute | solution.py:52
  46.7 2.2 %collective-permute-done.9.refs_2_ = bf16[32,128]{1,0:T(8,128)(2,1)S(1)} collective-permute-done((bf16[32,128]{1,0:T(8,128)(2,1)S(1)}, bf16[32,128]{1,0:T(8,128)(2,1)S(1)}, u32[]{:S(2)}, u32[]{:S(2)}) %collective-permute-start.9) | collective-permute-done | bytes 8224 | tf_op jit(solution)/shard_map/ppermute | solution.py:52
  49.0 3.3 %fit.1 = (bf16[768,1024]{1,0:T(8,128)(2,1)S(1)}, bf16[768,512]{1,0:T(8,128)(2,1)S(1)}, bf16[3072,768]{1,0:T(8,128)(2,1)S(1)}) custom-call(bf16[6,16,3072]{2,1,0:T(8,128)(2,1)S(1)} %get-tuple-element.36.refs_0_, bf16[6,16,3072]{2,1,0:T(8,128)(2,1)S(1)} %collective-permute-done.refs_1_, bf16[6,16,3072]{2,1,0:T(8,128)(2,1)S(1)} %collective-permute-done.1.refs_2_, ...), custom_call_target="tpu_custom_call" | custom-call | flops 603979776 | bytes 14155776 | tf_op jit(solution)/shard_map/fit/pallas_call | solution.py:179
  52.3 1.7 %shard_map.38 = (s16[400,1024]{1,0:T(8,128)(2,1)S(1)}, s16[400,1024]{1,0:T(8,128)(2,1)S(1)}) custom-call(bf16[768,1024]{1,0:T(8,128)(2,1)S(1)} %get-tuple-element.40.bulk, bf16[3072,768]{1,0:T(8,128)(2,1)S(1)} %get-tuple-element.41.turned), custom_call_target="tpu_custom_call" | custom-call | flops 1207959552 | bytes 1572864 | tf_op jit(solution)/shard_map/pallas_call | solution.py:248
  55.6 1.7 %collective-permute-start.12 = (s16[400,1024]{1,0:T(8,128)(2,1)S(1)}, s16[400,1024]{1,0:T(8,128)(2,1)S(1)}, u32[]{:S(2)}, u32[]{:S(2)}) collective-permute-start(s16[400,1024]{1,0:T(8,128)(2,1)S(1)} %get-tuple-element.43), channel_id=1, source_target_pairs={{0,12},{1,13},{2,14},{3,15},{4,0},{5,1},{6,2},{7,3},{8,4},{9,5},{1... | collective-permute-start | bytes 2457608 | tf_op jit(solution)/shard_map/ppermute | solution.py:52
  57.4 1.9 %shard_map.42 = (s16[3136,128]{1,0:T(8,128)(2,1)S(1)}, s16[3136,128]{1,0:T(8,128)(2,1)S(1)}) custom-call(bf16[768,512]{1,0:T(8,128)(2,1)S(1)} %get-tuple-element.56.rest, bf16[3072,768]{1,0:T(8,128)(2,1)S(1)} %get-tuple-element.41.turned), custom_call_target="tpu_custom_call" | custom-call | flops 1207959552 | bytes 1572864 | tf_op jit(solution)/shard_map/pallas_call | solution.py:276
  60.6 1.7 %collective-permute-start.25 = (s16[3136,128]{1,0:T(8,128)(2,1)S(1)}, s16[3136,128]{1,0:T(8,128)(2,1)S(1)}, u32[]{:S(2)}, u32[]{:S(2)}) collective-permute-start(s16[3136,128]{1,0:T(8,128)(2,1)S(1)} %get-tuple-element.58), channel_id=1, source_target_pairs={{0,96},{1,97},{2,98},{3,99},{4,100},{5,101},{6,102},{7,103},{8,104... | collective-permute-start | bytes 2408456 | tf_op jit(solution)/shard_map/ppermute | solution.py:52
  62.3 1.7 %shard_map.40 = (s16[400,1024]{1,0:T(8,128)(2,1)S(1)}, s16[400,1024]{1,0:T(8,128)(2,1)S(1)}) custom-call(bf16[768,1024]{1,0:T(8,128)(2,1)S(1)} %get-tuple-element.40.bulk, bf16[3072,768]{1,0:T(8,128)(2,1)S(1)} %get-tuple-element.41.turned), custom_call_target="tpu_custom_call" | custom-call | flops 1207959552 | bytes 1572864 | tf_op jit(solution)/shard_map/pallas_call | solution.py:248
  64.0 1.6 %collective-permute-start.14 = (s16[400,1024]{1,0:T(8,128)(2,1)S(1)}, s16[400,1024]{1,0:T(8,128)(2,1)S(1)}, u32[]{:S(2)}, u32[]{:S(2)}) collective-permute-start(s16[400,1024]{1,0:T(8,128)(2,1)S(1)} %get-tuple-element.45), channel_id=1, source_target_pairs={{0,12},{1,13},{2,14},{3,15},{4,0},{5,1},{6,2},{7,3},{8,4},{9,5},{1... | collective-permute-start | bytes 2457608 | tf_op jit(solution)/shard_map/ppermute | solution.py:52
  65.6 2.1 %collective-permute-done.11.refs_0_ = s16[400,1024]{1,0:T(8,128)(2,1)S(1)} collective-permute-done((s16[400,1024]{1,0:T(8,128)(2,1)S(1)}, s16[400,1024]{1,0:T(8,128)(2,1)S(1)}, u32[]{:S(2)}, u32[]{:S(2)}) %collective-permute-start.11) | collective-permute-done | bytes 819232 | tf_op jit(solution)/shard_map/ppermute | solution.py:52
  68.0 1.7 %shard_map.39 = (s16[400,1024]{1,0:T(8,128)(2,1)S(1)}, s16[400,1024]{1,0:T(8,128)(2,1)S(1)}) custom-call(bf16[768,1024]{1,0:T(8,128)(2,1)S(1)} %get-tuple-element.40.bulk, bf16[3072,768]{1,0:T(8,128)(2,1)S(1)} %get-tuple-element.41.turned, s16[400,1024]{1,0:T(8,128)(2,1)S(1)} %collective-permute-done.11.refs_0_, ...), custom_call_target="tpu_custom_call" | custom-call | flops 1207959552 | bytes 1572864 | tf_op jit(solution)/shard_map/pallas_call | solution.py:248
  71.3 4.2 %collective-permute-done.23.a = s16[3136,128]{1,0:T(8,128)(2,1)S(1)} collective-permute-done((s16[3136,128]{1,0:T(8,128)(2,1)S(1)}, s16[3136,128]{1,0:T(8,128)(2,1)S(1)}, u32[]{:S(2)}, u32[]{:S(2)}) %collective-permute-start.23) | collective-permute-done | bytes 802848 | tf_op jit(solution)/shard_map/ppermute | solution.py:52
  75.5 2.5 %collective-permute-start.16 = (s16[400,1024]{1,0:T(8,128)(2,1)S(1)}, s16[400,1024]{1,0:T(8,128)(2,1)S(1)}, u32[]{:S(2)}, u32[]{:S(2)}) collective-permute-start(s16[400,1024]{1,0:T(8,128)(2,1)S(1)} %get-tuple-element.47), channel_id=1, source_target_pairs={{0,12},{1,13},{2,14},{3,15},{4,0},{5,1},{6,2},{7,3},{8,4},{9,5},{1... | collective-permute-start | bytes 2457608 | tf_op jit(solution)/shard_map/ppermute | solution.py:52
  78.0 1.6 %shard_map.43 = s16[3136,128]{1,0:T(8,128)(2,1)S(1)} custom-call(bf16[768,512]{1,0:T(8,128)(2,1)S(1)} %get-tuple-element.56.rest, bf16[3072,768]{1,0:T(8,128)(2,1)S(1)} %get-tuple-element.41.turned), custom_call_target="tpu_custom_call" | custom-call | flops 603979776 | bytes 1572864 | tf_op jit(solution)/shard_map/pallas_call | solution.py:276
  79.6 9.0 %collective-permute-start.24 = (s16[3136,128]{1,0:T(8,128)(2,1)S(1)}, s16[3136,128]{1,0:T(8,128)(2,1)S(1)}, u32[]{:S(2)}, u32[]{:S(2)}) collective-permute-start(s16[3136,128]{1,0:T(8,128)(2,1)S(1)} %shard_map.43), channel_id=1, source_target_pairs={{0,64},{1,65},{2,66},{3,67},{4,68},{5,69},{6,70},{7,71},{8,72},{9,... | collective-permute-start | bytes 2408456 | tf_op jit(solution)/shard_map/ppermute | solution.py:52
  91.3 7.4 %collective-permute-done.24.b = s16[3136,128]{1,0:T(8,128)(2,1)S(1)} collective-permute-done((s16[3136,128]{1,0:T(8,128)(2,1)S(1)}, s16[3136,128]{1,0:T(8,128)(2,1)S(1)}, u32[]{:S(2)}, u32[]{:S(2)}) %collective-permute-start.24) | collective-permute-done | bytes 802848 | tf_op jit(solution)/shard_map/ppermute | solution.py:52
  102.3 1.6 %collective-permute-start.17 = (s16[208,1024]{1,0:T(8,128)(2,1)S(1)}, s16[208,1024]{1,0:T(8,128)(2,1)S(1)}, u32[]{:S(2)}, u32[]{:S(2)}) collective-permute-start(s16[208,1024]{1,0:T(8,128)(2,1)S(1)} %get-tuple-element.49), channel_id=1, source_target_pairs={{0,1},{1,2},{2,3},{3,0},{4,5},{5,6},{6,7},{7,4},{8,9},{9,10},{10,1... | collective-permute-start | bytes 1277960 | tf_op jit(solution)/shard_map/ppermute | solution.py:52
  105.6 2.9 %collective-permute-start.27 = (s16[208,512]{1,0:T(8,128)(2,1)S(1)}, s16[208,512]{1,0:T(8,128)(2,1)S(1)}, u32[]{:S(2)}, u32[]{:S(2)}) collective-permute-start(s16[208,512]{1,0:T(8,128)(2,1)S(1)} %get-tuple-element.61), channel_id=1, source_target_pairs={{0,2},{1,3},{2,0},{3,1},{4,6},{5,7},{6,4},{7,5},{8,10},{9,11},{10,... | collective-permute-start | bytes 638984 | tf_op jit(solution)/shard_map/ppermute | solution.py:52
  108.5 9.0 %collective-permute-done.27.b = s16[208,512]{1,0:T(8,128)(2,1)S(1)} collective-permute-done((s16[208,512]{1,0:T(8,128)(2,1)S(1)}, s16[208,512]{1,0:T(8,128)(2,1)S(1)}, u32[]{:S(2)}, u32[]{:S(2)}) %collective-permute-start.27) | collective-permute-done | bytes 213024 | tf_op jit(solution)/shard_map/ppermute | solution.py:52
  117.5 4.2 %collective-permute-done.28.d = s16[208,512]{1,0:T(8,128)(2,1)S(1)} collective-permute-done((s16[208,512]{1,0:T(8,128)(2,1)S(1)}, s16[208,512]{1,0:T(8,128)(2,1)S(1)}, u32[]{:S(2)}, u32[]{:S(2)}) %collective-permute-start.28) | collective-permute-done | bytes 213024 | tf_op jit(solution)/shard_map/ppermute | solution.py:52
  124.2 4.3 %collective-permute-start.21 = (s16[208,256]{1,0:T(8,128)(2,1)S(1)}, s16[208,256]{1,0:T(8,128)(2,1)S(1)}, u32[]{:S(2)}, u32[]{:S(2)}) collective-permute-start(s16[208,256]{1,0:T(8,128)(2,1)S(1)} %get-tuple-element.54), channel_id=1, source_target_pairs={{0,64},{1,65},{2,66},{3,67},{4,68},{5,69},{6,70},{7,71},{8,72},{9,... | collective-permute-start | bytes 319496 | tf_op jit(solution)/shard_map/ppermute | solution.py:52
  128.5 2.5 %collective-permute-start.22 = (s16[208,256]{1,0:T(8,128)(2,1)S(1)}, s16[208,256]{1,0:T(8,128)(2,1)S(1)}, u32[]{:S(2)}, u32[]{:S(2)}) collective-permute-start(s16[208,256]{1,0:T(8,128)(2,1)S(1)} %get-tuple-element.55), channel_id=1, source_target_pairs={{0,96},{1,97},{2,98},{3,99},{4,100},{5,101},{6,102},{7,103},{8,104... | collective-permute-start | bytes 319496 | tf_op jit(solution)/shard_map/ppermute | solution.py:52
  131.0 3.1 %collective-permute-start.30 = (s16[208,128]{1,0:T(8,128)(2,1)S(1)}, s16[208,128]{1,0:T(8,128)(2,1)S(1)}, u32[]{:S(2)}, u32[]{:S(2)}) collective-permute-start(s16[208,128]{1,0:T(8,128)(2,1)S(1)} %get-tuple-element.65), channel_id=1, source_target_pairs={{0,8},{1,9},{2,10},{3,11},{4,12},{5,13},{6,14},{7,15},{8,0},{9,1},... | collective-permute-start | bytes 159752 | tf_op jit(solution)/shard_map/ppermute | solution.py:52
  136.7 1.6 %collective-permute-done.31.rd = s16[208,128]{1,0:T(8,128)(2,1)S(1)} collective-permute-done((s16[208,128]{1,0:T(8,128)(2,1)S(1)}, s16[208,128]{1,0:T(8,128)(2,1)S(1)}, u32[]{:S(2)}, u32[]{:S(2)}) %collective-permute-start.31) | collective-permute-done | bytes 53280 | tf_op jit(solution)/shard_map/ppermute | solution.py:52
  (56 shorter events, 24.0 us)
Async XLA Ops:
  3.8 27.2 %collective-permute-start.1 = (bf16[6,16,3072]{2,1,0:T(8,128)(2,1)S(1)}, bf16[6,16,3072]{2,1,0:T(8,128)(2,1)S(1)}, u32[]{:S(2)}, u32[]{:S(2)}) collective-permute-start(bf16[6,16,3072]{2,1,0:T(8,128)(2,1)S(1)} %get-tuple-element.37), channel_id=1, source_target_pairs={{0,32},{1,33},{2,34},{3,35},{4,36},{5,37},{6,38},{7,39},{8,40},{9,... | collective-permute-start | bytes 1769480 | tf_op jit(solution)/shard_map/ppermute | solution.py:52
  5.8 25.3 %collective-permute-start.3 = (bf16[6,16,3072]{2,1,0:T(8,128)(2,1)S(1)}, bf16[6,16,3072]{2,1,0:T(8,128)(2,1)S(1)}, u32[]{:S(2)}, u32[]{:S(2)}) collective-permute-start(bf16[6,16,3072]{2,1,0:T(8,128)(2,1)S(1)} %get-tuple-element.38), channel_id=1, source_target_pairs={{0,64},{1,65},{2,66},{3,67},{4,68},{5,69},{6,70},{7,71},{8,72},{9,... | collective-permute-start | bytes 1769480 | tf_op jit(solution)/shard_map/ppermute | solution.py:52
  6.9 27.4 %collective-permute-start.5 = (bf16[6,16,3072]{2,1,0:T(8,128)(2,1)S(1)}, bf16[6,16,3072]{2,1,0:T(8,128)(2,1)S(1)}, u32[]{:S(2)}, u32[]{:S(2)}) collective-permute-start(bf16[6,16,3072]{2,1,0:T(8,128)(2,1)S(1)} %get-tuple-element.39), channel_id=1, source_target_pairs={{0,96},{1,97},{2,98},{3,99},{4,100},{5,101},{6,102},{7,103},{8,104... | collective-permute-start | bytes 1769480 | tf_op jit(solution)/shard_map/ppermute | solution.py:52
  9.5 39.5 %collective-permute-start = (bf16[6,16,3072]{2,1,0:T(8,128)(2,1)S(1)}, bf16[6,16,3072]{2,1,0:T(8,128)(2,1)S(1)}, u32[]{:S(2)}, u32[]{:S(2)}) collective-permute-start(bf16[6,16,3072]{2,1,0:T(8,128)(2,1)S(1)} %get-tuple-element.36.refs_0_), channel_id=1, source_target_pairs={{0,16},{1,17},{2,18},{3,19},{4,20},{5,21},{6,22},{7,23},{8,24},{9,... | collective-permute-start | bytes 1769480 | tf_op jit(solution)/shard_map/ppermute | solution.py:52
  31.0 18.0 %collective-permute-start.2 = (bf16[6,16,3072]{2,1,0:T(8,128)(2,1)S(1)}, bf16[6,16,3072]{2,1,0:T(8,128)(2,1)S(1)}, u32[]{:S(2)}, u32[]{:S(2)}) collective-permute-start(bf16[6,16,3072]{2,1,0:T(8,128)(2,1)S(1)} %collective-permute-done.1.refs_2_), channel_id=1, source_target_pairs={{0,16},{1,17},{2,18},{3,19},{4,20},{5,21},{6,22},{7,23},{8,24},{9,... | collective-permute-start | bytes 1769480 | tf_op jit(solution)/shard_map/ppermute | solution.py:52
  31.0 18.0 %collective-permute-start.4 = (bf16[6,16,3072]{2,1,0:T(8,128)(2,1)S(1)}, bf16[6,16,3072]{2,1,0:T(8,128)(2,1)S(1)}, u32[]{:S(2)}, u32[]{:S(2)}) collective-permute-start(bf16[6,16,3072]{2,1,0:T(8,128)(2,1)S(1)} %collective-permute-done.3.refs_4_), channel_id=1, source_target_pairs={{0,16},{1,17},{2,18},{3,19},{4,20},{5,21},{6,22},{7,23},{8,24},{9,... | collective-permute-start | bytes 1769480 | tf_op jit(solution)/shard_map/ppermute | solution.py:52
  34.4 14.7 %collective-permute-start.6 = (bf16[6,16,3072]{2,1,0:T(8,128)(2,1)S(1)}, bf16[6,16,3072]{2,1,0:T(8,128)(2,1)S(1)}, u32[]{:S(2)}, u32[]{:S(2)}) collective-permute-start(bf16[6,16,3072]{2,1,0:T(8,128)(2,1)S(1)} %collective-permute-done.5.refs_6_), channel_id=1, source_target_pairs={{0,16},{1,17},{2,18},{3,19},{4,20},{5,21},{6,22},{7,23},{8,24},{9,... | collective-permute-start | bytes 1769480 | tf_op jit(solution)/shard_map/ppermute | solution.py:52
  34.4 2.0 %collective-permute-start.7 = (bf16[16,128]{1,0:T(8,128)(2,1)S(1)}, bf16[16,128]{1,0:T(8,128)(2,1)S(1)}, u32[]{:S(2)}, u32[]{:S(2)}) collective-permute-start(bf16[16,128]{1,0:T(8,128)(2,1)S(1)} %copy-done), channel_id=1, source_target_pairs={{0,16},{1,17},{2,18},{3,19},{4,20},{5,21},{6,22},{7,23},{8,24},{9,... | collective-permute-start | bytes 12296 | tf_op jit(solution)/shard_map/ppermute | solution.py:52
  36.4 3.7 %collective-permute-start.10 = (bf16[32,128]{1,0:T(8,128)(2,1)S(1)}, bf16[32,128]{1,0:T(8,128)(2,1)S(1)}, u32[]{:S(2)}, u32[]{:S(2)}) collective-permute-start(bf16[32,128]{1,0:T(8,128)(2,1)S(1)} %constant_dynamic-update-slice_fusion.refs_0_), channel_id=1, source_target_pairs={{0,96},{1,97},{2,98},{3,99},{4,100},{5,101},{6,102},{7,103},{8,104... | collective-permute-start | bytes 24584 | tf_op jit(solution)/shard_map/ppermute | solution.py:52
  40.0 3.7 %collective-permute-start.8 = (bf16[32,128]{1,0:T(8,128)(2,1)S(1)}, bf16[32,128]{1,0:T(8,128)(2,1)S(1)}, u32[]{:S(2)}, u32[]{:S(2)}) collective-permute-start(bf16[32,128]{1,0:T(8,128)(2,1)S(1)} %constant_dynamic-update-slice_fusion.refs_0_), channel_id=1, source_target_pairs={{0,32},{1,33},{2,34},{3,35},{4,36},{5,37},{6,38},{7,39},{8,40},{9,... | collective-permute-start | bytes 24584 | tf_op jit(solution)/shard_map/ppermute | solution.py:52
  43.7 5.2 %collective-permute-start.9 = (bf16[32,128]{1,0:T(8,128)(2,1)S(1)}, bf16[32,128]{1,0:T(8,128)(2,1)S(1)}, u32[]{:S(2)}, u32[]{:S(2)}) collective-permute-start(bf16[32,128]{1,0:T(8,128)(2,1)S(1)} %constant_dynamic-update-slice_fusion.refs_0_), channel_id=1, source_target_pairs={{0,64},{1,65},{2,66},{3,67},{4,68},{5,69},{6,70},{7,71},{8,72},{9,... | collective-permute-start | bytes 24584 | tf_op jit(solution)/shard_map/ppermute | solution.py:52
  54.1 13.6 %collective-permute-start.11 = (s16[400,1024]{1,0:T(8,128)(2,1)S(1)}, s16[400,1024]{1,0:T(8,128)(2,1)S(1)}, u32[]{:S(2)}, u32[]{:S(2)}) collective-permute-start(s16[400,1024]{1,0:T(8,128)(2,1)S(1)} %get-tuple-element.42), channel_id=1, source_target_pairs={{0,4},{1,5},{2,6},{3,7},{4,8},{5,9},{6,10},{7,11},{8,12},{9,13},{1... | collective-permute-start | bytes 2457608 | tf_op jit(solution)/shard_map/ppermute | solution.py:52
  55.6 12.3 %collective-permute-start.12 = (s16[400,1024]{1,0:T(8,128)(2,1)S(1)}, s16[400,1024]{1,0:T(8,128)(2,1)S(1)}, u32[]{:S(2)}, u32[]{:S(2)}) collective-permute-start(s16[400,1024]{1,0:T(8,128)(2,1)S(1)} %get-tuple-element.43), channel_id=1, source_target_pairs={{0,12},{1,13},{2,14},{3,15},{4,0},{5,1},{6,2},{7,3},{8,4},{9,5},{1... | collective-permute-start | bytes 2457608 | tf_op jit(solution)/shard_map/ppermute | solution.py:52
  59.3 16.2 %collective-permute-start.23 = (s16[3136,128]{1,0:T(8,128)(2,1)S(1)}, s16[3136,128]{1,0:T(8,128)(2,1)S(1)}, u32[]{:S(2)}, u32[]{:S(2)}) collective-permute-start(s16[3136,128]{1,0:T(8,128)(2,1)S(1)} %get-tuple-element.57), channel_id=1, source_target_pairs={{0,32},{1,33},{2,34},{3,35},{4,36},{5,37},{6,38},{7,39},{8,40},{9,... | collective-permute-start | bytes 2408456 | tf_op jit(solution)/shard_map/ppermute | solution.py:52
  60.6 18.9 %collective-permute-start.25 = (s16[3136,128]{1,0:T(8,128)(2,1)S(1)}, s16[3136,128]{1,0:T(8,128)(2,1)S(1)}, u32[]{:S(2)}, u32[]{:S(2)}) collective-permute-start(s16[3136,128]{1,0:T(8,128)(2,1)S(1)} %get-tuple-element.58), channel_id=1, source_target_pairs={{0,96},{1,97},{2,98},{3,99},{4,100},{5,101},{6,102},{7,103},{8,104... | collective-permute-start | bytes 2408456 | tf_op jit(solution)/shard_map/ppermute | solution.py:52
  64.0 36.9 %collective-permute-start.14 = (s16[400,1024]{1,0:T(8,128)(2,1)S(1)}, s16[400,1024]{1,0:T(8,128)(2,1)S(1)}, u32[]{:S(2)}, u32[]{:S(2)}) collective-permute-start(s16[400,1024]{1,0:T(8,128)(2,1)S(1)} %get-tuple-element.45), channel_id=1, source_target_pairs={{0,12},{1,13},{2,14},{3,15},{4,0},{5,1},{6,2},{7,3},{8,4},{9,5},{1... | collective-permute-start | bytes 2457608 | tf_op jit(solution)/shard_map/ppermute | solution.py:52
  67.7 33.3 %collective-permute-start.15 = (s16[400,1024]{1,0:T(8,128)(2,1)S(1)}, s16[400,1024]{1,0:T(8,128)(2,1)S(1)}, u32[]{:S(2)}, u32[]{:S(2)}) collective-permute-start(s16[400,1024]{1,0:T(8,128)(2,1)S(1)} %get-tuple-element.46), channel_id=1, source_target_pairs={{0,4},{1,5},{2,6},{3,7},{4,8},{5,9},{6,10},{7,11},{8,12},{9,13},{1... | collective-permute-start | bytes 2457608 | tf_op jit(solution)/shard_map/ppermute | solution.py:52
  69.7 31.2 %collective-permute-start.13 = (s16[400,1024]{1,0:T(8,128)(2,1)S(1)}, s16[400,1024]{1,0:T(8,128)(2,1)S(1)}, u32[]{:S(2)}, u32[]{:S(2)}) collective-permute-start(s16[400,1024]{1,0:T(8,128)(2,1)S(1)} %get-tuple-element.44), channel_id=1, source_target_pairs={{0,4},{1,5},{2,6},{3,7},{4,8},{5,9},{6,10},{7,11},{8,12},{9,13},{1... | collective-permute-start | bytes 2457608 | tf_op jit(solution)/shard_map/ppermute | solution.py:52
  75.5 25.5 %collective-permute-start.16 = (s16[400,1024]{1,0:T(8,128)(2,1)S(1)}, s16[400,1024]{1,0:T(8,128)(2,1)S(1)}, u32[]{:S(2)}, u32[]{:S(2)}) collective-permute-start(s16[400,1024]{1,0:T(8,128)(2,1)S(1)} %get-tuple-element.47), channel_id=1, source_target_pairs={{0,12},{1,13},{2,14},{3,15},{4,0},{5,1},{6,2},{7,3},{8,4},{9,5},{1... | collective-permute-start | bytes 2457608 | tf_op jit(solution)/shard_map/ppermute | solution.py:52
  79.6 19.1 %collective-permute-start.24 = (s16[3136,128]{1,0:T(8,128)(2,1)S(1)}, s16[3136,128]{1,0:T(8,128)(2,1)S(1)}, u32[]{:S(2)}, u32[]{:S(2)}) collective-permute-start(s16[3136,128]{1,0:T(8,128)(2,1)S(1)} %shard_map.43), channel_id=1, source_target_pairs={{0,64},{1,65},{2,66},{3,67},{4,68},{5,69},{6,70},{7,71},{8,72},{9,... | collective-permute-start | bytes 2408456 | tf_op jit(solution)/shard_map/ppermute | solution.py:52
  99.6 8.9 %collective-permute-start.26 = (s16[208,512]{1,0:T(8,128)(2,1)S(1)}, s16[208,512]{1,0:T(8,128)(2,1)S(1)}, u32[]{:S(2)}, u32[]{:S(2)}) collective-permute-start(s16[208,512]{1,0:T(8,128)(2,1)S(1)} %get-tuple-element.60), channel_id=1, source_target_pairs={{0,1},{1,2},{2,3},{3,0},{4,5},{5,6},{6,7},{7,4},{8,9},{9,10},{10,1... | collective-permute-start | bytes 638984 | tf_op jit(solution)/shard_map/ppermute | solution.py:52
  102.3 21.3 %collective-permute-start.17 = (s16[208,1024]{1,0:T(8,128)(2,1)S(1)}, s16[208,1024]{1,0:T(8,128)(2,1)S(1)}, u32[]{:S(2)}, u32[]{:S(2)}) collective-permute-start(s16[208,1024]{1,0:T(8,128)(2,1)S(1)} %get-tuple-element.49), channel_id=1, source_target_pairs={{0,1},{1,2},{2,3},{3,0},{4,5},{5,6},{6,7},{7,4},{8,9},{9,10},{10,1... | collective-permute-start | bytes 1277960 | tf_op jit(solution)/shard_map/ppermute | solution.py:52
  103.9 19.7 %collective-permute-start.18 = (s16[208,1024]{1,0:T(8,128)(2,1)S(1)}, s16[208,1024]{1,0:T(8,128)(2,1)S(1)}, u32[]{:S(2)}, u32[]{:S(2)}) collective-permute-start(s16[208,1024]{1,0:T(8,128)(2,1)S(1)} %get-tuple-element.50), channel_id=1, source_target_pairs={{0,2},{1,3},{2,0},{3,1},{4,6},{5,7},{6,4},{7,5},{8,10},{9,11},{10,... | collective-permute-start | bytes 1277960 | tf_op jit(solution)/shard_map/ppermute | solution.py:52
  104.6 19.0 %collective-permute-start.19 = (s16[208,1024]{1,0:T(8,128)(2,1)S(1)}, s16[208,1024]{1,0:T(8,128)(2,1)S(1)}, u32[]{:S(2)}, u32[]{:S(2)}) collective-permute-start(s16[208,1024]{1,0:T(8,128)(2,1)S(1)} %get-tuple-element.51), channel_id=1, source_target_pairs={{0,3},{1,0},{2,1},{3,2},{4,7},{5,4},{6,5},{7,6},{8,11},{9,8},{10,9... | collective-permute-start | bytes 1277960 | tf_op jit(solution)/shard_map/ppermute | solution.py:52
  105.6 11.9 %collective-permute-start.27 = (s16[208,512]{1,0:T(8,128)(2,1)S(1)}, s16[208,512]{1,0:T(8,128)(2,1)S(1)}, u32[]{:S(2)}, u32[]{:S(2)}) collective-permute-start(s16[208,512]{1,0:T(8,128)(2,1)S(1)} %get-tuple-element.61), channel_id=1, source_target_pairs={{0,2},{1,3},{2,0},{3,1},{4,6},{5,7},{6,4},{7,5},{8,10},{9,11},{10,... | collective-permute-start | bytes 638984 | tf_op jit(solution)/shard_map/ppermute | solution.py:52
  108.5 13.3 %collective-permute-start.28 = (s16[208,512]{1,0:T(8,128)(2,1)S(1)}, s16[208,512]{1,0:T(8,128)(2,1)S(1)}, u32[]{:S(2)}, u32[]{:S(2)}) collective-permute-start(s16[208,512]{1,0:T(8,128)(2,1)S(1)} %get-tuple-element.62), channel_id=1, source_target_pairs={{0,3},{1,0},{2,1},{3,2},{4,7},{5,4},{6,5},{7,6},{8,11},{9,8},{10,9... | collective-permute-start | bytes 638984 | tf_op jit(solution)/shard_map/ppermute | solution.py:52
  122.0 12.1 %collective-permute-start.29 = (s16[208,128]{1,0:T(8,128)(2,1)S(1)}, s16[208,128]{1,0:T(8,128)(2,1)S(1)}, u32[]{:S(2)}, u32[]{:S(2)}) collective-permute-start(s16[208,128]{1,0:T(8,128)(2,1)S(1)} %get-tuple-element.64), channel_id=1, source_target_pairs={{0,4},{1,5},{2,6},{3,7},{4,8},{5,9},{6,10},{7,11},{8,12},{9,13},{1... | collective-permute-start | bytes 159752 | tf_op jit(solution)/shard_map/ppermute | solution.py:52
  124.1 14.2 %collective-permute-start.20 = (s16[208,256]{1,0:T(8,128)(2,1)S(1)}, s16[208,256]{1,0:T(8,128)(2,1)S(1)}, u32[]{:S(2)}, u32[]{:S(2)}) collective-permute-start(s16[208,256]{1,0:T(8,128)(2,1)S(1)} %get-tuple-element.53), channel_id=1, source_target_pairs={{0,32},{1,33},{2,34},{3,35},{4,36},{5,37},{6,38},{7,39},{8,40},{9,... | collective-permute-start | bytes 319496 | tf_op jit(solution)/shard_map/ppermute | solution.py:52
  124.2 14.1 %collective-permute-start.21 = (s16[208,256]{1,0:T(8,128)(2,1)S(1)}, s16[208,256]{1,0:T(8,128)(2,1)S(1)}, u32[]{:S(2)}, u32[]{:S(2)}) collective-permute-start(s16[208,256]{1,0:T(8,128)(2,1)S(1)} %get-tuple-element.54), channel_id=1, source_target_pairs={{0,64},{1,65},{2,66},{3,67},{4,68},{5,69},{6,70},{7,71},{8,72},{9,... | collective-permute-start | bytes 319496 | tf_op jit(solution)/shard_map/ppermute | solution.py:52
  128.5 9.8 %collective-permute-start.22 = (s16[208,256]{1,0:T(8,128)(2,1)S(1)}, s16[208,256]{1,0:T(8,128)(2,1)S(1)}, u32[]{:S(2)}, u32[]{:S(2)}) collective-permute-start(s16[208,256]{1,0:T(8,128)(2,1)S(1)} %get-tuple-element.55), channel_id=1, source_target_pairs={{0,96},{1,97},{2,98},{3,99},{4,100},{5,101},{6,102},{7,103},{8,104... | collective-permute-start | bytes 319496 | tf_op jit(solution)/shard_map/ppermute | solution.py:52
  131.0 5.6 %collective-permute-start.30 = (s16[208,128]{1,0:T(8,128)(2,1)S(1)}, s16[208,128]{1,0:T(8,128)(2,1)S(1)}, u32[]{:S(2)}, u32[]{:S(2)}) collective-permute-start(s16[208,128]{1,0:T(8,128)(2,1)S(1)} %get-tuple-element.65), channel_id=1, source_target_pairs={{0,8},{1,9},{2,10},{3,11},{4,12},{5,13},{6,14},{7,15},{8,0},{9,1},... | collective-permute-start | bytes 159752 | tf_op jit(solution)/shard_map/ppermute | solution.py:52
  134.2 4.1 %collective-permute-start.31 = (s16[208,128]{1,0:T(8,128)(2,1)S(1)}, s16[208,128]{1,0:T(8,128)(2,1)S(1)}, u32[]{:S(2)}, u32[]{:S(2)}) collective-permute-start(s16[208,128]{1,0:T(8,128)(2,1)S(1)} %get-tuple-element.66), channel_id=1, source_target_pairs={{0,12},{1,13},{2,14},{3,15},{4,0},{5,1},{6,2},{7,3},{8,4},{9,5},{1... | collective-permute-start | bytes 159752 | tf_op jit(solution)/shard_map/ppermute | solution.py:52
  (2 other events, 34.4 us)
